TPU v7x, 32 devices: a whole 2x2x4 slice. The times are simulated.
32 devices in a mesh: dom: 8 (over z, y), grp: 4 (over x, core).
Axes of the slice: x: 2, y: 2, z: 4, core: 2. Of those that a mesh axis runs over, the one named last changes fastest.
Arguments:
- deflation: bfloat16 [32, 1024, 3, 2, 128], P(('dom', 'grp')), may hold values from -1.5 to 1.5
- inverse: bfloat16 [32, 2, 1024, 1024], P(('dom', 'grp'))
- operator: bfloat16 [32, 2, 1024, 1024], P(('dom', 'grp'))
- neighbours: int32 [32, 6], P(('dom', 'grp')), may hold values from -1 to 31, as said below
- counts: int32 [32, 6], P(('dom', 'grp')), may hold values from 0 to 256, as said below
- margin_rows: int32 [32, 6, 256], P(('dom', 'grp')), may hold values from 0 to 1023, as said below
- owners: int32 [32, 6, 1], P(('dom', 'grp')), may hold values from 0 to 3; in each aligned block of 6 rows (0 to 5, 6 to 11, ..., all dimensions but the last counted through in order) at most 2 rows name the same one
Outputs:
- owned_blocks: float32 [256, 3, 2, 128, 128], P(('dom', 'grp'))
Inputs may be any that keep to these rules, and one draw needn't show every extreme that they name: `neighbours`: entry n of a subdomain's list is the subdomain with the same group index whose dom index is d + o_n modulo 8 (o_n = -3, -2, -1, 1, 2, 3), or -1 where that pair shares no rows; the relation is symmetric. `counts`: equal on both sides of a pair, 0 exactly where the list holds -1, and 256 for some pair in every draw. `margin_rows`: distinct within each slot; for k below the pair's count, entry k on one side and entry k on the other side name the same global edge. `owners`: among one subdomain's 6 blocks no group index is named more than 2 times; some subdomain names one exactly 2 times.
All inputs are finite; a program needn't handle non-finite values.
Results may differ from a plain program's by a relative error of at most 0.0048.
Values may be sent and summed in bfloat16 or wider, within the bound.
No kernel may reach another device: no remote copies, remote signals or barrier semaphores. Data moves between devices by JAX's collectives and lax.ppermute only.
A program may use at most 64 MiB of HBM per device.

v0:
```python
import jax
import jax.numpy as jnp
from jax import lax
from jax.sharding import PartitionSpec as P

OFFSETS = (-3, -2, -1, 1, 2, 3)


def passed_along(value, axis, steps):
    count = lax.axis_size(axis)
    pairs = [(source, (source + steps) % count) for source in range(count)]
    return lax.ppermute(value, axis, pairs)


def complex_apply(matrix, vectors):
    edges = vectors.shape[0]
    flat = vectors.reshape(edges, -1)
    real_part = jnp.dot(matrix[0], flat, preferred_element_type=jnp.float32).reshape(vectors.shape)
    imag_part = jnp.dot(matrix[1], flat, preferred_element_type=jnp.float32).reshape(vectors.shape)
    result_real = real_part[:, :, 0] - imag_part[:, :, 1]
    result_imag = real_part[:, :, 1] + imag_part[:, :, 0]
    return jnp.stack([result_real, result_imag], axis=2).astype(jnp.bfloat16)


def on_device(deflation, inverse, operator, neighbours, counts, margin_rows, owners):
    set_count = deflation.shape[2]
    width = deflation.shape[4]
    margin = margin_rows.shape[2]
    slots = margin_rows.shape[1]
    vectors = deflation[0]
    first_pass = complex_apply(inverse[0], vectors)
    second_pass = complex_apply(inverse[0], first_pass)
    imaged = complex_apply(operator[0], second_pass)
    slot_rows = margin_rows[0]
    positions = jnp.arange(margin, dtype=jnp.int32)
    live = (neighbours[0][:, None] >= 0) & (positions[None, :] < counts[0][:, None])
    outgoing = jnp.where(
        live[:, :, None, None, None], imaged[slot_rows], jnp.zeros((), jnp.bfloat16)
    )
    pieces = [None] * len(OFFSETS)
    for slot_index, offset in enumerate(OFFSETS):
        pieces[len(OFFSETS) - 1 - slot_index] = passed_along(outgoing[slot_index], "dom", offset)
    incoming = jnp.stack(pieces).reshape(slots, margin, set_count, 2 * width)
    projector = vectors[slot_rows].reshape(slots, margin, set_count, 2 * width)
    gram = jnp.einsum("nrsk,nrsl->nskl", projector, incoming, preferred_element_type=jnp.float32)
    real_part = gram[:, :, :width, :width] - gram[:, :, width:, width:]
    imag_part = gram[:, :, :width, width:] + gram[:, :, width:, :width]
    coupling = jnp.stack([real_part, imag_part], axis=2)
    group_count = lax.axis_size("grp")
    capacity = (slots + group_count - 1) // group_count
    targets_grp = owners[0, :, 0]
    same = targets_grp[:, None] == targets_grp[None, :]
    slot_ids = jnp.arange(slots, dtype=jnp.int32)
    earlier = slot_ids[None, :] < slot_ids[:, None]
    rank = jnp.sum((same & earlier).astype(jnp.int32), axis=1)
    place = targets_grp * capacity + rank
    holders = jnp.arange(group_count * capacity, dtype=jnp.int32)
    selector = (holders[:, None] == place[None, :]).astype(jnp.float32)
    packed_blocks = jnp.einsum(
        "pn,nwxyz->pwxyz", selector, coupling, precision=lax.Precision.HIGHEST
    )
    return lax.all_to_all(packed_blocks, "grp", split_axis=0, concat_axis=0, tiled=True)


def solution(mesh):
    placed = (
        P(("dom", "grp"), None, None, None, None),
        P(("dom", "grp"), None, None, None),
        P(("dom", "grp"), None, None, None),
        P(("dom", "grp"), None),
        P(("dom", "grp"), None),
        P(("dom", "grp"), None, None),
        P(("dom", "grp"), None, None),
    )
    return jax.shard_map(
        on_device,
        mesh=mesh,
        in_specs=placed,
        out_specs=P(("dom", "grp"), None, None, None, None),
        check_vma=False,
    )
```

profile of v0, /device:TPU:0, one launch (start us, length us, event | category | flops | bytes accessed | tf_op | source)
XLA Modules:
  0.0 198.2 jit_solution(17161314080144062758)
XLA Ops:
  0.0 3.9 %reshape_squeeze.3 = bf16[1024,768]{1,0:T(8,128)(2,1)S(1)} reshape(bf16[1,1024,3,2,128]{4,3,2,1,0:T(2,128)(2,1)} %param.7) | data formatting | bytes 3145728 | tf_op jit(solution)/shard_map/reshape;squeeze | solution.py:17
  4.9 3.6 %fusion.4 = f32[1024,3,2,128]{0,3,2,1:T(8,128)S(1)} fusion(bf16[3,2,128,1024]{3,2,1,0:T(8,128)(2,1)S(1)} %bitcast.100, bf16[1,2,1024,1024]{3,2,1,0:T(8,128)(2,1)} %param.8), kind=kOutput, calls=%fused_computation.8 | convolution fusion | flops 1610612736 | bytes 6815744 | tf_op jit(solution)/shard_map/dot_general | solution.py:19
  8.5 1.8 fusion.6
  11.3 1.8 fusion.14
  13.1 1.8 fusion.12
  17.1 1.8 fusion.10
  19.0 3.5 %fusion.8 = f32[768,1024]{1,0:T(8,128)} fusion(bf16[1024,768]{0,1:T(8,128)(2,1)S(1)} %bitcast.99, bf16[1,2,1024,1024]{3,2,1,0:T(8,128)(2,1)S(1)} %copy-done.7), kind=kOutput, calls=%fused_computation.12 | convolution fusion | flops 1610612736 | bytes 6815744 | tf_op jit(solution)/shard_map/dot_general | solution.py:19
  25.6 3.9 %fusion.34 = (f32[1024,3,1,128]{0,3,2,1:T(8,128)}, f32[1024,3,1,128]{0,3,2,1:T(8,128)}) fusion(f32[1024,3,2,128]{0,3,2,1:T(8,128)} %bitcast.92), kind=kLoop, calls=%fused_computation.68 | loop fusion | bytes 6291456 | tf_op jit(solution)/shard_map/slice | solution.py:20
  29.6 4.0 %copy.69 = f32[1024,3,1,128]{3,2,1,0:T(1,128)S(1)} copy(f32[1024,3,1,128]{0,3,2,1:T(8,128)} %get-tuple-element.11) | data formatting | bytes 3145728
  33.5 4.8 %copy.70 = f32[1024,3,1,128]{3,2,1,0:T(1,128)} copy(f32[1024,3,1,128]{0,3,2,1:T(8,128)} %get-tuple-element.14) | data formatting | bytes 3145728
  38.3 4.9 %copy.71 = f32[1024,3,1,128]{3,2,1,0:T(1,128)} copy(f32[1024,3,1,128]{0,3,2,1:T(8,128)} %get-tuple-element.12) | data formatting | bytes 3145728
  43.3 4.6 %add_convert_fusion = (bf16[1024,3,1,128]{3,2,1,0:T(2,128)(2,1)S(1)}, bf16[1024,3,1,128]{3,2,1,0:T(2,128)(2,1)S(1)}) fusion(f32[1024,3,1,128]{3,2,1,0:T(1,128)} %copy.70, f32[1024,3,1,128]{3,2,1,0:T(1,128)} %copy.71, f32[1024,3,1,128]{3,2,1,0:T(1,128)S(1)} %copy.68, f32[1024,3,1,128]{3,2,1,0:T(1,128)S(1)} %copy.69), kind=kLoop, calls=%fused_computation.37 | loop fusion | flops 1572864 | bytes 7864320 | tf_op jit(solution)/shard_map/convert.1
  48.0 3.6 %pad_maximum_fusion.3 = bf16[1024,3,2,128]{3,2,1,0:T(2,128)(2,1)S(1)} fusion(bf16[1024,3,1,128]{3,2,1,0:T(2,128)(2,1)S(1)} %get-tuple-element.21, bf16[1024,3,1,128]{3,2,1,0:T(2,128)(2,1)S(1)} %get-tuple-element.22), kind=kLoop, calls=%fused_computation.36 | loop fusion | flops 3145728 | bytes 3145728 | tf_op jit(solution)/shard_map/stack | solution.py:22
  51.6 8.1 %gather_fusion.1 = bf16[1536,3,2,128]{3,2,1,0:T(2,128)(2,1)} fusion(bf16[1024,3,2,128]{3,2,1,0:T(2,128)(2,1)S(1)} %pad_maximum_fusion.3, s32[2048]{0:T(1024)S(1)} %pad_clamp_fusion), kind=kCustom, calls=%fused_computation.1 | custom fusion | bytes 4724736 | tf_op jit(solution)/shard_map/gather | solution.py:38
  59.7 2.0 %copy.51 = bf16[1536,3,2,128]{3,0,2,1:T(8,128)(2,1)S(1)} copy(bf16[1536,3,2,128]{3,2,1,0:T(2,128)(2,1)} %gather_fusion.1) | data formatting | bytes 4718592 | tf_op jit(solution)/shard_map/gather | solution.py:38
  63.5 4.0 %collective-permute-start = (bf16[256,3,2,128]{3,0,2,1:T(8,128)(2,1)S(1)}, bf16[256,3,2,128]{3,0,2,1:T(8,128)(2,1)S(1)}, u32[]{:S(2)}, u32[]{:S(2)}) collective-permute-start(bf16[256,3,2,128]{3,0,2,1:T(8,128)(2,1)S(1)} %get-tuple-element.20), channel_id=1, source_target_pairs={{0,12},{4,16},{8,20},{12,24},{16,28},{20,0},{24,4},{28,8},{1,13},{... | collective-permute-start | bytes 1179656 | tf_op jit(solution)/shard_map/ppermute | solution.py:12
  70.6 3.2 %collective-permute-start.3 = (bf16[256,3,2,128]{3,0,2,1:T(8,128)(2,1)}, bf16[256,3,2,128]{3,0,2,1:T(8,128)(2,1)}, u32[]{:S(2)}, u32[]{:S(2)}) collective-permute-start(bf16[256,3,2,128]{3,0,2,1:T(8,128)(2,1)} %get-tuple-element.17), channel_id=1, source_target_pairs={{0,28},{4,0},{8,4},{12,8},{16,12},{20,16},{24,20},{28,24},{1,29},{... | collective-permute-start | bytes 1179656 | tf_op jit(solution)/shard_map/ppermute | solution.py:12
  74.3 29.6 %collective-permute-done = bf16[256,3,2,128]{3,0,2,1:T(8,128)(2,1)S(1)} collective-permute-done((bf16[256,3,2,128]{3,0,2,1:T(8,128)(2,1)S(1)}, bf16[256,3,2,128]{3,0,2,1:T(8,128)(2,1)S(1)}, u32[]{:S(2)}, u32[]{:S(2)}) %collective-permute-start) | collective-permute-done | bytes 393248 | tf_op jit(solution)/shard_map/ppermute | solution.py:12
  104.8 8.1 %gather_fusion = bf16[1536,3,2,128]{3,2,1,0:T(2,128)(2,1)} fusion(bf16[1024,3,2,128]{3,2,1,0:T(2,128)(2,1)S(1)} %bitcast.89, s32[2048]{0:T(1024)S(1)} %pad_clamp_fusion), kind=kCustom, calls=%fused_computation | custom fusion | bytes 4724736 | tf_op jit(solution)/shard_map/gather | solution.py:44
  112.9 7.4 %reshape.179 = bf16[6,256,3,256]{3,2,1,0:T(4,128)(2,1)S(1)} reshape(bf16[1536,3,2,128]{3,2,1,0:T(2,128)(2,1)} %gather_fusion) | data formatting | bytes 4718592 | tf_op jit(solution)/shard_map/reshape | solution.py:44
  122.7 2.1 %copy.53 = bf16[256,3,2,128]{3,2,0,1:T(2,128)(2,1)} copy(bf16[256,3,2,128]{3,0,2,1:T(8,128)(2,1)} %collective-permute-done.1) | data formatting | bytes 786432 | tf_op jit(solution)/shard_map/ppermute | solution.py:12
  126.1 2.1 %copy.54 = bf16[256,3,2,128]{3,2,0,1:T(2,128)(2,1)} copy(bf16[256,3,2,128]{3,0,2,1:T(8,128)(2,1)} %collective-permute-done.2) | data formatting | bytes 786432 | tf_op jit(solution)/shard_map/ppermute | solution.py:12
  128.3 2.0 %stack.53 = bf16[1,256,3,256]{3,1,2,0:T(8,128)(2,1)} reshape(bf16[256,3,2,128]{3,2,0,1:T(2,128)(2,1)} %copy.54) | data formatting | bytes 786432 | tf_op jit(solution)/shard_map/stack | solution.py:43
  130.3 2.1 %copy.55 = bf16[256,3,2,128]{3,2,0,1:T(2,128)(2,1)} copy(bf16[256,3,2,128]{3,0,2,1:T(8,128)(2,1)} %collective-permute-done.3) | data formatting | bytes 786432 | tf_op jit(solution)/shard_map/ppermute | solution.py:12
  132.4 2.0 %stack.54 = bf16[1,256,3,256]{3,1,2,0:T(8,128)(2,1)} reshape(bf16[256,3,2,128]{3,2,0,1:T(2,128)(2,1)} %copy.55) | data formatting | bytes 786432 | tf_op jit(solution)/shard_map/stack | solution.py:43
  134.4 2.1 %copy.56 = bf16[256,3,2,128]{3,2,0,1:T(2,128)(2,1)} copy(bf16[256,3,2,128]{3,0,2,1:T(8,128)(2,1)} %collective-permute-done.4) | data formatting | bytes 786432 | tf_op jit(solution)/shard_map/ppermute | solution.py:12
  136.6 2.0 %stack.55 = bf16[1,256,3,256]{3,1,2,0:T(8,128)(2,1)} reshape(bf16[256,3,2,128]{3,2,0,1:T(2,128)(2,1)} %copy.56) | data formatting | bytes 786432 | tf_op jit(solution)/shard_map/stack | solution.py:43
  140.3 2.2 %copy.57 = bf16[256,3,2,128]{3,2,0,1:T(2,128)(2,1)} copy(bf16[256,3,2,128]{3,0,2,1:T(8,128)(2,1)} %collective-permute-done.5) | data formatting | bytes 786432 | tf_op jit(solution)/shard_map/ppermute | solution.py:12
  142.5 2.0 %stack.56 = bf16[1,256,3,256]{3,1,2,0:T(8,128)(2,1)} reshape(bf16[256,3,2,128]{3,2,0,1:T(2,128)(2,1)} %copy.57) | data formatting | bytes 786432 | tf_op jit(solution)/shard_map/stack | solution.py:43
  150.3 2.5 %fusion.2 = f32[6,3,256,256]{3,2,1,0:T(8,128)S(1)} fusion(bf16[6,256,3,256]{3,1,2,0:T(8,128)(2,1)} %constant_dynamic-update-slice_fusion, bf16[6,256,3,256]{3,2,1,0:T(4,128)(2,1)S(1)} %reshape.179), kind=kOutput, calls=%fused_computation.5 | convolution fusion | flops 603979776 | bytes 9437184 | tf_op jit(solution)/shard_map/nrsk,nrsl->nskl/dot_general | solution.py:45
  153.3 2.9 %fusion = f32[8,3,2,128,128]{4,0,3,2,1:T(8,128)S(1)} fusion(f32[6,3,2,128,128]{4,3,1,0,2:T(8,128)S(1)} %pad_maximum_fusion, s32[6]{0:T(128)S(1)} %multiply_add_fusion), kind=kOutput, calls=%fused_computation.2 | convolution fusion | flops 56623152 | bytes 5505048 | tf_op jit(solution)/shard_map/pn,nwxyz->pwxyz/dot_general | solution.py:59
  156.8 39.7 %all_to_all.5 = f32[8,3,2,128,128]{4,3,2,1,0:T(8,128)S(1)} all-to-all(f32[8,3,2,128,128]{4,3,2,1,0:T(8,128)S(1)} %copy.60), channel_id=1, replica_groups=mesh['dom'=8,'grp'=4] {'grp'}, dimensions={0} | all-to-all | bytes 6291456 | tf_op jit(solution)/shard_map/all_to_all | solution.py:62
  (58 shorter events, 27.5 us)
Async XLA Ops:
  4.9 3.6 %copy-start.6 = (bf16[1,2,1024,1024]{3,2,1,0:T(8,128)(2,1)S(1)}, bf16[1,2,1024,1024]{3,2,1,0:T(8,128)(2,1)}, u32[]{:S(2)}) copy-start(bf16[1,2,1024,1024]{3,2,1,0:T(8,128)(2,1)} %param.8) | copy-start | bytes 12582916
  14.9 2.2 %copy-start.7 = (bf16[1,2,1024,1024]{3,2,1,0:T(8,128)(2,1)S(1)}, bf16[1,2,1024,1024]{3,2,1,0:T(8,128)(2,1)}, u32[]{:S(2)}) copy-start(bf16[1,2,1024,1024]{3,2,1,0:T(8,128)(2,1)} %param.9) | copy-start | bytes 12582916
  38.3 4.9 %copy-start.4 = (s32[1,6,256]{2,0,1:T(1,128)S(1)}, s32[1,6,256]{2,0,1:T(1,128)}, u32[]{:S(2)}) copy-start(s32[1,6,256]{2,0,1:T(1,128)} %param.12) | copy-start | bytes 18436
  59.7 2.0 %copy-start.8 = (s32[1,6]{1,0:T(1,128)S(1)}, s32[1,6]{1,0:T(1,128)}, u32[]{:S(2)}) copy-start(s32[1,6]{1,0:T(1,128)} %param.10) | copy-start | bytes 76
  59.7 2.0 %copy-start.5 = (s32[1,6]{1,0:T(1,128)S(1)}, s32[1,6]{1,0:T(1,128)}, u32[]{:S(2)}) copy-start(s32[1,6]{1,0:T(1,128)} %param.11) | copy-start | bytes 76
  62.2 42.4 %copy-start.9 = (s32[1,6,1]{1,2,0:T(1,128)S(1)}, s32[1,6,1]{1,2,0:T(1,128)}, u32[]{:S(2)}) copy-start(s32[1,6,1]{1,2,0:T(1,128)} %param.13) | copy-start | bytes 76
  62.2 42.6 %copy-start = (bf16[1,1024,3,2,128]{4,3,2,1,0:T(2,128)(2,1)S(1)}, bf16[1,1024,3,2,128]{4,3,2,1,0:T(2,128)(2,1)}, u32[]{:S(2)}) copy-start(bf16[1,1024,3,2,128]{4,3,2,1,0:T(2,128)(2,1)} %param.7) | copy-start | bytes 4718596
  63.5 40.3 %collective-permute-start = (bf16[256,3,2,128]{3,0,2,1:T(8,128)(2,1)S(1)}, bf16[256,3,2,128]{3,0,2,1:T(8,128)(2,1)S(1)}, u32[]{:S(2)}, u32[]{:S(2)}) collective-permute-start(bf16[256,3,2,128]{3,0,2,1:T(8,128)(2,1)S(1)} %get-tuple-element.20), channel_id=1, source_target_pairs={{0,12},{4,16},{8,20},{12,24},{16,28},{20,0},{24,4},{28,8},{1,13},{... | collective-permute-start | bytes 1179656 | tf_op jit(solution)/shard_map/ppermute | solution.py:12
  67.5 55.2 %collective-permute-start.1 = (bf16[256,3,2,128]{3,0,2,1:T(8,128)(2,1)}, bf16[256,3,2,128]{3,0,2,1:T(8,128)(2,1)}, u32[]{:S(2)}, u32[]{:S(2)}) collective-permute-start(bf16[256,3,2,128]{3,0,2,1:T(8,128)(2,1)} %get-tuple-element.19), channel_id=1, source_target_pairs={{0,8},{4,12},{8,16},{12,20},{16,24},{20,28},{24,0},{28,4},{1,9},{5... | collective-permute-start | bytes 1179656 | tf_op jit(solution)/shard_map/ppermute | solution.py:12
  69.1 57.0 %collective-permute-start.2 = (bf16[256,3,2,128]{3,0,2,1:T(8,128)(2,1)}, bf16[256,3,2,128]{3,0,2,1:T(8,128)(2,1)}, u32[]{:S(2)}, u32[]{:S(2)}) collective-permute-start(bf16[256,3,2,128]{3,0,2,1:T(8,128)(2,1)} %get-tuple-element.18), channel_id=1, source_target_pairs={{0,4},{4,8},{8,12},{12,16},{16,20},{20,24},{24,28},{28,0},{1,5},{5... | collective-permute-start | bytes 1179656 | tf_op jit(solution)/shard_map/ppermute | solution.py:12
  70.6 59.7 %collective-permute-start.3 = (bf16[256,3,2,128]{3,0,2,1:T(8,128)(2,1)}, bf16[256,3,2,128]{3,0,2,1:T(8,128)(2,1)}, u32[]{:S(2)}, u32[]{:S(2)}) collective-permute-start(bf16[256,3,2,128]{3,0,2,1:T(8,128)(2,1)} %get-tuple-element.17), channel_id=1, source_target_pairs={{0,28},{4,0},{8,4},{12,8},{16,12},{20,16},{24,20},{28,24},{1,29},{... | collective-permute-start | bytes 1179656 | tf_op jit(solution)/shard_map/ppermute | solution.py:12
  73.8 60.6 %collective-permute-start.4 = (bf16[256,3,2,128]{3,0,2,1:T(8,128)(2,1)}, bf16[256,3,2,128]{3,0,2,1:T(8,128)(2,1)}, u32[]{:S(2)}, u32[]{:S(2)}) collective-permute-start(bf16[256,3,2,128]{3,0,2,1:T(8,128)(2,1)} %get-tuple-element.16), channel_id=1, source_target_pairs={{0,24},{4,28},{8,0},{12,4},{16,8},{20,12},{24,16},{28,20},{1,25},{... | collective-permute-start | bytes 1179656 | tf_op jit(solution)/shard_map/ppermute | solution.py:12
  103.8 0.8 copy-start.3
  104.6 35.7 %collective-permute-start.5 = (bf16[256,3,2,128]{3,0,2,1:T(8,128)(2,1)}, bf16[256,3,2,128]{3,0,2,1:T(8,128)(2,1)}, u32[]{:S(2)}, u32[]{:S(2)}) collective-permute-start(bf16[256,3,2,128]{3,0,2,1:T(8,128)(2,1)} %get-tuple-element.15), channel_id=1, source_target_pairs={{0,20},{4,24},{8,28},{12,0},{16,4},{20,8},{24,12},{28,16},{1,21},{... | collective-permute-start | bytes 1179656 | tf_op jit(solution)/shard_map/ppermute | solution.py:12
  144.5 4.3 %copy-start.1 = (bf16[1,256,3,256]{3,1,2,0:T(8,128)(2,1)S(1)}, bf16[1,256,3,256]{3,1,2,0:T(8,128)(2,1)}, u32[]{:S(2)}) copy-start(bf16[1,256,3,256]{3,1,2,0:T(8,128)(2,1)} %stack.55) | copy-start | bytes 1179652
  144.5 5.1 %copy-start.2 = (bf16[1,256,3,256]{3,1,2,0:T(8,128)(2,1)S(1)}, bf16[1,256,3,256]{3,1,2,0:T(8,128)(2,1)}, u32[]{:S(2)}) copy-start(bf16[1,256,3,256]{3,1,2,0:T(8,128)(2,1)} %stack.56) | copy-start | bytes 1179652
where the time goes:
time: 200 us; the launch traced here: 198 us
  local copies, waits for them, and re-layouts  86.8 us (43%)
  blocking collectives  39.7 us (20%)
  waiting for transfers between devices  29.6 us (15%)
  matrix products  19.7 us (10%)
  other arithmetic  11.3 us (6%)
  starting transfers between devices  10.8 us (5%)
    all_to_all x1, blocking collectives, on_device(): lax.all_to_all(packed_blocks, 'grp', split_axis=0, concat_axis=0, tiled=T...  39.7 us
    ppermute x6, waiting for transfers between devices, passed_along(): return lax.ppermute(value, axis, pairs)  29.6 us
    unnamed x30, local copies, waits for them, and re-layouts  25.9 us
    ppermute x6, local copies, waits for them, and re-layouts, passed_along(): return lax.ppermute(value, axis, pairs)  12.1 us
    another operation x7, local copies, waits for them, and re-layouts, on_device(): incoming = jnp.stack(pieces).reshape(slots, margin, set_count, 2 * width)  11 us
    ppermute x6, starting transfers between devices, passed_along(): return lax.ppermute(value, axis, pairs)  10.8 us
    gather x2, local copies, waits for them, and re-layouts, on_device(): imaged[slot_rows]  10.1 us
    dot_general x3, matrix products, complex_apply(): jnp.dot(matrix[1], flat, preferred_element_type=jnp.float32)  8.89 us
  transfers between devices with their start and end apart: 6, of which 1 were waited for; matrix products, arithmetic and copies ran while one was open for 18% of the time, Pallas kernels for 0%

commit v1 on v0

v1 whole, which is shorter than its diff:
```python
import functools

import jax
import jax.numpy as jnp
from jax import lax
from jax.experimental import pallas as pl
from jax.experimental.pallas import tpu as pltpu
from jax.sharding import PartitionSpec as P


OFFSETS = (-3, -2, -1, 1, 2, 3)
F32 = jnp.float32
BF16 = jnp.bfloat16
CHAIN_VMEM = 16 * 1024 * 1024
SMALL_VMEM = 12 * 1024 * 1024


def passed_along(value, axis, steps):
    count = lax.axis_size(axis)
    pairs = [(source, (source + steps) % count) for source in range(count)]
    return lax.ppermute(value, axis, pairs)


def partner(index, hop, count):
    if count & (count - 1) == 0:
        return index ^ hop
    return (index + hop) % count


def hop_to(index, target, count):
    if count & (count - 1) == 0:
        return index ^ target
    return lax.rem(target - index + count, count)


def hop_from(index, hop, count):
    if count & (count - 1) == 0:
        return index ^ hop
    return lax.rem(index - hop + count, count)


def fill_selector(rows_ref, counts_ref, neighbours_ref, selector):
    slots, _, margin = rows_ref.shape
    edges = selector.shape[1]
    positions = lax.broadcasted_iota(jnp.int32, (1, margin), 1)
    lanes = lax.broadcasted_iota(jnp.int32, (1, edges), 1).astype(F32)
    masked = []
    for slot in range(8):
        if slot < slots:
            live = (positions < counts_ref[0, slot]) & (neighbours_ref[0, slot] >= 0)
            masked.append(jnp.where(live, rows_ref[slot], -1).astype(F32))
        else:
            masked.append(jnp.full((1, margin), -1.0, F32))
    columns = jnp.transpose(jnp.concatenate(masked, axis=0))
    for slot in range(slots):
        hit = columns[:, slot : slot + 1] == lanes
        selector[slot * margin : (slot + 1) * margin, :] = jnp.where(hit, 1.0, 0.0).astype(BF16)


def gather_vectors(z_wide, index, sets, width, a, b):
    edges = a.shape[0]
    real = z_wide[pl.ds(2 * index, edges, stride=2 * sets), :]
    imag = z_wide[pl.ds(2 * index + 1, edges, stride=2 * sets), :]
    a[:, :width] = real.astype(BF16)
    a[:, width:] = imag.astype(BF16)
    b[:, :width] = (-imag).astype(BF16)
    b[:, width:] = real.astype(BF16)


def apply(matrix, waits, width, a, b, to_a, to_b):
    edges = a.shape[0]
    block = edges // 4
    for part in range(4):
        if part in waits:
            waits[part]()
        at = slice(part * block, (part + 1) * block)
        total = jnp.dot(matrix[0, at, :], a[...], preferred_element_type=F32)
        total += jnp.dot(matrix[1, at, :], b[...], preferred_element_type=F32)
        to_a[at, :] = total.astype(BF16)
        if to_b is not None:
            to_b[at, :width] = (-total[:, width:]).astype(BF16)
            to_b[at, width:] = total[:, :width].astype(BF16)


def pick_rows(selector, image, outs):
    margin = outs[0].shape[0]
    for slot, out in enumerate(outs):
        out[...] = jnp.dot(
            selector[slot * margin : (slot + 1) * margin, :], image[...], preferred_element_type=F32
        ).astype(BF16)


def first_chain_kernel(sets, width, *refs):
    counts_ref, neighbours_ref, rows_ref, z_ref, inverse_ref, operator_ref = refs[:6]
    slots = rows_ref.shape[0]
    outs = refs[6 : 6 + slots]
    inverse, operator, selector, z_wide = refs[6 + slots : 10 + slots]
    z_in, first_a, first_b, second_a, second_b, sems = refs[10 + slots :]
    block = inverse.shape[1] // 2
    z_copy = pltpu.make_async_copy(z_ref, z_in, sems.at[0])
    z_copy.start()

    def fetch(source, target, half, sem):
        at = pl.ds(half * block, block)
        return pltpu.make_async_copy(source.at[:, at], target.at[:, at], sem)

    loads = [fetch(inverse_ref, inverse, half, sems.at[1 + half]) for half in range(2)]
    loads += [fetch(operator_ref, operator, half, sems.at[3 + half]) for half in range(2)]
    loads[0].start()
    loads[1].start()
    fill_selector(rows_ref, counts_ref, neighbours_ref, selector)
    z_copy.wait()
    z_wide[...] = z_in[...].astype(F32)
    gather_vectors(z_wide, 0, sets, width, first_a, first_b)

    def begin():
        loads[0].wait()
        loads[2].start()
        loads[3].start()

    apply(inverse, {0: begin, 2: loads[1].wait}, width, first_a, first_b, second_a, second_b)
    apply(inverse, {}, width, second_a, second_b, first_a, first_b)
    apply(operator, {0: loads[2].wait, 2: loads[3].wait}, width, first_a, first_b, second_a, None)
    pick_rows(selector, second_a, outs)


def in_hbm(*values):
    return [pltpu.with_memory_space_constraint(value, pltpu.HBM) for value in values]


def in_vmem(*values):
    return [pltpu.with_memory_space_constraint(value, pltpu.VMEM) for value in values]


def first_chain(sets, width, counts, neighbours, rows, z, inverse, operator):
    slots, _, margin = rows.shape
    edges = inverse.shape[1]
    hbm = pl.BlockSpec(memory_space=pltpu.HBM)
    smem = pl.BlockSpec(memory_space=pltpu.SMEM)
    vmem = pl.BlockSpec(memory_space=pltpu.VMEM)
    flops = 4 * edges * width * (6 * edges + slots * margin)
    outs = [pltpu.VMEM((margin, 2 * width), BF16)] * slots + [
        pltpu.VMEM(inverse.shape, BF16),
        pltpu.VMEM(operator.shape, BF16),
        pltpu.VMEM((slots * margin, edges), BF16),
        pltpu.VMEM(z.shape, F32),
    ]
    results = pl.pallas_call(
        functools.partial(first_chain_kernel, sets, width),
        out_shape=outs,
        in_specs=[smem, smem, vmem, hbm, hbm, hbm],
        out_specs=[vmem] * len(outs),
        scratch_shapes=[pltpu.VMEM(z.shape, BF16)]
        + [pltpu.VMEM((edges, 2 * width), BF16)] * 4
        + [pltpu.SemaphoreType.DMA((5,))],
        compiler_params=pltpu.CompilerParams(vmem_limit_bytes=CHAIN_VMEM),
        cost_estimate=pl.CostEstimate(flops=flops, bytes_accessed=12 << 20, transcendentals=0),
        name="chain0",
    )(*in_hbm(counts, neighbours, rows, z, inverse, operator))
    return results[:slots], results[slots:]


def next_chain_kernel(index, sets, width, inverse, operator, selector, z_wide, *refs):
    outs, (first_a, first_b, second_a, second_b) = refs[:-4], refs[-4:]
    gather_vectors(z_wide, index, sets, width, first_a, first_b)
    apply(inverse, {}, width, first_a, first_b, second_a, second_b)
    apply(inverse, {}, width, second_a, second_b, first_a, first_b)
    apply(operator, {}, width, first_a, first_b, second_a, None)
    pick_rows(selector, second_a, outs)


def next_chain(index, sets, width, slots, held):
    inverse, _, selector, _ = held
    edges = inverse.shape[1]
    margin = selector.shape[0] // slots
    vmem = pl.BlockSpec(memory_space=pltpu.VMEM)
    flops = 4 * edges * width * (6 * edges + slots * margin)
    return pl.pallas_call(
        functools.partial(next_chain_kernel, index, sets, width),
        out_shape=[pltpu.VMEM((margin, 2 * width), BF16)] * slots,
        in_specs=[vmem] * 4,
        out_specs=[vmem] * slots,
        scratch_shapes=[pltpu.VMEM((edges, 2 * width), BF16)] * 4,
        compiler_params=pltpu.CompilerParams(vmem_limit_bytes=SMALL_VMEM),
        cost_estimate=pl.CostEstimate(flops=flops, bytes_accessed=12 << 20, transcendentals=0),
    )(*in_vmem(*held))


def project_kernel(width, selector, z_wide, *refs):
    outs, turned = refs[:-1], refs[-1]
    edges = turned.shape[1]
    slots, _, margin = outs[0].shape
    for index, out in enumerate(outs):
        for part in range(2):
            turned[part * width : (part + 1) * width, :] = jnp.transpose(
                z_wide[pl.ds(2 * index + part, edges, stride=2 * len(outs)), :]
            ).astype(BF16)
        for slot in range(slots):
            out[slot] = lax.dot_general(
                turned[...],
                selector[slot * margin : (slot + 1) * margin, :],
                (((1,), (1,)), ((), ())),
                preferred_element_type=F32,
            ).astype(BF16)


def project(sets, width, slots, held):
    _, _, selector, z_wide = held
    margin, edges = selector.shape[0] // slots, selector.shape[1]
    vmem = pl.BlockSpec(memory_space=pltpu.VMEM)
    return pl.pallas_call(
        functools.partial(project_kernel, width),
        out_shape=[pltpu.VMEM((slots, 2 * width, margin), BF16)] * sets,
        in_specs=[vmem] * 2,
        out_specs=[vmem] * sets,
        scratch_shapes=[pltpu.VMEM((2 * width, edges), BF16)],
        compiler_params=pltpu.CompilerParams(vmem_limit_bytes=SMALL_VMEM),
        cost_estimate=pl.CostEstimate(
            flops=4 * edges * width * slots * margin * sets, bytes_accessed=6 << 20, transcendentals=0
        ),
        name="project",
    )(*in_vmem(selector, z_wide))


def gram_kernel(group, width, hops, capacity, owners_ref, me_ref, *rest):
    projectors, rest = rest[: len(group)], rest[len(group) :]
    slots = projectors[0].shape[0]
    incoming, outs, packed = rest[:slots], rest[slots : slots + hops], rest[-1]
    me = me_ref[0]
    packed[...] = jnp.zeros_like(packed)
    step = 2 * width
    for slot in range(slots):
        owner = owners_ref[0, slot]
        rank = jnp.int32(0)
        for other in range(slot):
            rank += (owners_ref[0, other] == owner).astype(jnp.int32)
        place = hop_to(me, owner, hops) * capacity + rank
        for at in range(len(group)):
            gram = jnp.dot(
                projectors[at][slot],
                incoming[slot][:, at * step : (at + 1) * step],
                preferred_element_type=F32,
            )
            packed[place, at, 0] = (gram[:width, :width] - gram[width:, width:]).astype(BF16)
            packed[place, at, 1] = (gram[:width, width:] + gram[width:, :width]).astype(BF16)
    for hop in range(hops):
        outs[hop][...] = packed[hop * capacity : (hop + 1) * capacity]


def gram_blocks(group, width, hops, capacity, owners, me, projectors, incoming):
    smem = pl.BlockSpec(memory_space=pltpu.SMEM)
    vmem = pl.BlockSpec(memory_space=pltpu.VMEM)
    block = (capacity, len(group), 2, width, width)
    slots, _, margin = projectors[0].shape
    return pl.pallas_call(
        functools.partial(gram_kernel, group, width, hops, capacity),
        out_shape=[jax.ShapeDtypeStruct(block, BF16)] * hops,
        in_specs=[smem, smem] + [vmem] * (len(group) + len(incoming)),
        out_specs=[vmem] * hops,
        scratch_shapes=[pltpu.VMEM((hops * capacity,) + block[1:], BF16)],
        compiler_params=pltpu.CompilerParams(vmem_limit_bytes=SMALL_VMEM),
        cost_estimate=pl.CostEstimate(
            flops=2 * slots * margin * 4 * width * width * len(group),
            bytes_accessed=2 << 20,
            transcendentals=0,
        ),
    )(owners, me, *projectors, *incoming)


def spread(group, sets, width, capacity, me, arrived, held):
    hops = len(arrived)
    smem = pl.BlockSpec(memory_space=pltpu.SMEM)
    vmem = pl.BlockSpec(memory_space=pltpu.VMEM)
    any_space = pl.BlockSpec(memory_space=pl.ANY)
    places = hops * capacity
    extra = [] if held is None else [held]

    def body(me_ref, *rest):
        inputs, (out_ref, wide, sem) = rest[:hops], rest[-3:]
        mine = me_ref[0]
        copies = []
        for hop in range(hops):
            source = hop_from(mine, hop, hops)
            for place in range(capacity):
                wide[source * capacity + place] = inputs[hop][place].astype(F32)
            span = pl.ds(source * capacity, capacity)
            copy = pltpu.make_async_copy(
                wide.at[span],
                out_ref.at[span, group[0] : group[0] + len(group)],
                sem.at[hop],
            )
            copy.start()
            copies.append(copy)
        for copy in copies:
            copy.wait()

    return pl.pallas_call(
        body,
        out_shape=jax.ShapeDtypeStruct((places, sets, 2, width, width), F32),
        in_specs=[smem] + [vmem] * hops + [any_space] * len(extra),
        out_specs=any_space,
        scratch_shapes=[
            pltpu.VMEM((places, len(group), 2, width, width), F32),
            pltpu.SemaphoreType.DMA((hops,)),
        ],
        input_output_aliases={1 + hops: 0} if extra else {},
        compiler_params=pltpu.CompilerParams(vmem_limit_bytes=SMALL_VMEM),
        cost_estimate=pl.CostEstimate(flops=1 << 20, bytes_accessed=2 << 20, transcendentals=0),
    )(me, *arrived, *extra)


def exchanged(outgoing):
    pieces = [None] * len(outgoing)
    for slot, offset in enumerate(OFFSETS):
        pieces[len(outgoing) - 1 - slot] = passed_along(outgoing[slot], "dom", offset)
    return pieces


def on_device(deflation, inverse, operator, neighbours, counts, margin_rows, owners):
    _, edges, sets, _, width = deflation.shape
    _, slots, margin = margin_rows.shape
    group_count = lax.axis_size("grp")
    capacity = (slots + group_count - 1) // group_count
    z = deflation.reshape(edges * sets * 2, width)
    rows = margin_rows.reshape(slots, 1, margin)
    owned = owners.reshape(1, slots)
    me = lax.axis_index("grp").astype(jnp.int32).reshape(1)
    arrived = []
    for index in range(sets):
        if index == 0:
            outgoing, held = first_chain(
                sets, width, counts, neighbours, rows, z, inverse[0], operator[0]
            )
        else:
            outgoing = next_chain(index, sets, width, slots, held)
        arrived.append(exchanged(outgoing))
    projectors = project(sets, width, slots, held)
    received = []
    for index, pieces in enumerate(arrived):
        blocks = gram_blocks(
            (index,), width, group_count, capacity, owned, me, [projectors[index]], pieces
        )
        sent = [blocks[0]]
        for hop in range(1, group_count):
            pairs = [(s, partner(s, hop, group_count)) for s in range(group_count)]
            sent.append(lax.ppermute(blocks[hop], "grp", pairs))
        received.append(sent)
    result = None
    for index in range(sets):
        result = spread((index,), sets, width, capacity, me, received[index], result)
    return result


def solution(mesh):
    placed = (
        P(("dom", "grp"), None, None, None, None),
        P(("dom", "grp"), None, None, None),
        P(("dom", "grp"), None, None, None),
        P(("dom", "grp"), None),
        P(("dom", "grp"), None),
        P(("dom", "grp"), None, None),
        P(("dom", "grp"), None, None),
    )
    return jax.shard_map(
        on_device,
        mesh=mesh,
        in_specs=placed,
        out_specs=P(("dom", "grp"), None, None, None, None),
        check_vma=False,
    )
```

time: 200 us -> 87.9 us (0.44)
  local copies, waits for them, and re-layouts: 86.8 us -> 3.64 us
  blocking collectives: 39.7 us -> 0 us
  starting transfers between devices: 10.8 us -> 39.5 us
  Pallas kernels: 0 us -> 26 us
  matrix products: 19.7 us -> 0 us
  waiting for transfers between devices: 29.6 us -> 17.9 us
  other arithmetic: 11.3 us -> 0 us
    all_to_all x1 -> x0, blocking collectives: 39.7 us -> none  [on_device(): lax.all_to_all(packed_blocks, 'grp', split_axis=0, concat_axis=0, tiled=T...]
    pallas_call x0 -> x10, Pallas kernels: none -> 26 us  [the longest x2 9.33 us: next_chain(): pl.pallas_call(functools.partial(next_chain_kernel, index, sets, width),...]
    unnamed x30 -> x20, local copies, waits for them, and re-layouts: 25.9 us -> 3.64 us
    ppermute x6 -> x18, starting transfers between devices: 10.8 us -> 31.8 us  [passed_along(): return lax.ppermute(value, axis, pairs)]
    dot_general x8 -> x0, matrix products: 19.7 us -> none  [the longest x3 8.89 us: complex_apply(): jnp.dot(matrix[1], flat, preferred_element_type=jnp.float32)]
    ppermute x6 -> x18, waiting for transfers between devices: 29.6 us -> 10 us  [passed_along(): return lax.ppermute(value, axis, pairs)]
    gather x3 -> x0, local copies, waits for them, and re-layouts: 18.3 us -> none  [the longest x2 10.1 us: on_device(): imaged[slot_rows]]
    another operation x8 -> x0, local copies, waits for them, and re-layouts: 14.9 us -> none  [the longest x7 11 us: on_device(): incoming = jnp.stack(pieces).reshape(slots, margin, set_count, 2 * width)]
  transfers between devices with their start and end apart: 6 -> 27, of which waited for: 1 -> 9; matrix products, arithmetic and copies ran while one was open for 18% -> 0% of each run, Pallas kernels for 0% -> 20%
where the time goes in v1:
time: 87.9 us; the launch traced here: 87.4 us
  starting transfers between devices  39.5 us (45%)
  Pallas kernels  26 us (30%)
  waiting for transfers between devices  17.9 us (20%)
  local copies, waits for them, and re-layouts  3.64 us (4%)
    ppermute x18, starting transfers between devices, passed_along(): return lax.ppermute(value, axis, pairs)  31.8 us
    ppermute x18, waiting for transfers between devices, passed_along(): return lax.ppermute(value, axis, pairs)  10 us
    pallas_call x2, Pallas kernels, next_chain(): pl.pallas_call(functools.partial(next_chain_kernel, index, sets, width),...  9.33 us
    ppermute x9, waiting for transfers between devices, on_device(): sent.append(lax.ppermute(blocks[hop], 'grp', pairs))  7.92 us
    ppermute x9, starting transfers between devices, on_device(): sent.append(lax.ppermute(blocks[hop], 'grp', pairs))  7.69 us
    pallas_call x1, Pallas kernels, first_chain(): pl.pallas_call(functools.partial(first_chain_kernel, sets, width), out_sh...  7.57 us
    unnamed x20, local copies, waits for them, and re-layouts  3.64 us
    pallas_call x3, Pallas kernels, gram_blocks(): pl.pallas_call(functools.partial(gram_kernel, group, width, hops, capacit...  3.44 us
  transfers between devices with their start and end apart: 27, of which 9 were waited for; matrix products, arithmetic and copies ran while one was open for 0% of the time, Pallas kernels for 20%

profile of v1, /device:TPU:0, one launch (start us, length us, event | category | flops | bytes accessed | tf_op | source)
XLA Modules:
  0.0 87.4 jit_solution(18249585560063379182)
XLA Ops:
  0.0 7.6 %chain0.1 = (bf16[256,256]{1,0:T(8,128)(2,1)S(1)}, bf16[256,256]{1,0:T(8,128)(2,1)S(1)}, bf16[256,256]{1,0:T(8,128)(2,1)S(1)}, bf16[256,256]{1,0:T(8,128)(2,1)S(...) custom-call(s32[1,6]{1,0:T(1,128)} %refs_0_.1, ...), custom_call_target="tpu_custom_call" | custom-call | flops 4026531840 | bytes 12582912 | tf_op jit(solution)/shard_map/chain0/pallas_call | solution.py:148
  7.6 4.1 %collective-permute-start.18 = (bf16[256,256]{1,0:T(8,128)(2,1)S(1)}, bf16[256,256]{1,0:T(8,128)(2,1)S(1)}, u32[]{:S(2)}, u32[]{:S(2)}) collective-permute-start(bf16[256,256]{1,0:T(8,128)(2,1)S(1)} %get-tuple-element.69), channel_id=1, source_target_pairs={{0,12},{4,16},{8,20},{12,24},{16,28},{20,0},{24,4},{28,8},{1,13},{... | collective-permute-start | bytes 393224 | tf_op jit(solution)/shard_map/ppermute | solution.py:21
  11.6 1.6 %collective-permute-start.19 = (bf16[256,256]{1,0:T(8,128)(2,1)S(1)}, bf16[256,256]{1,0:T(8,128)(2,1)S(1)}, u32[]{:S(2)}, u32[]{:S(2)}) collective-permute-start(bf16[256,256]{1,0:T(8,128)(2,1)S(1)} %get-tuple-element.70), channel_id=1, source_target_pairs={{0,8},{4,12},{8,16},{12,20},{16,24},{20,28},{24,0},{28,4},{1,9},{5... | collective-permute-start | bytes 393224 | tf_op jit(solution)/shard_map/ppermute | solution.py:21
  13.2 1.5 %collective-permute-start.20 = (bf16[256,256]{1,0:T(8,128)(2,1)S(1)}, bf16[256,256]{1,0:T(8,128)(2,1)S(1)}, u32[]{:S(2)}, u32[]{:S(2)}) collective-permute-start(bf16[256,256]{1,0:T(8,128)(2,1)S(1)} %get-tuple-element.71), channel_id=1, source_target_pairs={{0,4},{4,8},{8,12},{12,16},{16,20},{20,24},{24,28},{28,0},{1,5},{5... | collective-permute-start | bytes 393224 | tf_op jit(solution)/shard_map/ppermute | solution.py:21
  14.7 3.2 %collective-permute-start.21 = (bf16[256,256]{1,0:T(8,128)(2,1)S(1)}, bf16[256,256]{1,0:T(8,128)(2,1)S(1)}, u32[]{:S(2)}, u32[]{:S(2)}) collective-permute-start(bf16[256,256]{1,0:T(8,128)(2,1)S(1)} %get-tuple-element.72), channel_id=1, source_target_pairs={{0,28},{4,0},{8,4},{12,8},{16,12},{20,16},{24,20},{28,24},{1,29},{... | collective-permute-start | bytes 393224 | tf_op jit(solution)/shard_map/ppermute | solution.py:21
  18.4 4.3 %shard_map.75 = (bf16[256,256]{1,0:T(8,128)(2,1)S(1)}, bf16[256,256]{1,0:T(8,128)(2,1)S(1)}, bf16[256,256]{1,0:T(8,128)(2,1)S(1)}, bf16[256,256]{1,0:T(8,128)(2,...) custom-call(bf16[2,1024,1024]{2,1,0:T(8,128)(2,1)S(1)} %get-tuple-element.45.inverse, ...), custom_call_target="tpu_custom_call" | custom-call | flops 4026531840 | bytes 12582912 | tf_op jit(solution)/shard_map/pallas_call | solution.py:178
  22.7 2.8 %collective-permute-done.18.rest_1_ = bf16[256,256]{1,0:T(8,128)(2,1)S(1)} collective-permute-done((bf16[256,256]{1,0:T(8,128)(2,1)S(1)}, bf16[256,256]{1,0:T(8,128)(2,1)S(1)}, u32[]{:S(2)}, u32[]{:S(2)}) %collective-permute-start.18) | collective-permute-done | bytes 131104 | tf_op jit(solution)/shard_map/ppermute | solution.py:21
  25.5 2.9 %collective-permute-start.9 = (bf16[256,256]{1,0:T(8,128)(2,1)S(1)}, bf16[256,256]{1,0:T(8,128)(2,1)S(1)}, u32[]{:S(2)}, u32[]{:S(2)}) collective-permute-start(bf16[256,256]{1,0:T(8,128)(2,1)S(1)} %get-tuple-element.58), channel_id=1, source_target_pairs={{0,12},{4,16},{8,20},{12,24},{16,28},{20,0},{24,4},{28,8},{1,13},{... | collective-permute-start | bytes 393224 | tf_op jit(solution)/shard_map/ppermute | solution.py:21
  28.4 3.7 %collective-permute-start.10 = (bf16[256,256]{1,0:T(8,128)(2,1)S(1)}, bf16[256,256]{1,0:T(8,128)(2,1)S(1)}, u32[]{:S(2)}, u32[]{:S(2)}) collective-permute-start(bf16[256,256]{1,0:T(8,128)(2,1)S(1)} %get-tuple-element.59), channel_id=1, source_target_pairs={{0,8},{4,12},{8,16},{12,20},{16,24},{20,28},{24,0},{28,4},{1,9},{5... | collective-permute-start | bytes 393224 | tf_op jit(solution)/shard_map/ppermute | solution.py:21
  32.1 2.3 %collective-permute-start.11 = (bf16[256,256]{1,0:T(8,128)(2,1)S(1)}, bf16[256,256]{1,0:T(8,128)(2,1)S(1)}, u32[]{:S(2)}, u32[]{:S(2)}) collective-permute-start(bf16[256,256]{1,0:T(8,128)(2,1)S(1)} %get-tuple-element.60), channel_id=1, source_target_pairs={{0,4},{4,8},{8,12},{12,16},{16,20},{20,24},{24,28},{28,0},{1,5},{5... | collective-permute-start | bytes 393224 | tf_op jit(solution)/shard_map/ppermute | solution.py:21
  34.4 2.4 %collective-permute-start.12 = (bf16[256,256]{1,0:T(8,128)(2,1)S(1)}, bf16[256,256]{1,0:T(8,128)(2,1)S(1)}, u32[]{:S(2)}, u32[]{:S(2)}) collective-permute-start(bf16[256,256]{1,0:T(8,128)(2,1)S(1)} %get-tuple-element.61), channel_id=1, source_target_pairs={{0,28},{4,0},{8,4},{12,8},{16,12},{20,16},{24,20},{28,24},{1,29},{... | collective-permute-start | bytes 393224 | tf_op jit(solution)/shard_map/ppermute | solution.py:21
  36.8 5.5 %collective-permute-done.9.rest_1_ = bf16[256,256]{1,0:T(8,128)(2,1)S(1)} collective-permute-done((bf16[256,256]{1,0:T(8,128)(2,1)S(1)}, bf16[256,256]{1,0:T(8,128)(2,1)S(1)}, u32[]{:S(2)}, u32[]{:S(2)}) %collective-permute-start.9) | collective-permute-done | bytes 131104 | tf_op jit(solution)/shard_map/ppermute | solution.py:21
  42.3 5.0 %shard_map.73 = (bf16[256,256]{1,0:T(8,128)(2,1)S(1)}, bf16[256,256]{1,0:T(8,128)(2,1)}, bf16[256,256]{1,0:T(8,128)(2,1)}, bf16[256,256]{1,0:T(8,128)(2,1)}, bf1...) custom-call(bf16[2,1024,1024]{2,1,0:T(8,128)(2,1)S(1)} %get-tuple-element.45.inverse, ...), custom_call_target="tpu_custom_call" | custom-call | flops 4026531840 | bytes 12582912 | tf_op jit(solution)/shard_map/pallas_call | solution.py:178
  47.3 2.9 %collective-permute-start = (bf16[256,256]{1,0:T(8,128)(2,1)}, bf16[256,256]{1,0:T(8,128)(2,1)S(1)}, u32[]{:S(2)}, u32[]{:S(2)}) collective-permute-start(bf16[256,256]{1,0:T(8,128)(2,1)} %get-tuple-element.47), channel_id=1, source_target_pairs={{0,12},{4,16},{8,20},{12,24},{16,28},{20,0},{24,4},{28,8},{1,13},{... | collective-permute-start | bytes 393224 | tf_op jit(solution)/shard_map/ppermute | solution.py:21
  50.9 4.2 %collective-permute-start.3 = (bf16[256,256]{1,0:T(8,128)(2,1)}, bf16[256,256]{1,0:T(8,128)(2,1)}, u32[]{:S(2)}, u32[]{:S(2)}) collective-permute-start(bf16[256,256]{1,0:T(8,128)(2,1)} %get-tuple-element.50), channel_id=1, source_target_pairs={{0,28},{4,0},{8,4},{12,8},{16,12},{20,16},{24,20},{28,24},{1,29},{... | collective-permute-start | bytes 393224 | tf_op jit(solution)/shard_map/ppermute | solution.py:21
  55.1 2.0 %collective-permute-start.4 = (bf16[256,256]{1,0:T(8,128)(2,1)}, bf16[256,256]{1,0:T(8,128)(2,1)}, u32[]{:S(2)}, u32[]{:S(2)}) collective-permute-start(bf16[256,256]{1,0:T(8,128)(2,1)} %get-tuple-element.51), channel_id=1, source_target_pairs={{0,24},{4,28},{8,0},{12,4},{16,8},{20,12},{24,16},{28,20},{1,25},{... | collective-permute-start | bytes 393224 | tf_op jit(solution)/shard_map/ppermute | solution.py:21
  57.0 2.7 %project.1 = (bf16[6,256,256]{2,1,0:T(8,128)(2,1)S(1)}, bf16[6,256,256]{2,1,0:T(8,128)(2,1)S(1)}, bf16[6,256,256]{2,1,0:T(8,128)(2,1)S(1)}) custom-call(bf16[1536,1024]{1,0:T(8,128)(2,1)S(1)} %get-tuple-element.42.selector, f32[6144,128]{1,0:T(8,128)S(1)} %get-tuple-element.43.z_wide), custom_call_target="tpu_custom_call" | custom-call | flops 2415919104 | bytes 6291456 | tf_op jit(solution)/shard_map/project/pallas_call | solution.py:211
  59.8 1.0 %shard_map.77 = (bf16[2,1,2,128,128]{4,3,2,1,0:T(8,128)(2,1)S(1)}, bf16[2,1,2,128,128]{4,3,2,1,0:T(8,128)(2,1)S(1)}, bf16[2,1,2,128,128]{4,3,2,1,0:T(8,128)(2,1)S(1)}, bf16[2,1,2,128,128]{4,3,2,1,0:T(8,128)(2,1)S(1)}) custom-call(s32[1,6]{1,0:T(1,128)S(1)} %bitcast.6, s32[1]{0:T(128)} %bitcast.me_ref, bf16[6,256,256]{2,1,0:T(8,128)(2,1)S(1)} %get-tuple-element.68.rest_0_, ...), custom_call_target="tpu_custom_call" | custom-call | flops 201326592 | bytes 2097152 | tf_op jit(solution)/shard_map/pallas_call | solution.py:255
  60.7 1.7 %collective-permute-done.rest_1_ = bf16[256,256]{1,0:T(8,128)(2,1)S(1)} collective-permute-done((bf16[256,256]{1,0:T(8,128)(2,1)}, bf16[256,256]{1,0:T(8,128)(2,1)S(1)}, u32[]{:S(2)}, u32[]{:S(2)}) %collective-permute-start) | collective-permute-done | bytes 131104 | tf_op jit(solution)/shard_map/ppermute | solution.py:21
  66.0 1.0 %shard_map.76 = (bf16[2,1,2,128,128]{4,3,2,1,0:T(8,128)(2,1)S(1)}, bf16[2,1,2,128,128]{4,3,2,1,0:T(8,128)(2,1)S(1)}, bf16[2,1,2,128,128]{4,3,2,1,0:T(8,128)(2,1)S(1)}, bf16[2,1,2,128,128]{4,3,2,1,0:T(8,128)(2,1)S(1)}) custom-call(s32[1,6]{1,0:T(1,128)S(1)} %bitcast.7, s32[1]{0:T(128)} %bitcast.me_ref, bf16[6,256,256]{2,1,0:T(8,128)(2,1)S(1)} %get-tuple-element.57.rest_0_, ...), custom_call_target="tpu_custom_call" | custom-call | flops 201326592 | bytes 2097152 | tf_op jit(solution)/shard_map/pallas_call | solution.py:255
  67.6 1.5 %collective-permute-start.25 = (bf16[2,1,2,128,128]{4,3,2,1,0:T(8,128)(2,1)S(1)}, bf16[2,1,2,128,128]{4,3,2,1,0:T(8,128)(2,1)S(1)}, u32[]{:S(2)}, u32[]{:S(2)}) collective-permute-start(bf16[2,1,2,128,128]{4,3,2,1,0:T(8,128)(2,1)S(1)} %get-tuple-element.77), channel_id=1, source_target_pairs={{0,2},{1,3},{2,0},{3,1},{4,6},{5,7},{6,4},{7,5},{8,10},{9,11},{10,... | collective-permute-start | bytes 393224 | tf_op jit(solution)/shard_map/ppermute | solution.py:346
  69.1 1.4 %collective-permute-start.16 = (bf16[2,1,2,128,128]{4,3,2,1,0:T(8,128)(2,1)S(1)}, bf16[2,1,2,128,128]{4,3,2,1,0:T(8,128)(2,1)S(1)}, u32[]{:S(2)}, u32[]{:S(2)}) collective-permute-start(bf16[2,1,2,128,128]{4,3,2,1,0:T(8,128)(2,1)S(1)} %get-tuple-element.66), channel_id=1, source_target_pairs={{0,2},{1,3},{2,0},{3,1},{4,6},{5,7},{6,4},{7,5},{8,10},{9,11},{10,... | collective-permute-start | bytes 393224 | tf_op jit(solution)/shard_map/ppermute | solution.py:346
  70.5 1.5 %shard_map.74 = (bf16[2,1,2,128,128]{4,3,2,1,0:T(8,128)(2,1)S(1)}, bf16[2,1,2,128,128]{4,3,2,1,0:T(8,128)(2,1)S(1)}, bf16[2,1,2,128,128]{4,3,2,1,0:T(8,128)(2,1)S(1)}, bf16[2,1,2,128,128]{4,3,2,1,0:T(8,128)(2,1)S(1)}) custom-call(s32[1,6]{1,0:T(1,128)S(1)} %bitcast.8, s32[1]{0:T(128)} %bitcast.me_ref, bf16[6,256,256]{2,1,0:T(8,128)(2,1)S(1)} %get-tuple-element.44.rest_0_, ...), custom_call_target="tpu_custom_call" | custom-call | flops 201326592 | bytes 2097152 | tf_op jit(solution)/shard_map/pallas_call | solution.py:255
  72.9 1.1 %collective-permute-done.25.rest_2_ = bf16[2,1,2,128,128]{4,3,2,1,0:T(8,128)(2,1)S(1)} collective-permute-done((bf16[2,1,2,128,128]{4,3,2,1,0:T(8,128)(2,1)S(1)}, bf16[2,1,2,128,128]{4,3,2,1,0:T(8,128)(2,1)S(1)}, u32[]{:S(2)}, u32[]{:S(2)}) %collective-permute-start.25) | collective-permute-done | bytes 131104 | tf_op jit(solution)/shard_map/ppermute | solution.py:346
  74.0 1.5 %collective-permute-start.7 = (bf16[2,1,2,128,128]{4,3,2,1,0:T(8,128)(2,1)S(1)}, bf16[2,1,2,128,128]{4,3,2,1,0:T(8,128)(2,1)S(1)}, u32[]{:S(2)}, u32[]{:S(2)}) collective-permute-start(bf16[2,1,2,128,128]{4,3,2,1,0:T(8,128)(2,1)S(1)} %get-tuple-element.55), channel_id=1, source_target_pairs={{0,2},{1,3},{2,0},{3,1},{4,6},{5,7},{6,4},{7,5},{8,10},{9,11},{10,... | collective-permute-start | bytes 393224 | tf_op jit(solution)/shard_map/ppermute | solution.py:346
  75.8 1.9 %collective-permute-start.8 = (bf16[2,1,2,128,128]{4,3,2,1,0:T(8,128)(2,1)S(1)}, bf16[2,1,2,128,128]{4,3,2,1,0:T(8,128)(2,1)S(1)}, u32[]{:S(2)}, u32[]{:S(2)}) collective-permute-start(bf16[2,1,2,128,128]{4,3,2,1,0:T(8,128)(2,1)S(1)} %get-tuple-element.56), channel_id=1, source_target_pairs={{0,3},{1,2},{2,1},{3,0},{4,7},{5,6},{6,5},{7,4},{8,11},{9,10},{10,... | collective-permute-start | bytes 393224 | tf_op jit(solution)/shard_map/ppermute | solution.py:346
  77.7 1.0 %shard_map.78.rest_4_ = f32[8,3,2,128,128]{4,3,2,1,0:T(8,128)} custom-call(s32[1]{0:T(128)} %bitcast.me_ref, bf16[2,1,2,128,128]{4,3,2,1,0:T(8,128)(2,1)S(1)} %get-tuple-element.75.rest_0_, bf16[2,1,2,128,128]{4,3,2,1,0:T(8,128)(2,1)S(1)} %collective-permute-done.24.rest_1_, bf16[2,1,2,128,128]{4,3,2,1,0:T(8,128)(2,1)S(1)} %collective-permute-done.25.rest_2_, ...), custom_call_target="tpu_custom_call" | custom-call | flops 1048576 | bytes 2097152 | tf_op jit(solution)/shard_map/pallas_call | solution.py:297
  79.6 1.8 %collective-permute-done.17.rest_3_ = bf16[2,1,2,128,128]{4,3,2,1,0:T(8,128)(2,1)S(1)} collective-permute-done((bf16[2,1,2,128,128]{4,3,2,1,0:T(8,128)(2,1)S(1)}, bf16[2,1,2,128,128]{4,3,2,1,0:T(8,128)(2,1)S(1)}, u32[]{:S(2)}, u32[]{:S(2)}) %collective-permute-start.17) | collective-permute-done | bytes 131104 | tf_op jit(solution)/shard_map/ppermute | solution.py:346
  81.4 1.0 %shard_map.79.rest_4_ = f32[8,3,2,128,128]{4,3,2,1,0:T(8,128)} custom-call(s32[1]{0:T(128)} %bitcast.me_ref, bf16[2,1,2,128,128]{4,3,2,1,0:T(8,128)(2,1)S(1)} %get-tuple-element.64.rest_0_, bf16[2,1,2,128,128]{4,3,2,1,0:T(8,128)(2,1)S(1)} %collective-permute-done.15.rest_1_, ...), custom_call_target="tpu_custom_call", output_to_operand_aliasing={{}: (5, {})} | custom-call | flops 1048576 | bytes 2097152 | tf_op jit(solution)/shard_map/pallas_call | solution.py:297
  82.4 2.8 %collective-permute-done.7.rest_2_ = bf16[2,1,2,128,128]{4,3,2,1,0:T(8,128)(2,1)S(1)} collective-permute-done((bf16[2,1,2,128,128]{4,3,2,1,0:T(8,128)(2,1)S(1)}, bf16[2,1,2,128,128]{4,3,2,1,0:T(8,128)(2,1)S(1)}, u32[]{:S(2)}, u32[]{:S(2)}) %collective-permute-start.7) | collective-permute-done | bytes 131104 | tf_op jit(solution)/shard_map/ppermute | solution.py:346
  85.2 1.0 %collective-permute-done.8.rest_3_ = bf16[2,1,2,128,128]{4,3,2,1,0:T(8,128)(2,1)S(1)} collective-permute-done((bf16[2,1,2,128,128]{4,3,2,1,0:T(8,128)(2,1)S(1)}, bf16[2,1,2,128,128]{4,3,2,1,0:T(8,128)(2,1)S(1)}, u32[]{:S(2)}, u32[]{:S(2)}) %collective-permute-start.8) | collective-permute-done | bytes 131104 | tf_op jit(solution)/shard_map/ppermute | solution.py:346
  86.2 1.0 %shard_map.80 = f32[8,3,2,128,128]{4,3,2,1,0:T(8,128)} custom-call(s32[1]{0:T(128)} %bitcast.me_ref, bf16[2,1,2,128,128]{4,3,2,1,0:T(8,128)(2,1)S(1)} %get-tuple-element.53.rest_0_, bf16[2,1,2,128,128]{4,3,2,1,0:T(8,128)(2,1)S(1)} %collective-permute-done.6.rest_1_, ...), custom_call_target="tpu_custom_call", output_to_operand_aliasing={{}: (5, {})} | custom-call | flops 1048576 | bytes 2097152 | tf_op jit(solution)/shard_map/pallas_call | solution.py:297
  (52 shorter events, 7.4 us)
Async XLA Ops:
  7.6 17.9 %collective-permute-start.18 = (bf16[256,256]{1,0:T(8,128)(2,1)S(1)}, bf16[256,256]{1,0:T(8,128)(2,1)S(1)}, u32[]{:S(2)}, u32[]{:S(2)}) collective-permute-start(bf16[256,256]{1,0:T(8,128)(2,1)S(1)} %get-tuple-element.69), channel_id=1, source_target_pairs={{0,12},{4,16},{8,20},{12,24},{16,28},{20,0},{24,4},{28,8},{1,13},{... | collective-permute-start | bytes 393224 | tf_op jit(solution)/shard_map/ppermute | solution.py:21
  11.6 13.8 %collective-permute-start.19 = (bf16[256,256]{1,0:T(8,128)(2,1)S(1)}, bf16[256,256]{1,0:T(8,128)(2,1)S(1)}, u32[]{:S(2)}, u32[]{:S(2)}) collective-permute-start(bf16[256,256]{1,0:T(8,128)(2,1)S(1)} %get-tuple-element.70), channel_id=1, source_target_pairs={{0,8},{4,12},{8,16},{12,20},{16,24},{20,28},{24,0},{28,4},{1,9},{5... | collective-permute-start | bytes 393224 | tf_op jit(solution)/shard_map/ppermute | solution.py:21
  13.2 15.2 %collective-permute-start.20 = (bf16[256,256]{1,0:T(8,128)(2,1)S(1)}, bf16[256,256]{1,0:T(8,128)(2,1)S(1)}, u32[]{:S(2)}, u32[]{:S(2)}) collective-permute-start(bf16[256,256]{1,0:T(8,128)(2,1)S(1)} %get-tuple-element.71), channel_id=1, source_target_pairs={{0,4},{4,8},{8,12},{12,16},{16,20},{20,24},{24,28},{28,0},{1,5},{5... | collective-permute-start | bytes 393224 | tf_op jit(solution)/shard_map/ppermute | solution.py:21
  14.7 17.3 %collective-permute-start.21 = (bf16[256,256]{1,0:T(8,128)(2,1)S(1)}, bf16[256,256]{1,0:T(8,128)(2,1)S(1)}, u32[]{:S(2)}, u32[]{:S(2)}) collective-permute-start(bf16[256,256]{1,0:T(8,128)(2,1)S(1)} %get-tuple-element.72), channel_id=1, source_target_pairs={{0,28},{4,0},{8,4},{12,8},{16,12},{20,16},{24,20},{28,24},{1,29},{... | collective-permute-start | bytes 393224 | tf_op jit(solution)/shard_map/ppermute | solution.py:21
  17.9 16.4 %collective-permute-start.22 = (bf16[256,256]{1,0:T(8,128)(2,1)S(1)}, bf16[256,256]{1,0:T(8,128)(2,1)S(1)}, u32[]{:S(2)}, u32[]{:S(2)}) collective-permute-start(bf16[256,256]{1,0:T(8,128)(2,1)S(1)} %get-tuple-element.73), channel_id=1, source_target_pairs={{0,24},{4,28},{8,0},{12,4},{16,8},{20,12},{24,16},{28,20},{1,25},{... | collective-permute-start | bytes 393224 | tf_op jit(solution)/shard_map/ppermute | solution.py:21
  25.5 11.3 %collective-permute-start.23 = (bf16[256,256]{1,0:T(8,128)(2,1)S(1)}, bf16[256,256]{1,0:T(8,128)(2,1)S(1)}, u32[]{:S(2)}, u32[]{:S(2)}) collective-permute-start(bf16[256,256]{1,0:T(8,128)(2,1)S(1)} %get-tuple-element.74), channel_id=1, source_target_pairs={{0,20},{4,24},{8,28},{12,0},{16,4},{20,8},{24,12},{28,16},{1,21},{... | collective-permute-start | bytes 393224 | tf_op jit(solution)/shard_map/ppermute | solution.py:21
  25.5 16.9 %collective-permute-start.9 = (bf16[256,256]{1,0:T(8,128)(2,1)S(1)}, bf16[256,256]{1,0:T(8,128)(2,1)S(1)}, u32[]{:S(2)}, u32[]{:S(2)}) collective-permute-start(bf16[256,256]{1,0:T(8,128)(2,1)S(1)} %get-tuple-element.58), channel_id=1, source_target_pairs={{0,12},{4,16},{8,20},{12,24},{16,28},{20,0},{24,4},{28,8},{1,13},{... | collective-permute-start | bytes 393224 | tf_op jit(solution)/shard_map/ppermute | solution.py:21
  28.4 18.9 %collective-permute-start.10 = (bf16[256,256]{1,0:T(8,128)(2,1)S(1)}, bf16[256,256]{1,0:T(8,128)(2,1)S(1)}, u32[]{:S(2)}, u32[]{:S(2)}) collective-permute-start(bf16[256,256]{1,0:T(8,128)(2,1)S(1)} %get-tuple-element.59), channel_id=1, source_target_pairs={{0,8},{4,12},{8,16},{12,20},{16,24},{20,28},{24,0},{28,4},{1,9},{5... | collective-permute-start | bytes 393224 | tf_op jit(solution)/shard_map/ppermute | solution.py:21
  32.1 18.2 %collective-permute-start.11 = (bf16[256,256]{1,0:T(8,128)(2,1)S(1)}, bf16[256,256]{1,0:T(8,128)(2,1)S(1)}, u32[]{:S(2)}, u32[]{:S(2)}) collective-permute-start(bf16[256,256]{1,0:T(8,128)(2,1)S(1)} %get-tuple-element.60), channel_id=1, source_target_pairs={{0,4},{4,8},{8,12},{12,16},{16,20},{20,24},{24,28},{28,0},{1,5},{5... | collective-permute-start | bytes 393224 | tf_op jit(solution)/shard_map/ppermute | solution.py:21
  34.4 15.9 %collective-permute-start.12 = (bf16[256,256]{1,0:T(8,128)(2,1)S(1)}, bf16[256,256]{1,0:T(8,128)(2,1)S(1)}, u32[]{:S(2)}, u32[]{:S(2)}) collective-permute-start(bf16[256,256]{1,0:T(8,128)(2,1)S(1)} %get-tuple-element.61), channel_id=1, source_target_pairs={{0,28},{4,0},{8,4},{12,8},{16,12},{20,16},{24,20},{28,24},{1,29},{... | collective-permute-start | bytes 393224 | tf_op jit(solution)/shard_map/ppermute | solution.py:21
  36.8 14.1 %collective-permute-start.13 = (bf16[256,256]{1,0:T(8,128)(2,1)S(1)}, bf16[256,256]{1,0:T(8,128)(2,1)S(1)}, u32[]{:S(2)}, u32[]{:S(2)}) collective-permute-start(bf16[256,256]{1,0:T(8,128)(2,1)S(1)} %get-tuple-element.62), channel_id=1, source_target_pairs={{0,24},{4,28},{8,0},{12,4},{16,8},{20,12},{24,16},{28,20},{1,25},{... | collective-permute-start | bytes 393224 | tf_op jit(solution)/shard_map/ppermute | solution.py:21
  42.3 12.7 %collective-permute-start.14 = (bf16[256,256]{1,0:T(8,128)(2,1)S(1)}, bf16[256,256]{1,0:T(8,128)(2,1)S(1)}, u32[]{:S(2)}, u32[]{:S(2)}) collective-permute-start(bf16[256,256]{1,0:T(8,128)(2,1)S(1)} %get-tuple-element.63), channel_id=1, source_target_pairs={{0,20},{4,24},{8,28},{12,0},{16,4},{20,8},{24,12},{28,16},{1,21},{... | collective-permute-start | bytes 393224 | tf_op jit(solution)/shard_map/ppermute | solution.py:21
  47.3 12.4 %copy-start.9 = (bf16[256,256]{1,0:T(8,128)(2,1)}, bf16[256,256]{1,0:T(8,128)(2,1)S(1)}, u32[]{:S(2)}) copy-start(bf16[256,256]{1,0:T(8,128)(2,1)S(1)} %get-tuple-element.52) | copy-start | bytes 393220
  47.3 15.1 %collective-permute-start = (bf16[256,256]{1,0:T(8,128)(2,1)}, bf16[256,256]{1,0:T(8,128)(2,1)S(1)}, u32[]{:S(2)}, u32[]{:S(2)}) collective-permute-start(bf16[256,256]{1,0:T(8,128)(2,1)} %get-tuple-element.47), channel_id=1, source_target_pairs={{0,12},{4,16},{8,20},{12,24},{16,28},{20,0},{24,4},{28,8},{1,13},{... | collective-permute-start | bytes 393224 | tf_op jit(solution)/shard_map/ppermute | solution.py:21
  50.3 9.4 %copy-start = (bf16[256,256]{1,0:T(8,128)(2,1)}, bf16[256,256]{1,0:T(8,128)(2,1)S(1)}, u32[]{:S(2)}) copy-start(bf16[256,256]{1,0:T(8,128)(2,1)S(1)} %collective-permute-done.11.rest_3_) | copy-start | bytes 393220
  50.3 16.7 %collective-permute-start.1 = (bf16[256,256]{1,0:T(8,128)(2,1)}, bf16[256,256]{1,0:T(8,128)(2,1)}, u32[]{:S(2)}, u32[]{:S(2)}) collective-permute-start(bf16[256,256]{1,0:T(8,128)(2,1)} %get-tuple-element.48), channel_id=1, source_target_pairs={{0,8},{4,12},{8,16},{12,20},{16,24},{20,28},{24,0},{28,4},{1,9},{5... | collective-permute-start | bytes 393224 | tf_op jit(solution)/shard_map/ppermute | solution.py:21
  50.3 9.4 %copy-start.2 = (bf16[256,256]{1,0:T(8,128)(2,1)}, bf16[256,256]{1,0:T(8,128)(2,1)S(1)}, u32[]{:S(2)}) copy-start(bf16[256,256]{1,0:T(8,128)(2,1)S(1)} %collective-permute-done.12.rest_4_) | copy-start | bytes 393220
  50.3 16.8 %collective-permute-start.2 = (bf16[256,256]{1,0:T(8,128)(2,1)}, bf16[256,256]{1,0:T(8,128)(2,1)}, u32[]{:S(2)}, u32[]{:S(2)}) collective-permute-start(bf16[256,256]{1,0:T(8,128)(2,1)} %get-tuple-element.49), channel_id=1, source_target_pairs={{0,4},{4,8},{8,12},{12,16},{16,20},{20,24},{24,28},{28,0},{1,5},{5... | collective-permute-start | bytes 393224 | tf_op jit(solution)/shard_map/ppermute | solution.py:21
  50.9 8.8 %copy-start.4 = (bf16[256,256]{1,0:T(8,128)(2,1)}, bf16[256,256]{1,0:T(8,128)(2,1)S(1)}, u32[]{:S(2)}) copy-start(bf16[256,256]{1,0:T(8,128)(2,1)S(1)} %collective-permute-done.13.rest_5_) | copy-start | bytes 393220
  50.9 16.7 %collective-permute-start.3 = (bf16[256,256]{1,0:T(8,128)(2,1)}, bf16[256,256]{1,0:T(8,128)(2,1)}, u32[]{:S(2)}, u32[]{:S(2)}) collective-permute-start(bf16[256,256]{1,0:T(8,128)(2,1)} %get-tuple-element.50), channel_id=1, source_target_pairs={{0,28},{4,0},{8,4},{12,8},{16,12},{20,16},{24,20},{28,24},{1,29},{... | collective-permute-start | bytes 393224 | tf_op jit(solution)/shard_map/ppermute | solution.py:21
  55.1 4.7 %copy-start.8 = (s32[1,6,1]{1,2,0:T(1,128)S(1)}, s32[1,6,1]{1,2,0:T(1,128)}, u32[]{:S(2)}) copy-start(s32[1,6,1]{1,2,0:T(1,128)} %param.13) | copy-start | bytes 76
  55.1 14.0 %collective-permute-start.4 = (bf16[256,256]{1,0:T(8,128)(2,1)}, bf16[256,256]{1,0:T(8,128)(2,1)}, u32[]{:S(2)}, u32[]{:S(2)}) collective-permute-start(bf16[256,256]{1,0:T(8,128)(2,1)} %get-tuple-element.51), channel_id=1, source_target_pairs={{0,24},{4,28},{8,0},{12,4},{16,8},{20,12},{24,16},{28,20},{1,25},{... | collective-permute-start | bytes 393224 | tf_op jit(solution)/shard_map/ppermute | solution.py:21
  62.4 6.7 %collective-permute-start.5 = (bf16[256,256]{1,0:T(8,128)(2,1)}, bf16[256,256]{1,0:T(8,128)(2,1)S(1)}, u32[]{:S(2)}, u32[]{:S(2)}) collective-permute-start(bf16[256,256]{1,0:T(8,128)(2,1)} %copy-done.9), channel_id=1, source_target_pairs={{0,20},{4,24},{8,28},{12,0},{16,4},{20,8},{24,12},{28,16},{1,21},{... | collective-permute-start | bytes 393224 | tf_op jit(solution)/shard_map/ppermute | solution.py:21
  67.0 5.0 %collective-permute-start.15 = (bf16[2,1,2,128,128]{4,3,2,1,0:T(8,128)(2,1)S(1)}, bf16[2,1,2,128,128]{4,3,2,1,0:T(8,128)(2,1)S(1)}, u32[]{:S(2)}, u32[]{:S(2)}) collective-permute-start(bf16[2,1,2,128,128]{4,3,2,1,0:T(8,128)(2,1)S(1)} %get-tuple-element.65), channel_id=1, source_target_pairs={{0,1},{1,0},{2,3},{3,2},{4,5},{5,4},{6,7},{7,6},{8,9},{9,8},{10,11... | collective-permute-start | bytes 393224 | tf_op jit(solution)/shard_map/ppermute | solution.py:346
  67.1 5.6 %collective-permute-start.24 = (bf16[2,1,2,128,128]{4,3,2,1,0:T(8,128)(2,1)S(1)}, bf16[2,1,2,128,128]{4,3,2,1,0:T(8,128)(2,1)S(1)}, u32[]{:S(2)}, u32[]{:S(2)}) collective-permute-start(bf16[2,1,2,128,128]{4,3,2,1,0:T(8,128)(2,1)S(1)} %get-tuple-element.76), channel_id=1, source_target_pairs={{0,1},{1,0},{2,3},{3,2},{4,5},{5,4},{6,7},{7,6},{8,9},{9,8},{10,11... | collective-permute-start | bytes 393224 | tf_op jit(solution)/shard_map/ppermute | solution.py:346
  67.6 6.4 %collective-permute-start.25 = (bf16[2,1,2,128,128]{4,3,2,1,0:T(8,128)(2,1)S(1)}, bf16[2,1,2,128,128]{4,3,2,1,0:T(8,128)(2,1)S(1)}, u32[]{:S(2)}, u32[]{:S(2)}) collective-permute-start(bf16[2,1,2,128,128]{4,3,2,1,0:T(8,128)(2,1)S(1)} %get-tuple-element.77), channel_id=1, source_target_pairs={{0,2},{1,3},{2,0},{3,1},{4,6},{5,7},{6,4},{7,5},{8,10},{9,11},{10,... | collective-permute-start | bytes 393224 | tf_op jit(solution)/shard_map/ppermute | solution.py:346
  69.1 6.7 %collective-permute-start.26 = (bf16[2,1,2,128,128]{4,3,2,1,0:T(8,128)(2,1)S(1)}, bf16[2,1,2,128,128]{4,3,2,1,0:T(8,128)(2,1)S(1)}, u32[]{:S(2)}, u32[]{:S(2)}) collective-permute-start(bf16[2,1,2,128,128]{4,3,2,1,0:T(8,128)(2,1)S(1)} %get-tuple-element.78), channel_id=1, source_target_pairs={{0,3},{1,2},{2,1},{3,0},{4,7},{5,6},{6,5},{7,4},{8,11},{9,10},{10,... | collective-permute-start | bytes 393224 | tf_op jit(solution)/shard_map/ppermute | solution.py:346
  69.1 10.5 %collective-permute-start.16 = (bf16[2,1,2,128,128]{4,3,2,1,0:T(8,128)(2,1)S(1)}, bf16[2,1,2,128,128]{4,3,2,1,0:T(8,128)(2,1)S(1)}, u32[]{:S(2)}, u32[]{:S(2)}) collective-permute-start(bf16[2,1,2,128,128]{4,3,2,1,0:T(8,128)(2,1)S(1)} %get-tuple-element.66), channel_id=1, source_target_pairs={{0,2},{1,3},{2,0},{3,1},{4,6},{5,7},{6,4},{7,5},{8,10},{9,11},{10,... | collective-permute-start | bytes 393224 | tf_op jit(solution)/shard_map/ppermute | solution.py:346
  72.1 9.3 %collective-permute-start.17 = (bf16[2,1,2,128,128]{4,3,2,1,0:T(8,128)(2,1)S(1)}, bf16[2,1,2,128,128]{4,3,2,1,0:T(8,128)(2,1)S(1)}, u32[]{:S(2)}, u32[]{:S(2)}) collective-permute-start(bf16[2,1,2,128,128]{4,3,2,1,0:T(8,128)(2,1)S(1)} %get-tuple-element.67), channel_id=1, source_target_pairs={{0,3},{1,2},{2,1},{3,0},{4,7},{5,6},{6,5},{7,4},{8,11},{9,10},{10,... | collective-permute-start | bytes 393224 | tf_op jit(solution)/shard_map/ppermute | solution.py:346
  72.7 9.7 %collective-permute-start.6 = (bf16[2,1,2,128,128]{4,3,2,1,0:T(8,128)(2,1)S(1)}, bf16[2,1,2,128,128]{4,3,2,1,0:T(8,128)(2,1)S(1)}, u32[]{:S(2)}, u32[]{:S(2)}) collective-permute-start(bf16[2,1,2,128,128]{4,3,2,1,0:T(8,128)(2,1)S(1)} %get-tuple-element.54), channel_id=1, source_target_pairs={{0,1},{1,0},{2,3},{3,2},{4,5},{5,4},{6,7},{7,6},{8,9},{9,8},{10,11... | collective-permute-start | bytes 393224 | tf_op jit(solution)/shard_map/ppermute | solution.py:346
  74.0 11.2 %collective-permute-start.7 = (bf16[2,1,2,128,128]{4,3,2,1,0:T(8,128)(2,1)S(1)}, bf16[2,1,2,128,128]{4,3,2,1,0:T(8,128)(2,1)S(1)}, u32[]{:S(2)}, u32[]{:S(2)}) collective-permute-start(bf16[2,1,2,128,128]{4,3,2,1,0:T(8,128)(2,1)S(1)} %get-tuple-element.55), channel_id=1, source_target_pairs={{0,2},{1,3},{2,0},{3,1},{4,6},{5,7},{6,4},{7,5},{8,10},{9,11},{10,... | collective-permute-start | bytes 393224 | tf_op jit(solution)/shard_map/ppermute | solution.py:346
  75.8 10.5 %collective-permute-start.8 = (bf16[2,1,2,128,128]{4,3,2,1,0:T(8,128)(2,1)S(1)}, bf16[2,1,2,128,128]{4,3,2,1,0:T(8,128)(2,1)S(1)}, u32[]{:S(2)}, u32[]{:S(2)}) collective-permute-start(bf16[2,1,2,128,128]{4,3,2,1,0:T(8,128)(2,1)S(1)} %get-tuple-element.56), channel_id=1, source_target_pairs={{0,3},{1,2},{2,1},{3,0},{4,7},{5,6},{6,5},{7,4},{8,11},{9,10},{10,... | collective-permute-start | bytes 393224 | tf_op jit(solution)/shard_map/ppermute | solution.py:346
  (5 other events, 8.3 us)

commit v2 on v1

--- a/solution.py
+++ b/solution.py
@@ -15,10 +15,28 @@
 SMALL_VMEM = 12 * 1024 * 1024
 
 
-def passed_along(value, axis, steps):
-    count = lax.axis_size(axis)
-    pairs = [(source, (source + steps) % count) for source in range(count)]
-    return lax.ppermute(value, axis, pairs)
+def exchange_plan(count):
+    wanted = sorted(offset % count for offset in OFFSETS)
+    masks = [
+        mask
+        for mask in range(1, count)
+        if all(((node ^ mask) - node) % count in wanted for node in range(count))
+    ]
+    if count & (count - 1) == 0 and len(masks) == len(OFFSETS):
+        masks.sort(key=lambda mask: (mask < count // 2, bin(mask).count("1"), -mask))
+        return [("xor", mask) for mask in masks]
+    return [("shift", offset) for offset in OFFSETS[::-1]]
+
+
+def exchange_slot(plan, count, me):
+    kind, amount = plan
+    if kind == "shift":
+        return OFFSETS.index(amount)
+    step = lax.rem((me ^ amount) - me + count, count)
+    slot = jnp.int32(0)
+    for index, offset in enumerate(OFFSETS):
+        slot += jnp.where(step == offset % count, index, 0)
+    return slot
 
 
 def partner(index, hop, count):
@@ -39,22 +57,24 @@
     return lax.rem(index - hop + count, count)
 
 
-def fill_selector(rows_ref, counts_ref, neighbours_ref, selector):
+def fill_selector(plans, count, rows_ref, counts_ref, neighbours_ref, selector):
     slots, _, margin = rows_ref.shape
     edges = selector.shape[1]
+    me = lax.axis_index("dom")
     positions = lax.broadcasted_iota(jnp.int32, (1, margin), 1)
     lanes = lax.broadcasted_iota(jnp.int32, (1, edges), 1).astype(F32)
     masked = []
-    for slot in range(8):
-        if slot < slots:
+    for place in range(8):
+        if place < slots:
+            slot = exchange_slot(plans[place], count, me)
             live = (positions < counts_ref[0, slot]) & (neighbours_ref[0, slot] >= 0)
             masked.append(jnp.where(live, rows_ref[slot], -1).astype(F32))
         else:
             masked.append(jnp.full((1, margin), -1.0, F32))
     columns = jnp.transpose(jnp.concatenate(masked, axis=0))
-    for slot in range(slots):
-        hit = columns[:, slot : slot + 1] == lanes
-        selector[slot * margin : (slot + 1) * margin, :] = jnp.where(hit, 1.0, 0.0).astype(BF16)
+    for place in range(slots):
+        hit = columns[:, place : place + 1] == lanes
+        selector[place * margin : (place + 1) * margin, :] = jnp.where(hit, 1.0, 0.0).astype(BF16)
 
 
 def gather_vectors(z_wide, index, sets, width, a, b):
@@ -90,37 +110,42 @@
         ).astype(BF16)
 
 
-def first_chain_kernel(sets, width, *refs):
-    counts_ref, neighbours_ref, rows_ref, z_ref, inverse_ref, operator_ref = refs[:6]
-    slots = rows_ref.shape[0]
+def first_chain_kernel(plans, count, sets, width, *refs):
+    counts, neighbours, rows, z_ref, inverse_ref, operator_ref = refs[:6]
+    slots = rows.shape[0]
     outs = refs[6 : 6 + slots]
     inverse, operator, selector, z_wide = refs[6 + slots : 10 + slots]
     z_in, first_a, first_b, second_a, second_b, sems = refs[10 + slots :]
     block = inverse.shape[1] // 2
+
+    def fetch(source, target, part, sem):
+        at = pl.ds(part * block, block)
+        return pltpu.make_async_copy(source.at[:, at], target.at[:, at], sem)
+
     z_copy = pltpu.make_async_copy(z_ref, z_in, sems.at[0])
-    z_copy.start()
-
-    def fetch(source, target, half, sem):
-        at = pl.ds(half * block, block)
-        return pltpu.make_async_copy(source.at[:, at], target.at[:, at], sem)
-
-    loads = [fetch(inverse_ref, inverse, half, sems.at[1 + half]) for half in range(2)]
-    loads += [fetch(operator_ref, operator, half, sems.at[3 + half]) for half in range(2)]
-    loads[0].start()
-    loads[1].start()
-    fill_selector(rows_ref, counts_ref, neighbours_ref, selector)
+    inverse_loads = [fetch(inverse_ref, inverse, part, sems.at[1 + part]) for part in range(2)]
+    operator_loads = [fetch(operator_ref, operator, part, sems.at[3 + part]) for part in range(2)]
+    for copy in [z_copy] + inverse_loads:
+        copy.start()
+    fill_selector(plans, count, rows, counts, neighbours, selector)
     z_copy.wait()
     z_wide[...] = z_in[...].astype(F32)
     gather_vectors(z_wide, 0, sets, width, first_a, first_b)
 
     def begin():
-        loads[0].wait()
-        loads[2].start()
-        loads[3].start()
-
-    apply(inverse, {0: begin, 2: loads[1].wait}, width, first_a, first_b, second_a, second_b)
+        inverse_loads[0].wait()
+        for copy in operator_loads:
+            copy.start()
+
+    waits = {2: inverse_loads[1].wait}
+    apply(inverse, {0: begin, **waits}, width, first_a, first_b, second_a, second_b)
     apply(inverse, {}, width, second_a, second_b, first_a, first_b)
-    apply(operator, {0: loads[2].wait, 2: loads[3].wait}, width, first_a, first_b, second_a, None)
+
+    def ready():
+        operator_loads[0].wait()
+        operator_loads[1].wait()
+
+    apply(operator, {0: ready}, width, first_a, first_b, second_a, None)
     pick_rows(selector, second_a, outs)
 
 
@@ -132,7 +157,7 @@
     return [pltpu.with_memory_space_constraint(value, pltpu.VMEM) for value in values]
 
 
-def first_chain(sets, width, counts, neighbours, rows, z, inverse, operator):
+def first_chain(plans, count, sets, width, counts, neighbours, rows, z, inverse, operator):
     slots, _, margin = rows.shape
     edges = inverse.shape[1]
     hbm = pl.BlockSpec(memory_space=pltpu.HBM)
@@ -146,11 +171,13 @@
         pltpu.VMEM(z.shape, F32),
     ]
     results = pl.pallas_call(
-        functools.partial(first_chain_kernel, sets, width),
+        functools.partial(first_chain_kernel, plans, count, sets, width),
         out_shape=outs,
         in_specs=[smem, smem, vmem, hbm, hbm, hbm],
         out_specs=[vmem] * len(outs),
-        scratch_shapes=[pltpu.VMEM(z.shape, BF16)]
+        scratch_shapes=[
+            pltpu.VMEM(z.shape, BF16),
+        ]
         + [pltpu.VMEM((edges, 2 * width), BF16)] * 4
         + [pltpu.SemaphoreType.DMA((5,))],
         compiler_params=pltpu.CompilerParams(vmem_limit_bytes=CHAIN_VMEM),
@@ -222,18 +249,21 @@
     )(*in_vmem(selector, z_wide))
 
 
-def gram_kernel(group, width, hops, capacity, owners_ref, me_ref, *rest):
+def gram_kernel(plans, count, group, width, hops, capacity, owners_ref, *rest):
     projectors, rest = rest[: len(group)], rest[len(group) :]
     slots = projectors[0].shape[0]
     incoming, outs, packed = rest[:slots], rest[slots : slots + hops], rest[-1]
-    me = me_ref[0]
+    me = lax.axis_index("grp")
+    here = lax.axis_index("dom")
     packed[...] = jnp.zeros_like(packed)
     step = 2 * width
     for slot in range(slots):
-        owner = owners_ref[0, slot]
+        mine = exchange_slot(plans[slot], count, here)
+        owner = owners_ref[0, mine]
         rank = jnp.int32(0)
-        for other in range(slot):
-            rank += (owners_ref[0, other] == owner).astype(jnp.int32)
+        for other in range(slots):
+            same = (owners_ref[0, other] == owner) & (other < mine)
+            rank += same.astype(jnp.int32)
         place = hop_to(me, owner, hops) * capacity + rank
         for at in range(len(group)):
             gram = jnp.dot(
@@ -247,15 +277,15 @@
         outs[hop][...] = packed[hop * capacity : (hop + 1) * capacity]
 
 
-def gram_blocks(group, width, hops, capacity, owners, me, projectors, incoming):
+def gram_blocks(plans, count, group, width, hops, capacity, owners, projectors, incoming):
     smem = pl.BlockSpec(memory_space=pltpu.SMEM)
     vmem = pl.BlockSpec(memory_space=pltpu.VMEM)
     block = (capacity, len(group), 2, width, width)
     slots, _, margin = projectors[0].shape
     return pl.pallas_call(
-        functools.partial(gram_kernel, group, width, hops, capacity),
+        functools.partial(gram_kernel, plans, count, group, width, hops, capacity),
         out_shape=[jax.ShapeDtypeStruct(block, BF16)] * hops,
-        in_specs=[smem, smem] + [vmem] * (len(group) + len(incoming)),
+        in_specs=[smem] + [vmem] * (len(group) + len(incoming)),
         out_specs=[vmem] * hops,
         scratch_shapes=[pltpu.VMEM((hops * capacity,) + block[1:], BF16)],
         compiler_params=pltpu.CompilerParams(vmem_limit_bytes=SMALL_VMEM),
@@ -264,20 +294,19 @@
             bytes_accessed=2 << 20,
             transcendentals=0,
         ),
-    )(owners, me, *projectors, *incoming)
-
-
-def spread(group, sets, width, capacity, me, arrived, held):
+    )(owners, *projectors, *incoming)
+
+
+def spread(group, sets, width, capacity, arrived, held):
     hops = len(arrived)
-    smem = pl.BlockSpec(memory_space=pltpu.SMEM)
     vmem = pl.BlockSpec(memory_space=pltpu.VMEM)
     any_space = pl.BlockSpec(memory_space=pl.ANY)
     places = hops * capacity
     extra = [] if held is None else [held]
 
-    def body(me_ref, *rest):
+    def body(*rest):
         inputs, (out_ref, wide, sem) = rest[:hops], rest[-3:]
-        mine = me_ref[0]
+        mine = lax.axis_index("grp")
         copies = []
         for hop in range(hops):
             source = hop_from(mine, hop, hops)
@@ -297,22 +326,27 @@
     return pl.pallas_call(
         body,
         out_shape=jax.ShapeDtypeStruct((places, sets, 2, width, width), F32),
-        in_specs=[smem] + [vmem] * hops + [any_space] * len(extra),
+        in_specs=[vmem] * hops + [any_space] * len(extra),
         out_specs=any_space,
         scratch_shapes=[
             pltpu.VMEM((places, len(group), 2, width, width), F32),
             pltpu.SemaphoreType.DMA((hops,)),
         ],
-        input_output_aliases={1 + hops: 0} if extra else {},
+        input_output_aliases={hops: 0} if extra else {},
         compiler_params=pltpu.CompilerParams(vmem_limit_bytes=SMALL_VMEM),
         cost_estimate=pl.CostEstimate(flops=1 << 20, bytes_accessed=2 << 20, transcendentals=0),
-    )(me, *arrived, *extra)
-
-
-def exchanged(outgoing):
+    )(*arrived, *extra)
+
+
+def exchanged(plans, count, outgoing):
     pieces = [None] * len(outgoing)
-    for slot, offset in enumerate(OFFSETS):
-        pieces[len(outgoing) - 1 - slot] = passed_along(outgoing[slot], "dom", offset)
+    for place, (kind, amount) in enumerate(plans):
+        if kind == "xor":
+            pairs, back = [(node, node ^ amount) for node in range(count)], place
+        else:
+            pairs = [(node, (node + amount) % count) for node in range(count)]
+            back = plans.index((kind, -amount))
+        pieces[back] = lax.ppermute(outgoing[place], "dom", pairs)
     return pieces
 
 
@@ -324,21 +358,22 @@
     z = deflation.reshape(edges * sets * 2, width)
     rows = margin_rows.reshape(slots, 1, margin)
     owned = owners.reshape(1, slots)
-    me = lax.axis_index("grp").astype(jnp.int32).reshape(1)
+    count = lax.axis_size("dom")
+    plans = exchange_plan(count)
     arrived = []
     for index in range(sets):
         if index == 0:
             outgoing, held = first_chain(
-                sets, width, counts, neighbours, rows, z, inverse[0], operator[0]
+                plans, count, sets, width, counts, neighbours, rows, z, inverse[0], operator[0]
             )
         else:
             outgoing = next_chain(index, sets, width, slots, held)
-        arrived.append(exchanged(outgoing))
+        arrived.append(exchanged(plans, count, outgoing))
     projectors = project(sets, width, slots, held)
     received = []
     for index, pieces in enumerate(arrived):
         blocks = gram_blocks(
-            (index,), width, group_count, capacity, owned, me, [projectors[index]], pieces
+            plans, count, (index,), width, group_count, capacity, owned, [projectors[index]], pieces
         )
         sent = [blocks[0]]
         for hop in range(1, group_count):
@@ -347,7 +382,7 @@
         received.append(sent)
     result = None
     for index in range(sets):
-        result = spread((index,), sets, width, capacity, me, received[index], result)
+        result = spread((index,), sets, width, capacity, received[index], result)
     return result
 
 

time: 87.9 us -> 84 us (0.956)
  starting transfers between devices: 39.5 us -> 46.7 us
  waiting for transfers between devices: 17.9 us -> 11.6 us
  local copies, waits for them, and re-layouts: 3.64 us -> 0.01 us
  Pallas kernels: 26 us -> 24.8 us
    ppermute x18, starting transfers between devices: 31.8 us -> 38.8 us  [exchanged(): pieces[back] = lax.ppermute(outgoing[place], 'dom', pairs)]
    ppermute x18, waiting for transfers between devices: 10 us -> 3.54 us  [exchanged(): pieces[back] = lax.ppermute(outgoing[place], 'dom', pairs)]
    unnamed x20 -> x2, local copies, waits for them, and re-layouts: 3.64 us -> 0.01 us
  transfers between devices with their start and end apart: 27 -> 27, of which waited for: 9 -> 8; matrix products, arithmetic and copies ran while one was open for 0% -> 0% of each run, Pallas kernels for 20% -> 20%
where the time goes in v2:
time: 84 us; the launch traced here: 83.5 us
  starting transfers between devices  46.7 us (56%)
  Pallas kernels  24.8 us (30%)
  waiting for transfers between devices  11.6 us (14%)
    ppermute x18, starting transfers between devices, exchanged(): pieces[back] = lax.ppermute(outgoing[place], 'dom', pairs)  38.8 us
    pallas_call x2, Pallas kernels, next_chain(): pl.pallas_call(functools.partial(next_chain_kernel, index, sets, width),...  8.8 us
    ppermute x9, waiting for transfers between devices, on_device(): sent.append(lax.ppermute(blocks[hop], 'grp', pairs))  8.05 us
    ppermute x9, starting transfers between devices, on_device(): sent.append(lax.ppermute(blocks[hop], 'grp', pairs))  7.93 us
    pallas_call x1, Pallas kernels, first_chain(): pl.pallas_call(functools.partial(first_chain_kernel, plans, count, sets,...  7.46 us
    ppermute x18, waiting for transfers between devices, exchanged(): pieces[back] = lax.ppermute(outgoing[place], 'dom', pairs)  3.54 us
    pallas_call x3, Pallas kernels, spread(): pl.pallas_call(body, out_shape=jax.ShapeDtypeStruct((places, sets, 2, wid...  3.06 us
    pallas_call x3, Pallas kernels, gram_blocks(): pl.pallas_call(functools.partial(gram_kernel, plans, count, group, width,...  2.87 us
  transfers between devices with their start and end apart: 27, of which 8 were waited for; matrix products, arithmetic and copies ran while one was open for 0% of the time, Pallas kernels for 20%

profile of v2, /device:TPU:0, one launch (start us, length us, event | category | flops | bytes accessed | tf_op | source)
XLA Modules:
  0.0 83.5 jit_solution(4151261305619530279)
XLA Ops:
  0.0 7.5 %chain0.1 = (bf16[256,256]{1,0:T(8,128)(2,1)S(1)}, bf16[256,256]{1,0:T(8,128)(2,1)S(1)}, bf16[256,256]{1,0:T(8,128)(2,1)S(1)}, bf16[256,256]{1,0:T(8,128)(2,1)S(...) custom-call(s32[1,6]{1,0:T(1,128)} %refs_0_.1, ...), custom_call_target="tpu_custom_call" | custom-call | flops 4026531840 | bytes 12582912 | tf_op jit(solution)/shard_map/chain0/pallas_call | solution.py:173
  7.5 5.1 %collective-permute-start.18 = (bf16[256,256]{1,0:T(8,128)(2,1)S(1)}, bf16[256,256]{1,0:T(8,128)(2,1)S(1)}, u32[]{:S(2)}, u32[]{:S(2)}) collective-permute-start(bf16[256,256]{1,0:T(8,128)(2,1)S(1)} %get-tuple-element.69), channel_id=1, source_target_pairs={{0,24},{4,28},{8,16},{12,20},{16,8},{20,12},{24,0},{28,4},{1,25},{... | collective-permute-start | bytes 393224 | tf_op jit(solution)/shard_map/ppermute | solution.py:349
  13.0 2.4 %collective-permute-start.20 = (bf16[256,256]{1,0:T(8,128)(2,1)S(1)}, bf16[256,256]{1,0:T(8,128)(2,1)S(1)}, u32[]{:S(2)}, u32[]{:S(2)}) collective-permute-start(bf16[256,256]{1,0:T(8,128)(2,1)S(1)} %get-tuple-element.71), channel_id=1, source_target_pairs={{0,28},{4,24},{8,20},{12,16},{16,12},{20,8},{24,4},{28,0},{1,29},{... | collective-permute-start | bytes 393224 | tf_op jit(solution)/shard_map/ppermute | solution.py:349
  15.4 1.6 %collective-permute-start.21 = (bf16[256,256]{1,0:T(8,128)(2,1)S(1)}, bf16[256,256]{1,0:T(8,128)(2,1)S(1)}, u32[]{:S(2)}, u32[]{:S(2)}) collective-permute-start(bf16[256,256]{1,0:T(8,128)(2,1)S(1)} %get-tuple-element.72), channel_id=1, source_target_pairs={{0,8},{4,12},{8,0},{12,4},{16,24},{20,28},{24,16},{28,20},{1,9},{5... | collective-permute-start | bytes 393224 | tf_op jit(solution)/shard_map/ppermute | solution.py:349
  17.0 1.5 %collective-permute-start.22 = (bf16[256,256]{1,0:T(8,128)(2,1)S(1)}, bf16[256,256]{1,0:T(8,128)(2,1)S(1)}, u32[]{:S(2)}, u32[]{:S(2)}) collective-permute-start(bf16[256,256]{1,0:T(8,128)(2,1)S(1)} %get-tuple-element.73), channel_id=1, source_target_pairs={{0,4},{4,0},{8,12},{12,8},{16,20},{20,16},{24,28},{28,24},{1,5},{5... | collective-permute-start | bytes 393224 | tf_op jit(solution)/shard_map/ppermute | solution.py:349
  18.5 4.3 %shard_map.75 = (bf16[256,256]{1,0:T(8,128)(2,1)S(1)}, bf16[256,256]{1,0:T(8,128)(2,1)S(1)}, bf16[256,256]{1,0:T(8,128)(2,1)S(1)}, bf16[256,256]{1,0:T(8,128)(2,...) custom-call(bf16[2,1024,1024]{2,1,0:T(8,128)(2,1)S(1)} %get-tuple-element.45.inverse, ...), custom_call_target="tpu_custom_call" | custom-call | flops 4026531840 | bytes 12582912 | tf_op jit(solution)/shard_map/pallas_call | solution.py:205
  22.8 3.3 %collective-permute-start.23 = (bf16[256,256]{1,0:T(8,128)(2,1)S(1)}, bf16[256,256]{1,0:T(8,128)(2,1)S(1)}, u32[]{:S(2)}, u32[]{:S(2)}) collective-permute-start(bf16[256,256]{1,0:T(8,128)(2,1)S(1)} %get-tuple-element.74), channel_id=1, source_target_pairs={{0,12},{4,8},{8,4},{12,0},{16,28},{20,24},{24,20},{28,16},{1,13},{... | collective-permute-start | bytes 393224 | tf_op jit(solution)/shard_map/ppermute | solution.py:349
  26.1 2.2 %collective-permute-done.19.rest_2_ = bf16[256,256]{1,0:T(8,128)(2,1)S(1)} collective-permute-done((bf16[256,256]{1,0:T(8,128)(2,1)S(1)}, bf16[256,256]{1,0:T(8,128)(2,1)S(1)}, u32[]{:S(2)}, u32[]{:S(2)}) %collective-permute-start.19) | collective-permute-done | bytes 131104 | tf_op jit(solution)/shard_map/ppermute | solution.py:349
  28.4 2.7 %collective-permute-start.9 = (bf16[256,256]{1,0:T(8,128)(2,1)S(1)}, bf16[256,256]{1,0:T(8,128)(2,1)S(1)}, u32[]{:S(2)}, u32[]{:S(2)}) collective-permute-start(bf16[256,256]{1,0:T(8,128)(2,1)S(1)} %get-tuple-element.58), channel_id=1, source_target_pairs={{0,24},{4,28},{8,16},{12,20},{16,8},{20,12},{24,0},{28,4},{1,25},{... | collective-permute-start | bytes 393224 | tf_op jit(solution)/shard_map/ppermute | solution.py:349
  31.1 1.8 %collective-permute-start.10 = (bf16[256,256]{1,0:T(8,128)(2,1)S(1)}, bf16[256,256]{1,0:T(8,128)(2,1)S(1)}, u32[]{:S(2)}, u32[]{:S(2)}) collective-permute-start(bf16[256,256]{1,0:T(8,128)(2,1)S(1)} %get-tuple-element.59), channel_id=1, source_target_pairs={{0,20},{4,16},{8,28},{12,24},{16,4},{20,0},{24,12},{28,8},{1,21},{... | collective-permute-start | bytes 393224 | tf_op jit(solution)/shard_map/ppermute | solution.py:349
  32.9 3.9 %collective-permute-start.11 = (bf16[256,256]{1,0:T(8,128)(2,1)S(1)}, bf16[256,256]{1,0:T(8,128)(2,1)S(1)}, u32[]{:S(2)}, u32[]{:S(2)}) collective-permute-start(bf16[256,256]{1,0:T(8,128)(2,1)S(1)} %get-tuple-element.60), channel_id=1, source_target_pairs={{0,28},{4,24},{8,20},{12,16},{16,12},{20,8},{24,4},{28,0},{1,29},{... | collective-permute-start | bytes 393224 | tf_op jit(solution)/shard_map/ppermute | solution.py:349
  36.9 5.3 %collective-permute-start.14 = (bf16[256,256]{1,0:T(8,128)(2,1)S(1)}, bf16[256,256]{1,0:T(8,128)(2,1)S(1)}, u32[]{:S(2)}, u32[]{:S(2)}) collective-permute-start(bf16[256,256]{1,0:T(8,128)(2,1)S(1)} %get-tuple-element.63), channel_id=1, source_target_pairs={{0,12},{4,8},{8,4},{12,0},{16,28},{20,24},{24,20},{28,16},{1,13},{... | collective-permute-start | bytes 393224 | tf_op jit(solution)/shard_map/ppermute | solution.py:349
  42.2 4.5 %shard_map.73 = (bf16[256,256]{1,0:T(8,128)(2,1)S(1)}, bf16[256,256]{1,0:T(8,128)(2,1)S(1)}, bf16[256,256]{1,0:T(8,128)(2,1)S(1)}, bf16[256,256]{1,0:T(8,128)(2,...) custom-call(bf16[2,1024,1024]{2,1,0:T(8,128)(2,1)S(1)} %get-tuple-element.45.inverse, ...), custom_call_target="tpu_custom_call" | custom-call | flops 4026531840 | bytes 12582912 | tf_op jit(solution)/shard_map/pallas_call | solution.py:205
  46.7 2.5 %collective-permute-start = (bf16[256,256]{1,0:T(8,128)(2,1)S(1)}, bf16[256,256]{1,0:T(8,128)(2,1)S(1)}, u32[]{:S(2)}, u32[]{:S(2)}) collective-permute-start(bf16[256,256]{1,0:T(8,128)(2,1)S(1)} %get-tuple-element.47), channel_id=1, source_target_pairs={{0,24},{4,28},{8,16},{12,20},{16,8},{20,12},{24,0},{28,4},{1,25},{... | collective-permute-start | bytes 393224 | tf_op jit(solution)/shard_map/ppermute | solution.py:349
  50.0 3.8 %collective-permute-start.2 = (bf16[256,256]{1,0:T(8,128)(2,1)S(1)}, bf16[256,256]{1,0:T(8,128)(2,1)S(1)}, u32[]{:S(2)}, u32[]{:S(2)}) collective-permute-start(bf16[256,256]{1,0:T(8,128)(2,1)S(1)} %get-tuple-element.49), channel_id=1, source_target_pairs={{0,28},{4,24},{8,20},{12,16},{16,12},{20,8},{24,4},{28,0},{1,29},{... | collective-permute-start | bytes 393224 | tf_op jit(solution)/shard_map/ppermute | solution.py:349
  53.9 2.7 %project.1 = (bf16[6,256,256]{2,1,0:T(8,128)(2,1)S(1)}, bf16[6,256,256]{2,1,0:T(8,128)(2,1)S(1)}, bf16[6,256,256]{2,1,0:T(8,128)(2,1)S(1)}) custom-call(bf16[1536,1024]{1,0:T(8,128)(2,1)S(1)} %get-tuple-element.42.selector, f32[6144,128]{1,0:T(8,128)S(1)} %get-tuple-element.43.z_wide), custom_call_target="tpu_custom_call" | custom-call | flops 2415919104 | bytes 6291456 | tf_op jit(solution)/shard_map/project/pallas_call | solution.py:238
  56.6 1.0 %shard_map.77 = (bf16[2,1,2,128,128]{4,3,2,1,0:T(8,128)(2,1)S(1)}, bf16[2,1,2,128,128]{4,3,2,1,0:T(8,128)(2,1)S(1)}, bf16[2,1,2,128,128]{4,3,2,1,0:T(8,128)(2,1)S(1)}, bf16[2,1,2,128,128]{4,3,2,1,0:T(8,128)(2,1)S(1)}) custom-call(s32[1,6]{1,0:T(1,128)S(1)} %bitcast.5, bf16[6,256,256]{2,1,0:T(8,128)(2,1)S(1)} %get-tuple-element.68.rest_0_, ...), custom_call_target="tpu_custom_call" | custom-call | flops 201326592 | bytes 2097152 | tf_op jit(solution)/shard_map/pallas_call | solution.py:285
  57.6 3.5 %collective-permute-start.5 = (bf16[256,256]{1,0:T(8,128)(2,1)S(1)}, bf16[256,256]{1,0:T(8,128)(2,1)S(1)}, u32[]{:S(2)}, u32[]{:S(2)}) collective-permute-start(bf16[256,256]{1,0:T(8,128)(2,1)S(1)} %get-tuple-element.52), channel_id=1, source_target_pairs={{0,12},{4,8},{8,4},{12,0},{16,28},{20,24},{24,20},{28,16},{1,13},{... | collective-permute-start | bytes 393224 | tf_op jit(solution)/shard_map/ppermute | solution.py:349
  61.0 1.0 %shard_map.76 = (bf16[2,1,2,128,128]{4,3,2,1,0:T(8,128)(2,1)S(1)}, bf16[2,1,2,128,128]{4,3,2,1,0:T(8,128)(2,1)S(1)}, bf16[2,1,2,128,128]{4,3,2,1,0:T(8,128)(2,1)S(1)}, bf16[2,1,2,128,128]{4,3,2,1,0:T(8,128)(2,1)S(1)}) custom-call(s32[1,6]{1,0:T(1,128)S(1)} %bitcast.6, bf16[6,256,256]{2,1,0:T(8,128)(2,1)S(1)} %get-tuple-element.57.rest_0_, ...), custom_call_target="tpu_custom_call" | custom-call | flops 201326592 | bytes 2097152 | tf_op jit(solution)/shard_map/pallas_call | solution.py:285
  63.2 1.5 %collective-permute-start.25 = (bf16[2,1,2,128,128]{4,3,2,1,0:T(8,128)(2,1)S(1)}, bf16[2,1,2,128,128]{4,3,2,1,0:T(8,128)(2,1)S(1)}, u32[]{:S(2)}, u32[]{:S(2)}) collective-permute-start(bf16[2,1,2,128,128]{4,3,2,1,0:T(8,128)(2,1)S(1)} %get-tuple-element.77), channel_id=1, source_target_pairs={{0,2},{1,3},{2,0},{3,1},{4,6},{5,7},{6,4},{7,5},{8,10},{9,11},{10,... | collective-permute-start | bytes 393224 | tf_op jit(solution)/shard_map/ppermute | solution.py:381
  65.3 1.5 %collective-permute-start.16 = (bf16[2,1,2,128,128]{4,3,2,1,0:T(8,128)(2,1)S(1)}, bf16[2,1,2,128,128]{4,3,2,1,0:T(8,128)(2,1)S(1)}, u32[]{:S(2)}, u32[]{:S(2)}) collective-permute-start(bf16[2,1,2,128,128]{4,3,2,1,0:T(8,128)(2,1)S(1)} %get-tuple-element.66), channel_id=1, source_target_pairs={{0,2},{1,3},{2,0},{3,1},{4,6},{5,7},{6,4},{7,5},{8,10},{9,11},{10,... | collective-permute-start | bytes 393224 | tf_op jit(solution)/shard_map/ppermute | solution.py:381
  66.8 1.0 %shard_map.74 = (bf16[2,1,2,128,128]{4,3,2,1,0:T(8,128)(2,1)S(1)}, bf16[2,1,2,128,128]{4,3,2,1,0:T(8,128)(2,1)S(1)}, bf16[2,1,2,128,128]{4,3,2,1,0:T(8,128)(2,1)S(1)}, bf16[2,1,2,128,128]{4,3,2,1,0:T(8,128)(2,1)S(1)}) custom-call(s32[1,6]{1,0:T(1,128)S(1)} %bitcast.7, bf16[6,256,256]{2,1,0:T(8,128)(2,1)S(1)} %get-tuple-element.44.rest_0_, ...), custom_call_target="tpu_custom_call" | custom-call | flops 201326592 | bytes 2097152 | tf_op jit(solution)/shard_map/pallas_call | solution.py:285
  67.7 1.5 %collective-permute-start.17 = (bf16[2,1,2,128,128]{4,3,2,1,0:T(8,128)(2,1)S(1)}, bf16[2,1,2,128,128]{4,3,2,1,0:T(8,128)(2,1)S(1)}, u32[]{:S(2)}, u32[]{:S(2)}) collective-permute-start(bf16[2,1,2,128,128]{4,3,2,1,0:T(8,128)(2,1)S(1)} %get-tuple-element.67), channel_id=1, source_target_pairs={{0,3},{1,2},{2,1},{3,0},{4,7},{5,6},{6,5},{7,4},{8,11},{9,10},{10,... | collective-permute-start | bytes 393224 | tf_op jit(solution)/shard_map/ppermute | solution.py:381
  69.3 1.2 %collective-permute-start.7 = (bf16[2,1,2,128,128]{4,3,2,1,0:T(8,128)(2,1)S(1)}, bf16[2,1,2,128,128]{4,3,2,1,0:T(8,128)(2,1)S(1)}, u32[]{:S(2)}, u32[]{:S(2)}) collective-permute-start(bf16[2,1,2,128,128]{4,3,2,1,0:T(8,128)(2,1)S(1)} %get-tuple-element.55), channel_id=1, source_target_pairs={{0,2},{1,3},{2,0},{3,1},{4,6},{5,7},{6,4},{7,5},{8,10},{9,11},{10,... | collective-permute-start | bytes 393224 | tf_op jit(solution)/shard_map/ppermute | solution.py:381
  71.1 1.7 %collective-permute-start.8 = (bf16[2,1,2,128,128]{4,3,2,1,0:T(8,128)(2,1)S(1)}, bf16[2,1,2,128,128]{4,3,2,1,0:T(8,128)(2,1)S(1)}, u32[]{:S(2)}, u32[]{:S(2)}) collective-permute-start(bf16[2,1,2,128,128]{4,3,2,1,0:T(8,128)(2,1)S(1)} %get-tuple-element.56), channel_id=1, source_target_pairs={{0,3},{1,2},{2,1},{3,0},{4,7},{5,6},{6,5},{7,4},{8,11},{9,10},{10,... | collective-permute-start | bytes 393224 | tf_op jit(solution)/shard_map/ppermute | solution.py:381
  72.7 1.0 %shard_map.78.rest_4_ = f32[8,3,2,128,128]{4,3,2,1,0:T(8,128)} custom-call(bf16[2,1,2,128,128]{4,3,2,1,0:T(8,128)(2,1)S(1)} %get-tuple-element.75.rest_0_, bf16[2,1,2,128,128]{4,3,2,1,0:T(8,128)(2,1)S(1)} %collective-permute-done.24.rest_1_, bf16[2,1,2,128,128]{4,3,2,1,0:T(8,128)(2,1)S(1)} %collective-permute-done.25.rest_2_, ...), custom_call_target="tpu_custom_call" | custom-call | flops 1048576 | bytes 2097152 | tf_op jit(solution)/shard_map/pallas_call | solution.py:326
  73.8 0.9 %collective-permute-done.16.rest_2_ = bf16[2,1,2,128,128]{4,3,2,1,0:T(8,128)(2,1)S(1)} collective-permute-done((bf16[2,1,2,128,128]{4,3,2,1,0:T(8,128)(2,1)S(1)}, bf16[2,1,2,128,128]{4,3,2,1,0:T(8,128)(2,1)S(1)}, u32[]{:S(2)}, u32[]{:S(2)}) %collective-permute-start.16) | collective-permute-done | bytes 131104 | tf_op jit(solution)/shard_map/ppermute | solution.py:381
  74.6 2.0 %collective-permute-done.17.rest_3_ = bf16[2,1,2,128,128]{4,3,2,1,0:T(8,128)(2,1)S(1)} collective-permute-done((bf16[2,1,2,128,128]{4,3,2,1,0:T(8,128)(2,1)S(1)}, bf16[2,1,2,128,128]{4,3,2,1,0:T(8,128)(2,1)S(1)}, u32[]{:S(2)}, u32[]{:S(2)}) %collective-permute-start.17) | collective-permute-done | bytes 131104 | tf_op jit(solution)/shard_map/ppermute | solution.py:381
  76.7 1.0 %shard_map.79.rest_4_ = f32[8,3,2,128,128]{4,3,2,1,0:T(8,128)} custom-call(bf16[2,1,2,128,128]{4,3,2,1,0:T(8,128)(2,1)S(1)} %get-tuple-element.64.rest_0_, bf16[2,1,2,128,128]{4,3,2,1,0:T(8,128)(2,1)S(1)} %collective-permute-done.15.rest_1_, bf16[2,1,2,128,128]{4,3,2,1,0:T(8,128)(2,1)S(1)} %collective-permute-done.16.rest_2_, ...), custom_call_target="tpu_custom_call", output_to_operand_aliasing={{}: (4, {})} | custom-call | flops 1048576 | bytes 2097152 | tf_op jit(solution)/shard_map/pallas_call | solution.py:326
  77.7 2.5 %collective-permute-done.7.rest_2_ = bf16[2,1,2,128,128]{4,3,2,1,0:T(8,128)(2,1)S(1)} collective-permute-done((bf16[2,1,2,128,128]{4,3,2,1,0:T(8,128)(2,1)S(1)}, bf16[2,1,2,128,128]{4,3,2,1,0:T(8,128)(2,1)S(1)}, u32[]{:S(2)}, u32[]{:S(2)}) %collective-permute-start.7) | collective-permute-done | bytes 131104 | tf_op jit(solution)/shard_map/ppermute | solution.py:381
  80.2 2.0 %collective-permute-done.8.rest_3_ = bf16[2,1,2,128,128]{4,3,2,1,0:T(8,128)(2,1)S(1)} collective-permute-done((bf16[2,1,2,128,128]{4,3,2,1,0:T(8,128)(2,1)S(1)}, bf16[2,1,2,128,128]{4,3,2,1,0:T(8,128)(2,1)S(1)}, u32[]{:S(2)}, u32[]{:S(2)}) %collective-permute-start.8) | collective-permute-done | bytes 131104 | tf_op jit(solution)/shard_map/ppermute | solution.py:381
  82.3 1.0 %shard_map.80 = f32[8,3,2,128,128]{4,3,2,1,0:T(8,128)} custom-call(bf16[2,1,2,128,128]{4,3,2,1,0:T(8,128)(2,1)S(1)} %get-tuple-element.53.rest_0_, bf16[2,1,2,128,128]{4,3,2,1,0:T(8,128)(2,1)S(1)} %collective-permute-done.6.rest_1_, bf16[2,1,2,128,128]{4,3,2,1,0:T(8,128)(2,1)S(1)} %collective-permute-done.7.rest_2_, ...), custom_call_target="tpu_custom_call", output_to_operand_aliasing={{}: (4, {})} | custom-call | flops 1048576 | bytes 2097152 | tf_op jit(solution)/shard_map/pallas_call | solution.py:326
  (34 shorter events, 3.8 us)
Async XLA Ops:
  7.5 15.4 %collective-permute-start.18 = (bf16[256,256]{1,0:T(8,128)(2,1)S(1)}, bf16[256,256]{1,0:T(8,128)(2,1)S(1)}, u32[]{:S(2)}, u32[]{:S(2)}) collective-permute-start(bf16[256,256]{1,0:T(8,128)(2,1)S(1)} %get-tuple-element.69), channel_id=1, source_target_pairs={{0,24},{4,28},{8,16},{12,20},{16,8},{20,12},{24,0},{28,4},{1,25},{... | collective-permute-start | bytes 393224 | tf_op jit(solution)/shard_map/ppermute | solution.py:349
  12.6 15.8 %collective-permute-start.19 = (bf16[256,256]{1,0:T(8,128)(2,1)S(1)}, bf16[256,256]{1,0:T(8,128)(2,1)S(1)}, u32[]{:S(2)}, u32[]{:S(2)}) collective-permute-start(bf16[256,256]{1,0:T(8,128)(2,1)S(1)} %get-tuple-element.70), channel_id=1, source_target_pairs={{0,20},{4,16},{8,28},{12,24},{16,4},{20,0},{24,12},{28,8},{1,21},{... | collective-permute-start | bytes 393224 | tf_op jit(solution)/shard_map/ppermute | solution.py:349
  13.0 18.1 %collective-permute-start.20 = (bf16[256,256]{1,0:T(8,128)(2,1)S(1)}, bf16[256,256]{1,0:T(8,128)(2,1)S(1)}, u32[]{:S(2)}, u32[]{:S(2)}) collective-permute-start(bf16[256,256]{1,0:T(8,128)(2,1)S(1)} %get-tuple-element.71), channel_id=1, source_target_pairs={{0,28},{4,24},{8,20},{12,16},{16,12},{20,8},{24,4},{28,0},{1,29},{... | collective-permute-start | bytes 393224 | tf_op jit(solution)/shard_map/ppermute | solution.py:349
  15.4 17.5 %collective-permute-start.21 = (bf16[256,256]{1,0:T(8,128)(2,1)S(1)}, bf16[256,256]{1,0:T(8,128)(2,1)S(1)}, u32[]{:S(2)}, u32[]{:S(2)}) collective-permute-start(bf16[256,256]{1,0:T(8,128)(2,1)S(1)} %get-tuple-element.72), channel_id=1, source_target_pairs={{0,8},{4,12},{8,0},{12,4},{16,24},{20,28},{24,16},{28,20},{1,9},{5... | collective-permute-start | bytes 393224 | tf_op jit(solution)/shard_map/ppermute | solution.py:349
  17.0 19.8 %collective-permute-start.22 = (bf16[256,256]{1,0:T(8,128)(2,1)S(1)}, bf16[256,256]{1,0:T(8,128)(2,1)S(1)}, u32[]{:S(2)}, u32[]{:S(2)}) collective-permute-start(bf16[256,256]{1,0:T(8,128)(2,1)S(1)} %get-tuple-element.73), channel_id=1, source_target_pairs={{0,4},{4,0},{8,12},{12,8},{16,20},{20,16},{24,28},{28,24},{1,5},{5... | collective-permute-start | bytes 393224 | tf_op jit(solution)/shard_map/ppermute | solution.py:349
  22.8 13.9 %collective-permute-start.23 = (bf16[256,256]{1,0:T(8,128)(2,1)S(1)}, bf16[256,256]{1,0:T(8,128)(2,1)S(1)}, u32[]{:S(2)}, u32[]{:S(2)}) collective-permute-start(bf16[256,256]{1,0:T(8,128)(2,1)S(1)} %get-tuple-element.74), channel_id=1, source_target_pairs={{0,12},{4,8},{8,4},{12,0},{16,28},{20,24},{24,20},{28,16},{1,13},{... | collective-permute-start | bytes 393224 | tf_op jit(solution)/shard_map/ppermute | solution.py:349
  28.4 8.5 %collective-permute-start.9 = (bf16[256,256]{1,0:T(8,128)(2,1)S(1)}, bf16[256,256]{1,0:T(8,128)(2,1)S(1)}, u32[]{:S(2)}, u32[]{:S(2)}) collective-permute-start(bf16[256,256]{1,0:T(8,128)(2,1)S(1)} %get-tuple-element.58), channel_id=1, source_target_pairs={{0,24},{4,28},{8,16},{12,20},{16,8},{20,12},{24,0},{28,4},{1,25},{... | collective-permute-start | bytes 393224 | tf_op jit(solution)/shard_map/ppermute | solution.py:349
  31.1 15.6 %collective-permute-start.10 = (bf16[256,256]{1,0:T(8,128)(2,1)S(1)}, bf16[256,256]{1,0:T(8,128)(2,1)S(1)}, u32[]{:S(2)}, u32[]{:S(2)}) collective-permute-start(bf16[256,256]{1,0:T(8,128)(2,1)S(1)} %get-tuple-element.59), channel_id=1, source_target_pairs={{0,20},{4,16},{8,28},{12,24},{16,4},{20,0},{24,12},{28,8},{1,21},{... | collective-permute-start | bytes 393224 | tf_op jit(solution)/shard_map/ppermute | solution.py:349
  32.9 16.3 %collective-permute-start.11 = (bf16[256,256]{1,0:T(8,128)(2,1)S(1)}, bf16[256,256]{1,0:T(8,128)(2,1)S(1)}, u32[]{:S(2)}, u32[]{:S(2)}) collective-permute-start(bf16[256,256]{1,0:T(8,128)(2,1)S(1)} %get-tuple-element.60), channel_id=1, source_target_pairs={{0,28},{4,24},{8,20},{12,16},{16,12},{20,8},{24,4},{28,0},{1,29},{... | collective-permute-start | bytes 393224 | tf_op jit(solution)/shard_map/ppermute | solution.py:349
  36.8 13.3 %collective-permute-start.12 = (bf16[256,256]{1,0:T(8,128)(2,1)S(1)}, bf16[256,256]{1,0:T(8,128)(2,1)S(1)}, u32[]{:S(2)}, u32[]{:S(2)}) collective-permute-start(bf16[256,256]{1,0:T(8,128)(2,1)S(1)} %get-tuple-element.61), channel_id=1, source_target_pairs={{0,8},{4,12},{8,0},{12,4},{16,24},{20,28},{24,16},{28,20},{1,9},{5... | collective-permute-start | bytes 393224 | tf_op jit(solution)/shard_map/ppermute | solution.py:349
  36.8 17.1 %collective-permute-start.13 = (bf16[256,256]{1,0:T(8,128)(2,1)S(1)}, bf16[256,256]{1,0:T(8,128)(2,1)S(1)}, u32[]{:S(2)}, u32[]{:S(2)}) collective-permute-start(bf16[256,256]{1,0:T(8,128)(2,1)S(1)} %get-tuple-element.62), channel_id=1, source_target_pairs={{0,4},{4,0},{8,12},{12,8},{16,20},{20,16},{24,28},{28,24},{1,5},{5... | collective-permute-start | bytes 393224 | tf_op jit(solution)/shard_map/ppermute | solution.py:349
  36.9 17.0 %collective-permute-start.14 = (bf16[256,256]{1,0:T(8,128)(2,1)S(1)}, bf16[256,256]{1,0:T(8,128)(2,1)S(1)}, u32[]{:S(2)}, u32[]{:S(2)}) collective-permute-start(bf16[256,256]{1,0:T(8,128)(2,1)S(1)} %get-tuple-element.63), channel_id=1, source_target_pairs={{0,12},{4,8},{8,4},{12,0},{16,28},{20,24},{24,20},{28,16},{1,13},{... | collective-permute-start | bytes 393224 | tf_op jit(solution)/shard_map/ppermute | solution.py:349
  46.7 10.9 %collective-permute-start = (bf16[256,256]{1,0:T(8,128)(2,1)S(1)}, bf16[256,256]{1,0:T(8,128)(2,1)S(1)}, u32[]{:S(2)}, u32[]{:S(2)}) collective-permute-start(bf16[256,256]{1,0:T(8,128)(2,1)S(1)} %get-tuple-element.47), channel_id=1, source_target_pairs={{0,24},{4,28},{8,16},{12,20},{16,8},{20,12},{24,0},{28,4},{1,25},{... | collective-permute-start | bytes 393224 | tf_op jit(solution)/shard_map/ppermute | solution.py:349
  49.2 13.5 %collective-permute-start.1 = (bf16[256,256]{1,0:T(8,128)(2,1)S(1)}, bf16[256,256]{1,0:T(8,128)(2,1)S(1)}, u32[]{:S(2)}, u32[]{:S(2)}) collective-permute-start(bf16[256,256]{1,0:T(8,128)(2,1)S(1)} %get-tuple-element.48), channel_id=1, source_target_pairs={{0,20},{4,16},{8,28},{12,24},{16,4},{20,0},{24,12},{28,8},{1,21},{... | collective-permute-start | bytes 393224 | tf_op jit(solution)/shard_map/ppermute | solution.py:349
  50.0 12.6 %collective-permute-start.2 = (bf16[256,256]{1,0:T(8,128)(2,1)S(1)}, bf16[256,256]{1,0:T(8,128)(2,1)S(1)}, u32[]{:S(2)}, u32[]{:S(2)}) collective-permute-start(bf16[256,256]{1,0:T(8,128)(2,1)S(1)} %get-tuple-element.49), channel_id=1, source_target_pairs={{0,28},{4,24},{8,20},{12,16},{16,12},{20,8},{24,4},{28,0},{1,29},{... | collective-permute-start | bytes 393224 | tf_op jit(solution)/shard_map/ppermute | solution.py:349
  53.8 9.3 %collective-permute-start.3 = (bf16[256,256]{1,0:T(8,128)(2,1)S(1)}, bf16[256,256]{1,0:T(8,128)(2,1)S(1)}, u32[]{:S(2)}, u32[]{:S(2)}) collective-permute-start(bf16[256,256]{1,0:T(8,128)(2,1)S(1)} %get-tuple-element.50), channel_id=1, source_target_pairs={{0,8},{4,12},{8,0},{12,4},{16,24},{20,28},{24,16},{28,20},{1,9},{5... | collective-permute-start | bytes 393224 | tf_op jit(solution)/shard_map/ppermute | solution.py:349
  53.8 2.8 %copy-start = (s32[1,6,1]{1,2,0:T(1,128)S(1)}, s32[1,6,1]{1,2,0:T(1,128)}, u32[]{:S(2)}) copy-start(s32[1,6,1]{1,2,0:T(1,128)} %param.13) | copy-start | bytes 76
  53.9 11.4 %collective-permute-start.4 = (bf16[256,256]{1,0:T(8,128)(2,1)S(1)}, bf16[256,256]{1,0:T(8,128)(2,1)S(1)}, u32[]{:S(2)}, u32[]{:S(2)}) collective-permute-start(bf16[256,256]{1,0:T(8,128)(2,1)S(1)} %get-tuple-element.51), channel_id=1, source_target_pairs={{0,4},{4,0},{8,12},{12,8},{16,20},{20,16},{24,28},{28,24},{1,5},{5... | collective-permute-start | bytes 393224 | tf_op jit(solution)/shard_map/ppermute | solution.py:349
  57.6 7.7 %collective-permute-start.5 = (bf16[256,256]{1,0:T(8,128)(2,1)S(1)}, bf16[256,256]{1,0:T(8,128)(2,1)S(1)}, u32[]{:S(2)}, u32[]{:S(2)}) collective-permute-start(bf16[256,256]{1,0:T(8,128)(2,1)S(1)} %get-tuple-element.52), channel_id=1, source_target_pairs={{0,12},{4,8},{8,4},{12,0},{16,28},{20,24},{24,20},{28,16},{1,13},{... | collective-permute-start | bytes 393224 | tf_op jit(solution)/shard_map/ppermute | solution.py:349
  62.6 5.1 %collective-permute-start.15 = (bf16[2,1,2,128,128]{4,3,2,1,0:T(8,128)(2,1)S(1)}, bf16[2,1,2,128,128]{4,3,2,1,0:T(8,128)(2,1)S(1)}, u32[]{:S(2)}, u32[]{:S(2)}) collective-permute-start(bf16[2,1,2,128,128]{4,3,2,1,0:T(8,128)(2,1)S(1)} %get-tuple-element.65), channel_id=1, source_target_pairs={{0,1},{1,0},{2,3},{3,2},{4,5},{5,4},{6,7},{7,6},{8,9},{9,8},{10,11... | collective-permute-start | bytes 393224 | tf_op jit(solution)/shard_map/ppermute | solution.py:381
  62.6 6.6 %collective-permute-start.24 = (bf16[2,1,2,128,128]{4,3,2,1,0:T(8,128)(2,1)S(1)}, bf16[2,1,2,128,128]{4,3,2,1,0:T(8,128)(2,1)S(1)}, u32[]{:S(2)}, u32[]{:S(2)}) collective-permute-start(bf16[2,1,2,128,128]{4,3,2,1,0:T(8,128)(2,1)S(1)} %get-tuple-element.76), channel_id=1, source_target_pairs={{0,1},{1,0},{2,3},{3,2},{4,5},{5,4},{6,7},{7,6},{8,9},{9,8},{10,11... | collective-permute-start | bytes 393224 | tf_op jit(solution)/shard_map/ppermute | solution.py:381
  63.2 6.1 %collective-permute-start.25 = (bf16[2,1,2,128,128]{4,3,2,1,0:T(8,128)(2,1)S(1)}, bf16[2,1,2,128,128]{4,3,2,1,0:T(8,128)(2,1)S(1)}, u32[]{:S(2)}, u32[]{:S(2)}) collective-permute-start(bf16[2,1,2,128,128]{4,3,2,1,0:T(8,128)(2,1)S(1)} %get-tuple-element.77), channel_id=1, source_target_pairs={{0,2},{1,3},{2,0},{3,1},{4,6},{5,7},{6,4},{7,5},{8,10},{9,11},{10,... | collective-permute-start | bytes 393224 | tf_op jit(solution)/shard_map/ppermute | solution.py:381
  65.3 5.8 %collective-permute-start.26 = (bf16[2,1,2,128,128]{4,3,2,1,0:T(8,128)(2,1)S(1)}, bf16[2,1,2,128,128]{4,3,2,1,0:T(8,128)(2,1)S(1)}, u32[]{:S(2)}, u32[]{:S(2)}) collective-permute-start(bf16[2,1,2,128,128]{4,3,2,1,0:T(8,128)(2,1)S(1)} %get-tuple-element.78), channel_id=1, source_target_pairs={{0,3},{1,2},{2,1},{3,0},{4,7},{5,6},{6,5},{7,4},{8,11},{9,10},{10,... | collective-permute-start | bytes 393224 | tf_op jit(solution)/shard_map/ppermute | solution.py:381
  65.3 9.4 %collective-permute-start.16 = (bf16[2,1,2,128,128]{4,3,2,1,0:T(8,128)(2,1)S(1)}, bf16[2,1,2,128,128]{4,3,2,1,0:T(8,128)(2,1)S(1)}, u32[]{:S(2)}, u32[]{:S(2)}) collective-permute-start(bf16[2,1,2,128,128]{4,3,2,1,0:T(8,128)(2,1)S(1)} %get-tuple-element.66), channel_id=1, source_target_pairs={{0,2},{1,3},{2,0},{3,1},{4,6},{5,7},{6,4},{7,5},{8,10},{9,11},{10,... | collective-permute-start | bytes 393224 | tf_op jit(solution)/shard_map/ppermute | solution.py:381
  67.7 8.9 %collective-permute-start.17 = (bf16[2,1,2,128,128]{4,3,2,1,0:T(8,128)(2,1)S(1)}, bf16[2,1,2,128,128]{4,3,2,1,0:T(8,128)(2,1)S(1)}, u32[]{:S(2)}, u32[]{:S(2)}) collective-permute-start(bf16[2,1,2,128,128]{4,3,2,1,0:T(8,128)(2,1)S(1)} %get-tuple-element.67), channel_id=1, source_target_pairs={{0,3},{1,2},{2,1},{3,0},{4,7},{5,6},{6,5},{7,4},{8,11},{9,10},{10,... | collective-permute-start | bytes 393224 | tf_op jit(solution)/shard_map/ppermute | solution.py:381
  69.3 8.4 %collective-permute-start.6 = (bf16[2,1,2,128,128]{4,3,2,1,0:T(8,128)(2,1)S(1)}, bf16[2,1,2,128,128]{4,3,2,1,0:T(8,128)(2,1)S(1)}, u32[]{:S(2)}, u32[]{:S(2)}) collective-permute-start(bf16[2,1,2,128,128]{4,3,2,1,0:T(8,128)(2,1)S(1)} %get-tuple-element.54), channel_id=1, source_target_pairs={{0,1},{1,0},{2,3},{3,2},{4,5},{5,4},{6,7},{7,6},{8,9},{9,8},{10,11... | collective-permute-start | bytes 393224 | tf_op jit(solution)/shard_map/ppermute | solution.py:381
  69.3 11.0 %collective-permute-start.7 = (bf16[2,1,2,128,128]{4,3,2,1,0:T(8,128)(2,1)S(1)}, bf16[2,1,2,128,128]{4,3,2,1,0:T(8,128)(2,1)S(1)}, u32[]{:S(2)}, u32[]{:S(2)}) collective-permute-start(bf16[2,1,2,128,128]{4,3,2,1,0:T(8,128)(2,1)S(1)} %get-tuple-element.55), channel_id=1, source_target_pairs={{0,2},{1,3},{2,0},{3,1},{4,6},{5,7},{6,4},{7,5},{8,10},{9,11},{10,... | collective-permute-start | bytes 393224 | tf_op jit(solution)/shard_map/ppermute | solution.py:381
  71.1 11.2 %collective-permute-start.8 = (bf16[2,1,2,128,128]{4,3,2,1,0:T(8,128)(2,1)S(1)}, bf16[2,1,2,128,128]{4,3,2,1,0:T(8,128)(2,1)S(1)}, u32[]{:S(2)}, u32[]{:S(2)}) collective-permute-start(bf16[2,1,2,128,128]{4,3,2,1,0:T(8,128)(2,1)S(1)} %get-tuple-element.56), channel_id=1, source_target_pairs={{0,3},{1,2},{2,1},{3,0},{4,7},{5,6},{6,5},{7,4},{8,11},{9,10},{10,... | collective-permute-start | bytes 393224 | tf_op jit(solution)/shard_map/ppermute | solution.py:381

commit v3 on v2

--- a/solution.py
+++ b/solution.py
@@ -113,9 +113,10 @@
 def first_chain_kernel(plans, count, sets, width, *refs):
     counts, neighbours, rows, z_ref, inverse_ref, operator_ref = refs[:6]
     slots = rows.shape[0]
-    outs = refs[6 : 6 + slots]
-    inverse, operator, selector, z_wide = refs[6 + slots : 10 + slots]
-    z_in, first_a, first_b, second_a, second_b, sems = refs[10 + slots :]
+    early = slots // 2
+    outs = refs[6 : 6 + early]
+    inverse, operator, selector, z_wide, image = refs[6 + early : 11 + early]
+    z_in, first_a, first_b, second_a, second_b, sems = refs[11 + early :]
     block = inverse.shape[1] // 2
 
     def fetch(source, target, part, sem):
@@ -145,8 +146,32 @@
         operator_loads[0].wait()
         operator_loads[1].wait()
 
-    apply(operator, {0: ready}, width, first_a, first_b, second_a, None)
-    pick_rows(selector, second_a, outs)
+    apply(operator, {0: ready}, width, first_a, first_b, image, None)
+    pick_rows(selector, image, outs)
+
+
+def later_pick(slots, width, held, image):
+    _, _, selector, _ = held
+    margin = selector.shape[0] // slots
+    early = slots // 2
+    vmem = pl.BlockSpec(memory_space=pltpu.VMEM)
+
+    def body(selector_ref, image_ref, *outs):
+        pick_rows(selector_ref.at[early * margin :], image_ref, outs)
+
+    return pl.pallas_call(
+        body,
+        out_shape=[pltpu.VMEM((margin, 2 * width), BF16)] * (slots - early),
+        in_specs=[vmem] * 2,
+        out_specs=[vmem] * (slots - early),
+        compiler_params=pltpu.CompilerParams(vmem_limit_bytes=SMALL_VMEM),
+        cost_estimate=pl.CostEstimate(
+            flops=4 * image.shape[0] * width * slots * margin // 2,
+            bytes_accessed=4 << 20,
+            transcendentals=0,
+        ),
+        name="pick0",
+    )(*in_vmem(selector, image))
 
 
 def in_hbm(*values):
@@ -164,11 +189,13 @@
     smem = pl.BlockSpec(memory_space=pltpu.SMEM)
     vmem = pl.BlockSpec(memory_space=pltpu.VMEM)
     flops = 4 * edges * width * (6 * edges + slots * margin)
-    outs = [pltpu.VMEM((margin, 2 * width), BF16)] * slots + [
+    early = slots // 2
+    outs = [pltpu.VMEM((margin, 2 * width), BF16)] * early + [
         pltpu.VMEM(inverse.shape, BF16),
         pltpu.VMEM(operator.shape, BF16),
         pltpu.VMEM((slots * margin, edges), BF16),
         pltpu.VMEM(z.shape, F32),
+        pltpu.VMEM((edges, 2 * width), BF16),
     ]
     results = pl.pallas_call(
         functools.partial(first_chain_kernel, plans, count, sets, width),
@@ -184,7 +211,7 @@
         cost_estimate=pl.CostEstimate(flops=flops, bytes_accessed=12 << 20, transcendentals=0),
         name="chain0",
     )(*in_hbm(counts, neighbours, rows, z, inverse, operator))
-    return results[:slots], results[slots:]
+    return results[:early], results[early:-1], results[-1]
 
 
 def next_chain_kernel(index, sets, width, inverse, operator, selector, z_wide, *refs):
@@ -363,11 +390,13 @@
     arrived = []
     for index in range(sets):
         if index == 0:
-            outgoing, held = first_chain(
+            outgoing, held, image = first_chain(
                 plans, count, sets, width, counts, neighbours, rows, z, inverse[0], operator[0]
             )
         else:
             outgoing = next_chain(index, sets, width, slots, held)
+        if index == 0:
+            outgoing = list(outgoing) + list(later_pick(slots, width, held, image))
         arrived.append(exchanged(plans, count, outgoing))
     projectors = project(sets, width, slots, held)
     received = []

time: 84 us -> 83.9 us (level)
  no operation moved by 1% of the time
where the time goes in v3:
time: 83.9 us; the launch traced here: 83.3 us
  starting transfers between devices  46.1 us (55%)
  Pallas kernels  25.3 us (30%)
  waiting for transfers between devices  11.6 us (14%)
    ppermute x18, starting transfers between devices, exchanged(): pieces[back] = lax.ppermute(outgoing[place], 'dom', pairs)  38.2 us
    pallas_call x2, Pallas kernels, next_chain(): pl.pallas_call(functools.partial(next_chain_kernel, index, sets, width),...  8.82 us
    ppermute x9, waiting for transfers between devices, on_device(): sent.append(lax.ppermute(blocks[hop], 'grp', pairs))  8.03 us
    ppermute x9, starting transfers between devices, on_device(): sent.append(lax.ppermute(blocks[hop], 'grp', pairs))  7.96 us
    pallas_call x1, Pallas kernels, first_chain(): pl.pallas_call(functools.partial(first_chain_kernel, plans, count, sets,...  7.33 us
    ppermute x18, waiting for transfers between devices, exchanged(): pieces[back] = lax.ppermute(outgoing[place], 'dom', pairs)  3.52 us
    pallas_call x3, Pallas kernels, spread(): pl.pallas_call(body, out_shape=jax.ShapeDtypeStruct((places, sets, 2, wid...  3.06 us
    pallas_call x3, Pallas kernels, gram_blocks(): pl.pallas_call(functools.partial(gram_kernel, plans, count, group, width,...  2.87 us
  transfers between devices with their start and end apart: 27, of which 8 were waited for; matrix products, arithmetic and copies ran while one was open for 0% of the time, Pallas kernels for 20%

profile of v3, /device:TPU:0, one launch (start us, length us, event | category | flops | bytes accessed | tf_op | source)
XLA Modules:
  0.0 83.3 jit_solution(6151533126837298752)
XLA Ops:
  0.0 7.3 %chain0.1 = (bf16[256,256]{1,0:T(8,128)(2,1)S(1)}, bf16[256,256]{1,0:T(8,128)(2,1)S(1)}, bf16[256,256]{1,0:T(8,128)(2,1)S(1)}, bf16[2,1024,1024]{2,1,0:T(8,128)(...) custom-call(s32[1,6]{1,0:T(1,128)} %refs_0_.1, ...), custom_call_target="tpu_custom_call" | custom-call | flops 4026531840 | bytes 12582912 | tf_op jit(solution)/shard_map/chain0/pallas_call | solution.py:200
  7.3 5.1 %collective-permute-start.18 = (bf16[256,256]{1,0:T(8,128)(2,1)S(1)}, bf16[256,256]{1,0:T(8,128)(2,1)S(1)}, u32[]{:S(2)}, u32[]{:S(2)}) collective-permute-start(bf16[256,256]{1,0:T(8,128)(2,1)S(1)} %get-tuple-element.70), channel_id=1, source_target_pairs={{0,24},{4,28},{8,16},{12,20},{16,8},{20,12},{24,0},{28,4},{1,25},{... | collective-permute-start | bytes 393224 | tf_op jit(solution)/shard_map/ppermute | solution.py:376
  12.9 2.4 %collective-permute-start.20 = (bf16[256,256]{1,0:T(8,128)(2,1)S(1)}, bf16[256,256]{1,0:T(8,128)(2,1)S(1)}, u32[]{:S(2)}, u32[]{:S(2)}) collective-permute-start(bf16[256,256]{1,0:T(8,128)(2,1)S(1)} %get-tuple-element.72), channel_id=1, source_target_pairs={{0,28},{4,24},{8,20},{12,16},{16,12},{20,8},{24,4},{28,0},{1,29},{... | collective-permute-start | bytes 393224 | tf_op jit(solution)/shard_map/ppermute | solution.py:376
  15.9 1.6 %collective-permute-start.21 = (bf16[256,256]{1,0:T(8,128)(2,1)S(1)}, bf16[256,256]{1,0:T(8,128)(2,1)S(1)}, u32[]{:S(2)}, u32[]{:S(2)}) collective-permute-start(bf16[256,256]{1,0:T(8,128)(2,1)S(1)} %get-tuple-element.74), channel_id=1, source_target_pairs={{0,8},{4,12},{8,0},{12,4},{16,24},{20,28},{24,16},{28,20},{1,9},{5... | collective-permute-start | bytes 393224 | tf_op jit(solution)/shard_map/ppermute | solution.py:376
  17.5 1.5 %collective-permute-start.22 = (bf16[256,256]{1,0:T(8,128)(2,1)S(1)}, bf16[256,256]{1,0:T(8,128)(2,1)S(1)}, u32[]{:S(2)}, u32[]{:S(2)}) collective-permute-start(bf16[256,256]{1,0:T(8,128)(2,1)S(1)} %get-tuple-element.75), channel_id=1, source_target_pairs={{0,4},{4,0},{8,12},{12,8},{16,20},{20,16},{24,28},{28,24},{1,5},{5... | collective-permute-start | bytes 393224 | tf_op jit(solution)/shard_map/ppermute | solution.py:376
  19.0 4.3 %shard_map.75 = (bf16[256,256]{1,0:T(8,128)(2,1)S(1)}, bf16[256,256]{1,0:T(8,128)(2,1)S(1)}, bf16[256,256]{1,0:T(8,128)(2,1)S(1)}, bf16[256,256]{1,0:T(8,128)(2,...) custom-call(bf16[2,1024,1024]{2,1,0:T(8,128)(2,1)S(1)} %get-tuple-element.46.inverse, ...), custom_call_target="tpu_custom_call" | custom-call | flops 4026531840 | bytes 12582912 | tf_op jit(solution)/shard_map/pallas_call | solution.py:232
  23.4 2.7 %collective-permute-start.23 = (bf16[256,256]{1,0:T(8,128)(2,1)S(1)}, bf16[256,256]{1,0:T(8,128)(2,1)S(1)}, u32[]{:S(2)}, u32[]{:S(2)}) collective-permute-start(bf16[256,256]{1,0:T(8,128)(2,1)S(1)} %get-tuple-element.76), channel_id=1, source_target_pairs={{0,12},{4,8},{8,4},{12,0},{16,28},{20,24},{24,20},{28,16},{1,13},{... | collective-permute-start | bytes 393224 | tf_op jit(solution)/shard_map/ppermute | solution.py:376
  26.0 2.2 %collective-permute-done.19.rest_2_ = bf16[256,256]{1,0:T(8,128)(2,1)S(1)} collective-permute-done((bf16[256,256]{1,0:T(8,128)(2,1)S(1)}, bf16[256,256]{1,0:T(8,128)(2,1)S(1)}, u32[]{:S(2)}, u32[]{:S(2)}) %collective-permute-start.19) | collective-permute-done | bytes 131104 | tf_op jit(solution)/shard_map/ppermute | solution.py:376
  28.3 2.7 %collective-permute-start.9 = (bf16[256,256]{1,0:T(8,128)(2,1)S(1)}, bf16[256,256]{1,0:T(8,128)(2,1)S(1)}, u32[]{:S(2)}, u32[]{:S(2)}) collective-permute-start(bf16[256,256]{1,0:T(8,128)(2,1)S(1)} %get-tuple-element.59), channel_id=1, source_target_pairs={{0,24},{4,28},{8,16},{12,20},{16,8},{20,12},{24,0},{28,4},{1,25},{... | collective-permute-start | bytes 393224 | tf_op jit(solution)/shard_map/ppermute | solution.py:376
  30.9 1.8 %collective-permute-start.10 = (bf16[256,256]{1,0:T(8,128)(2,1)S(1)}, bf16[256,256]{1,0:T(8,128)(2,1)S(1)}, u32[]{:S(2)}, u32[]{:S(2)}) collective-permute-start(bf16[256,256]{1,0:T(8,128)(2,1)S(1)} %get-tuple-element.60), channel_id=1, source_target_pairs={{0,20},{4,16},{8,28},{12,24},{16,4},{20,0},{24,12},{28,8},{1,21},{... | collective-permute-start | bytes 393224 | tf_op jit(solution)/shard_map/ppermute | solution.py:376
  32.8 3.8 %collective-permute-start.11 = (bf16[256,256]{1,0:T(8,128)(2,1)S(1)}, bf16[256,256]{1,0:T(8,128)(2,1)S(1)}, u32[]{:S(2)}, u32[]{:S(2)}) collective-permute-start(bf16[256,256]{1,0:T(8,128)(2,1)S(1)} %get-tuple-element.61), channel_id=1, source_target_pairs={{0,28},{4,24},{8,20},{12,16},{16,12},{20,8},{24,4},{28,0},{1,29},{... | collective-permute-start | bytes 393224 | tf_op jit(solution)/shard_map/ppermute | solution.py:376
  36.7 5.3 %collective-permute-start.14 = (bf16[256,256]{1,0:T(8,128)(2,1)S(1)}, bf16[256,256]{1,0:T(8,128)(2,1)S(1)}, u32[]{:S(2)}, u32[]{:S(2)}) collective-permute-start(bf16[256,256]{1,0:T(8,128)(2,1)S(1)} %get-tuple-element.64), channel_id=1, source_target_pairs={{0,12},{4,8},{8,4},{12,0},{16,28},{20,24},{24,20},{28,16},{1,13},{... | collective-permute-start | bytes 393224 | tf_op jit(solution)/shard_map/ppermute | solution.py:376
  42.0 4.5 %shard_map.73 = (bf16[256,256]{1,0:T(8,128)(2,1)S(1)}, bf16[256,256]{1,0:T(8,128)(2,1)S(1)}, bf16[256,256]{1,0:T(8,128)(2,1)S(1)}, bf16[256,256]{1,0:T(8,128)(2,...) custom-call(bf16[2,1024,1024]{2,1,0:T(8,128)(2,1)S(1)} %get-tuple-element.46.inverse, ...), custom_call_target="tpu_custom_call" | custom-call | flops 4026531840 | bytes 12582912 | tf_op jit(solution)/shard_map/pallas_call | solution.py:232
  46.6 2.5 %collective-permute-start = (bf16[256,256]{1,0:T(8,128)(2,1)S(1)}, bf16[256,256]{1,0:T(8,128)(2,1)S(1)}, u32[]{:S(2)}, u32[]{:S(2)}) collective-permute-start(bf16[256,256]{1,0:T(8,128)(2,1)S(1)} %get-tuple-element.48), channel_id=1, source_target_pairs={{0,24},{4,28},{8,16},{12,20},{16,8},{20,12},{24,0},{28,4},{1,25},{... | collective-permute-start | bytes 393224 | tf_op jit(solution)/shard_map/ppermute | solution.py:376
  49.9 3.8 %collective-permute-start.2 = (bf16[256,256]{1,0:T(8,128)(2,1)S(1)}, bf16[256,256]{1,0:T(8,128)(2,1)S(1)}, u32[]{:S(2)}, u32[]{:S(2)}) collective-permute-start(bf16[256,256]{1,0:T(8,128)(2,1)S(1)} %get-tuple-element.50), channel_id=1, source_target_pairs={{0,28},{4,24},{8,20},{12,16},{16,12},{20,8},{24,4},{28,0},{1,29},{... | collective-permute-start | bytes 393224 | tf_op jit(solution)/shard_map/ppermute | solution.py:376
  53.8 2.7 %project.1 = (bf16[6,256,256]{2,1,0:T(8,128)(2,1)S(1)}, bf16[6,256,256]{2,1,0:T(8,128)(2,1)S(1)}, bf16[6,256,256]{2,1,0:T(8,128)(2,1)S(1)}) custom-call(bf16[1536,1024]{1,0:T(8,128)(2,1)S(1)} %get-tuple-element.43.selector.selector_ref, f32[6144,128]{1,0:T(8,128)S(1)} %get-tuple-element.44.z_wide), custom_call_target="tpu_custom_call" | custom-call | flops 2415919104 | bytes 6291456 | tf_op jit(solution)/shard_map/project/pallas_call | solution.py:265
  56.5 1.0 %shard_map.77 = (bf16[2,1,2,128,128]{4,3,2,1,0:T(8,128)(2,1)S(1)}, bf16[2,1,2,128,128]{4,3,2,1,0:T(8,128)(2,1)S(1)}, bf16[2,1,2,128,128]{4,3,2,1,0:T(8,128)(2,1)S(1)}, bf16[2,1,2,128,128]{4,3,2,1,0:T(8,128)(2,1)S(1)}) custom-call(s32[1,6]{1,0:T(1,128)S(1)} %bitcast.5, bf16[6,256,256]{2,1,0:T(8,128)(2,1)S(1)} %get-tuple-element.69.rest_0_, ...), custom_call_target="tpu_custom_call" | custom-call | flops 201326592 | bytes 2097152 | tf_op jit(solution)/shard_map/pallas_call | solution.py:312
  57.4 3.5 %collective-permute-start.5 = (bf16[256,256]{1,0:T(8,128)(2,1)S(1)}, bf16[256,256]{1,0:T(8,128)(2,1)S(1)}, u32[]{:S(2)}, u32[]{:S(2)}) collective-permute-start(bf16[256,256]{1,0:T(8,128)(2,1)S(1)} %get-tuple-element.53), channel_id=1, source_target_pairs={{0,12},{4,8},{8,4},{12,0},{16,28},{20,24},{24,20},{28,16},{1,13},{... | collective-permute-start | bytes 393224 | tf_op jit(solution)/shard_map/ppermute | solution.py:376
  60.9 1.0 %shard_map.76 = (bf16[2,1,2,128,128]{4,3,2,1,0:T(8,128)(2,1)S(1)}, bf16[2,1,2,128,128]{4,3,2,1,0:T(8,128)(2,1)S(1)}, bf16[2,1,2,128,128]{4,3,2,1,0:T(8,128)(2,1)S(1)}, bf16[2,1,2,128,128]{4,3,2,1,0:T(8,128)(2,1)S(1)}) custom-call(s32[1,6]{1,0:T(1,128)S(1)} %bitcast.6, bf16[6,256,256]{2,1,0:T(8,128)(2,1)S(1)} %get-tuple-element.58.rest_0_, ...), custom_call_target="tpu_custom_call" | custom-call | flops 201326592 | bytes 2097152 | tf_op jit(solution)/shard_map/pallas_call | solution.py:312
  63.0 1.5 %collective-permute-start.25 = (bf16[2,1,2,128,128]{4,3,2,1,0:T(8,128)(2,1)S(1)}, bf16[2,1,2,128,128]{4,3,2,1,0:T(8,128)(2,1)S(1)}, u32[]{:S(2)}, u32[]{:S(2)}) collective-permute-start(bf16[2,1,2,128,128]{4,3,2,1,0:T(8,128)(2,1)S(1)} %get-tuple-element.79), channel_id=1, source_target_pairs={{0,2},{1,3},{2,0},{3,1},{4,6},{5,7},{6,4},{7,5},{8,10},{9,11},{10,... | collective-permute-start | bytes 393224 | tf_op jit(solution)/shard_map/ppermute | solution.py:410
  65.1 1.5 %collective-permute-start.16 = (bf16[2,1,2,128,128]{4,3,2,1,0:T(8,128)(2,1)S(1)}, bf16[2,1,2,128,128]{4,3,2,1,0:T(8,128)(2,1)S(1)}, u32[]{:S(2)}, u32[]{:S(2)}) collective-permute-start(bf16[2,1,2,128,128]{4,3,2,1,0:T(8,128)(2,1)S(1)} %get-tuple-element.67), channel_id=1, source_target_pairs={{0,2},{1,3},{2,0},{3,1},{4,6},{5,7},{6,4},{7,5},{8,10},{9,11},{10,... | collective-permute-start | bytes 393224 | tf_op jit(solution)/shard_map/ppermute | solution.py:410
  66.6 1.0 %shard_map.74 = (bf16[2,1,2,128,128]{4,3,2,1,0:T(8,128)(2,1)S(1)}, bf16[2,1,2,128,128]{4,3,2,1,0:T(8,128)(2,1)S(1)}, bf16[2,1,2,128,128]{4,3,2,1,0:T(8,128)(2,1)S(1)}, bf16[2,1,2,128,128]{4,3,2,1,0:T(8,128)(2,1)S(1)}) custom-call(s32[1,6]{1,0:T(1,128)S(1)} %bitcast.7, bf16[6,256,256]{2,1,0:T(8,128)(2,1)S(1)} %get-tuple-element.45.rest_0_, ...), custom_call_target="tpu_custom_call" | custom-call | flops 201326592 | bytes 2097152 | tf_op jit(solution)/shard_map/pallas_call | solution.py:312
  67.6 1.5 %collective-permute-start.17 = (bf16[2,1,2,128,128]{4,3,2,1,0:T(8,128)(2,1)S(1)}, bf16[2,1,2,128,128]{4,3,2,1,0:T(8,128)(2,1)S(1)}, u32[]{:S(2)}, u32[]{:S(2)}) collective-permute-start(bf16[2,1,2,128,128]{4,3,2,1,0:T(8,128)(2,1)S(1)} %get-tuple-element.68), channel_id=1, source_target_pairs={{0,3},{1,2},{2,1},{3,0},{4,7},{5,6},{6,5},{7,4},{8,11},{9,10},{10,... | collective-permute-start | bytes 393224 | tf_op jit(solution)/shard_map/ppermute | solution.py:410
  69.2 1.2 %collective-permute-start.7 = (bf16[2,1,2,128,128]{4,3,2,1,0:T(8,128)(2,1)S(1)}, bf16[2,1,2,128,128]{4,3,2,1,0:T(8,128)(2,1)S(1)}, u32[]{:S(2)}, u32[]{:S(2)}) collective-permute-start(bf16[2,1,2,128,128]{4,3,2,1,0:T(8,128)(2,1)S(1)} %get-tuple-element.56), channel_id=1, source_target_pairs={{0,2},{1,3},{2,0},{3,1},{4,6},{5,7},{6,4},{7,5},{8,10},{9,11},{10,... | collective-permute-start | bytes 393224 | tf_op jit(solution)/shard_map/ppermute | solution.py:410
  70.9 1.7 %collective-permute-start.8 = (bf16[2,1,2,128,128]{4,3,2,1,0:T(8,128)(2,1)S(1)}, bf16[2,1,2,128,128]{4,3,2,1,0:T(8,128)(2,1)S(1)}, u32[]{:S(2)}, u32[]{:S(2)}) collective-permute-start(bf16[2,1,2,128,128]{4,3,2,1,0:T(8,128)(2,1)S(1)} %get-tuple-element.57), channel_id=1, source_target_pairs={{0,3},{1,2},{2,1},{3,0},{4,7},{5,6},{6,5},{7,4},{8,11},{9,10},{10,... | collective-permute-start | bytes 393224 | tf_op jit(solution)/shard_map/ppermute | solution.py:410
  72.6 1.0 %shard_map.78.rest_4_ = f32[8,3,2,128,128]{4,3,2,1,0:T(8,128)} custom-call(bf16[2,1,2,128,128]{4,3,2,1,0:T(8,128)(2,1)S(1)} %get-tuple-element.77.rest_0_, bf16[2,1,2,128,128]{4,3,2,1,0:T(8,128)(2,1)S(1)} %collective-permute-done.24.rest_1_, bf16[2,1,2,128,128]{4,3,2,1,0:T(8,128)(2,1)S(1)} %collective-permute-done.25.rest_2_, ...), custom_call_target="tpu_custom_call" | custom-call | flops 1048576 | bytes 2097152 | tf_op jit(solution)/shard_map/pallas_call | solution.py:353
  73.6 0.9 %collective-permute-done.16.rest_2_ = bf16[2,1,2,128,128]{4,3,2,1,0:T(8,128)(2,1)S(1)} collective-permute-done((bf16[2,1,2,128,128]{4,3,2,1,0:T(8,128)(2,1)S(1)}, bf16[2,1,2,128,128]{4,3,2,1,0:T(8,128)(2,1)S(1)}, u32[]{:S(2)}, u32[]{:S(2)}) %collective-permute-start.16) | collective-permute-done | bytes 131104 | tf_op jit(solution)/shard_map/ppermute | solution.py:410
  74.5 2.0 %collective-permute-done.17.rest_3_ = bf16[2,1,2,128,128]{4,3,2,1,0:T(8,128)(2,1)S(1)} collective-permute-done((bf16[2,1,2,128,128]{4,3,2,1,0:T(8,128)(2,1)S(1)}, bf16[2,1,2,128,128]{4,3,2,1,0:T(8,128)(2,1)S(1)}, u32[]{:S(2)}, u32[]{:S(2)}) %collective-permute-start.17) | collective-permute-done | bytes 131104 | tf_op jit(solution)/shard_map/ppermute | solution.py:410
  76.5 1.0 %shard_map.79.rest_4_ = f32[8,3,2,128,128]{4,3,2,1,0:T(8,128)} custom-call(bf16[2,1,2,128,128]{4,3,2,1,0:T(8,128)(2,1)S(1)} %get-tuple-element.65.rest_0_, bf16[2,1,2,128,128]{4,3,2,1,0:T(8,128)(2,1)S(1)} %collective-permute-done.15.rest_1_, bf16[2,1,2,128,128]{4,3,2,1,0:T(8,128)(2,1)S(1)} %collective-permute-done.16.rest_2_, ...), custom_call_target="tpu_custom_call", output_to_operand_aliasing={{}: (4, {})} | custom-call | flops 1048576 | bytes 2097152 | tf_op jit(solution)/shard_map/pallas_call | solution.py:353
  77.6 2.5 %collective-permute-done.7.rest_2_ = bf16[2,1,2,128,128]{4,3,2,1,0:T(8,128)(2,1)S(1)} collective-permute-done((bf16[2,1,2,128,128]{4,3,2,1,0:T(8,128)(2,1)S(1)}, bf16[2,1,2,128,128]{4,3,2,1,0:T(8,128)(2,1)S(1)}, u32[]{:S(2)}, u32[]{:S(2)}) %collective-permute-start.7) | collective-permute-done | bytes 131104 | tf_op jit(solution)/shard_map/ppermute | solution.py:410
  80.1 2.0 %collective-permute-done.8.rest_3_ = bf16[2,1,2,128,128]{4,3,2,1,0:T(8,128)(2,1)S(1)} collective-permute-done((bf16[2,1,2,128,128]{4,3,2,1,0:T(8,128)(2,1)S(1)}, bf16[2,1,2,128,128]{4,3,2,1,0:T(8,128)(2,1)S(1)}, u32[]{:S(2)}, u32[]{:S(2)}) %collective-permute-start.8) | collective-permute-done | bytes 131104 | tf_op jit(solution)/shard_map/ppermute | solution.py:410
  82.2 1.0 %shard_map.80 = f32[8,3,2,128,128]{4,3,2,1,0:T(8,128)} custom-call(bf16[2,1,2,128,128]{4,3,2,1,0:T(8,128)(2,1)S(1)} %get-tuple-element.54.rest_0_, bf16[2,1,2,128,128]{4,3,2,1,0:T(8,128)(2,1)S(1)} %collective-permute-done.6.rest_1_, bf16[2,1,2,128,128]{4,3,2,1,0:T(8,128)(2,1)S(1)} %collective-permute-done.7.rest_2_, ...), custom_call_target="tpu_custom_call", output_to_operand_aliasing={{}: (4, {})} | custom-call | flops 1048576 | bytes 2097152 | tf_op jit(solution)/shard_map/pallas_call | solution.py:353
  (35 shorter events, 4.3 us)
Async XLA Ops:
  7.3 16.0 %collective-permute-start.18 = (bf16[256,256]{1,0:T(8,128)(2,1)S(1)}, bf16[256,256]{1,0:T(8,128)(2,1)S(1)}, u32[]{:S(2)}, u32[]{:S(2)}) collective-permute-start(bf16[256,256]{1,0:T(8,128)(2,1)S(1)} %get-tuple-element.70), channel_id=1, source_target_pairs={{0,24},{4,28},{8,16},{12,20},{16,8},{20,12},{24,0},{28,4},{1,25},{... | collective-permute-start | bytes 393224 | tf_op jit(solution)/shard_map/ppermute | solution.py:376
  12.5 15.8 %collective-permute-start.19 = (bf16[256,256]{1,0:T(8,128)(2,1)S(1)}, bf16[256,256]{1,0:T(8,128)(2,1)S(1)}, u32[]{:S(2)}, u32[]{:S(2)}) collective-permute-start(bf16[256,256]{1,0:T(8,128)(2,1)S(1)} %get-tuple-element.71), channel_id=1, source_target_pairs={{0,20},{4,16},{8,28},{12,24},{16,4},{20,0},{24,12},{28,8},{1,21},{... | collective-permute-start | bytes 393224 | tf_op jit(solution)/shard_map/ppermute | solution.py:376
  12.9 18.1 %collective-permute-start.20 = (bf16[256,256]{1,0:T(8,128)(2,1)S(1)}, bf16[256,256]{1,0:T(8,128)(2,1)S(1)}, u32[]{:S(2)}, u32[]{:S(2)}) collective-permute-start(bf16[256,256]{1,0:T(8,128)(2,1)S(1)} %get-tuple-element.72), channel_id=1, source_target_pairs={{0,28},{4,24},{8,20},{12,16},{16,12},{20,8},{24,4},{28,0},{1,29},{... | collective-permute-start | bytes 393224 | tf_op jit(solution)/shard_map/ppermute | solution.py:376
  15.9 16.9 %collective-permute-start.21 = (bf16[256,256]{1,0:T(8,128)(2,1)S(1)}, bf16[256,256]{1,0:T(8,128)(2,1)S(1)}, u32[]{:S(2)}, u32[]{:S(2)}) collective-permute-start(bf16[256,256]{1,0:T(8,128)(2,1)S(1)} %get-tuple-element.74), channel_id=1, source_target_pairs={{0,8},{4,12},{8,0},{12,4},{16,24},{20,28},{24,16},{28,20},{1,9},{5... | collective-permute-start | bytes 393224 | tf_op jit(solution)/shard_map/ppermute | solution.py:376
  17.5 19.1 %collective-permute-start.22 = (bf16[256,256]{1,0:T(8,128)(2,1)S(1)}, bf16[256,256]{1,0:T(8,128)(2,1)S(1)}, u32[]{:S(2)}, u32[]{:S(2)}) collective-permute-start(bf16[256,256]{1,0:T(8,128)(2,1)S(1)} %get-tuple-element.75), channel_id=1, source_target_pairs={{0,4},{4,0},{8,12},{12,8},{16,20},{20,16},{24,28},{28,24},{1,5},{5... | collective-permute-start | bytes 393224 | tf_op jit(solution)/shard_map/ppermute | solution.py:376
  23.4 13.3 %collective-permute-start.23 = (bf16[256,256]{1,0:T(8,128)(2,1)S(1)}, bf16[256,256]{1,0:T(8,128)(2,1)S(1)}, u32[]{:S(2)}, u32[]{:S(2)}) collective-permute-start(bf16[256,256]{1,0:T(8,128)(2,1)S(1)} %get-tuple-element.76), channel_id=1, source_target_pairs={{0,12},{4,8},{8,4},{12,0},{16,28},{20,24},{24,20},{28,16},{1,13},{... | collective-permute-start | bytes 393224 | tf_op jit(solution)/shard_map/ppermute | solution.py:376
  28.3 8.5 %collective-permute-start.9 = (bf16[256,256]{1,0:T(8,128)(2,1)S(1)}, bf16[256,256]{1,0:T(8,128)(2,1)S(1)}, u32[]{:S(2)}, u32[]{:S(2)}) collective-permute-start(bf16[256,256]{1,0:T(8,128)(2,1)S(1)} %get-tuple-element.59), channel_id=1, source_target_pairs={{0,24},{4,28},{8,16},{12,20},{16,8},{20,12},{24,0},{28,4},{1,25},{... | collective-permute-start | bytes 393224 | tf_op jit(solution)/shard_map/ppermute | solution.py:376
  30.9 15.6 %collective-permute-start.10 = (bf16[256,256]{1,0:T(8,128)(2,1)S(1)}, bf16[256,256]{1,0:T(8,128)(2,1)S(1)}, u32[]{:S(2)}, u32[]{:S(2)}) collective-permute-start(bf16[256,256]{1,0:T(8,128)(2,1)S(1)} %get-tuple-element.60), channel_id=1, source_target_pairs={{0,20},{4,16},{8,28},{12,24},{16,4},{20,0},{24,12},{28,8},{1,21},{... | collective-permute-start | bytes 393224 | tf_op jit(solution)/shard_map/ppermute | solution.py:376
  32.8 16.3 %collective-permute-start.11 = (bf16[256,256]{1,0:T(8,128)(2,1)S(1)}, bf16[256,256]{1,0:T(8,128)(2,1)S(1)}, u32[]{:S(2)}, u32[]{:S(2)}) collective-permute-start(bf16[256,256]{1,0:T(8,128)(2,1)S(1)} %get-tuple-element.61), channel_id=1, source_target_pairs={{0,28},{4,24},{8,20},{12,16},{16,12},{20,8},{24,4},{28,0},{1,29},{... | collective-permute-start | bytes 393224 | tf_op jit(solution)/shard_map/ppermute | solution.py:376
  36.6 13.3 %collective-permute-start.12 = (bf16[256,256]{1,0:T(8,128)(2,1)S(1)}, bf16[256,256]{1,0:T(8,128)(2,1)S(1)}, u32[]{:S(2)}, u32[]{:S(2)}) collective-permute-start(bf16[256,256]{1,0:T(8,128)(2,1)S(1)} %get-tuple-element.62), channel_id=1, source_target_pairs={{0,8},{4,12},{8,0},{12,4},{16,24},{20,28},{24,16},{28,20},{1,9},{5... | collective-permute-start | bytes 393224 | tf_op jit(solution)/shard_map/ppermute | solution.py:376
  36.6 17.1 %collective-permute-start.13 = (bf16[256,256]{1,0:T(8,128)(2,1)S(1)}, bf16[256,256]{1,0:T(8,128)(2,1)S(1)}, u32[]{:S(2)}, u32[]{:S(2)}) collective-permute-start(bf16[256,256]{1,0:T(8,128)(2,1)S(1)} %get-tuple-element.63), channel_id=1, source_target_pairs={{0,4},{4,0},{8,12},{12,8},{16,20},{20,16},{24,28},{28,24},{1,5},{5... | collective-permute-start | bytes 393224 | tf_op jit(solution)/shard_map/ppermute | solution.py:376
  36.7 17.0 %collective-permute-start.14 = (bf16[256,256]{1,0:T(8,128)(2,1)S(1)}, bf16[256,256]{1,0:T(8,128)(2,1)S(1)}, u32[]{:S(2)}, u32[]{:S(2)}) collective-permute-start(bf16[256,256]{1,0:T(8,128)(2,1)S(1)} %get-tuple-element.64), channel_id=1, source_target_pairs={{0,12},{4,8},{8,4},{12,0},{16,28},{20,24},{24,20},{28,16},{1,13},{... | collective-permute-start | bytes 393224 | tf_op jit(solution)/shard_map/ppermute | solution.py:376
  46.6 10.9 %collective-permute-start = (bf16[256,256]{1,0:T(8,128)(2,1)S(1)}, bf16[256,256]{1,0:T(8,128)(2,1)S(1)}, u32[]{:S(2)}, u32[]{:S(2)}) collective-permute-start(bf16[256,256]{1,0:T(8,128)(2,1)S(1)} %get-tuple-element.48), channel_id=1, source_target_pairs={{0,24},{4,28},{8,16},{12,20},{16,8},{20,12},{24,0},{28,4},{1,25},{... | collective-permute-start | bytes 393224 | tf_op jit(solution)/shard_map/ppermute | solution.py:376
  49.1 13.4 %collective-permute-start.1 = (bf16[256,256]{1,0:T(8,128)(2,1)S(1)}, bf16[256,256]{1,0:T(8,128)(2,1)S(1)}, u32[]{:S(2)}, u32[]{:S(2)}) collective-permute-start(bf16[256,256]{1,0:T(8,128)(2,1)S(1)} %get-tuple-element.49), channel_id=1, source_target_pairs={{0,20},{4,16},{8,28},{12,24},{16,4},{20,0},{24,12},{28,8},{1,21},{... | collective-permute-start | bytes 393224 | tf_op jit(solution)/shard_map/ppermute | solution.py:376
  49.9 12.6 %collective-permute-start.2 = (bf16[256,256]{1,0:T(8,128)(2,1)S(1)}, bf16[256,256]{1,0:T(8,128)(2,1)S(1)}, u32[]{:S(2)}, u32[]{:S(2)}) collective-permute-start(bf16[256,256]{1,0:T(8,128)(2,1)S(1)} %get-tuple-element.50), channel_id=1, source_target_pairs={{0,28},{4,24},{8,20},{12,16},{16,12},{20,8},{24,4},{28,0},{1,29},{... | collective-permute-start | bytes 393224 | tf_op jit(solution)/shard_map/ppermute | solution.py:376
  53.7 9.3 %collective-permute-start.3 = (bf16[256,256]{1,0:T(8,128)(2,1)S(1)}, bf16[256,256]{1,0:T(8,128)(2,1)S(1)}, u32[]{:S(2)}, u32[]{:S(2)}) collective-permute-start(bf16[256,256]{1,0:T(8,128)(2,1)S(1)} %get-tuple-element.51), channel_id=1, source_target_pairs={{0,8},{4,12},{8,0},{12,4},{16,24},{20,28},{24,16},{28,20},{1,9},{5... | collective-permute-start | bytes 393224 | tf_op jit(solution)/shard_map/ppermute | solution.py:376
  53.7 2.8 %copy-start = (s32[1,6,1]{1,2,0:T(1,128)S(1)}, s32[1,6,1]{1,2,0:T(1,128)}, u32[]{:S(2)}) copy-start(s32[1,6,1]{1,2,0:T(1,128)} %param.13) | copy-start | bytes 76
  53.7 11.4 %collective-permute-start.4 = (bf16[256,256]{1,0:T(8,128)(2,1)S(1)}, bf16[256,256]{1,0:T(8,128)(2,1)S(1)}, u32[]{:S(2)}, u32[]{:S(2)}) collective-permute-start(bf16[256,256]{1,0:T(8,128)(2,1)S(1)} %get-tuple-element.52), channel_id=1, source_target_pairs={{0,4},{4,0},{8,12},{12,8},{16,20},{20,16},{24,28},{28,24},{1,5},{5... | collective-permute-start | bytes 393224 | tf_op jit(solution)/shard_map/ppermute | solution.py:376
  57.4 7.7 %collective-permute-start.5 = (bf16[256,256]{1,0:T(8,128)(2,1)S(1)}, bf16[256,256]{1,0:T(8,128)(2,1)S(1)}, u32[]{:S(2)}, u32[]{:S(2)}) collective-permute-start(bf16[256,256]{1,0:T(8,128)(2,1)S(1)} %get-tuple-element.53), channel_id=1, source_target_pairs={{0,12},{4,8},{8,4},{12,0},{16,28},{20,24},{24,20},{28,16},{1,13},{... | collective-permute-start | bytes 393224 | tf_op jit(solution)/shard_map/ppermute | solution.py:376
  62.5 5.1 %collective-permute-start.15 = (bf16[2,1,2,128,128]{4,3,2,1,0:T(8,128)(2,1)S(1)}, bf16[2,1,2,128,128]{4,3,2,1,0:T(8,128)(2,1)S(1)}, u32[]{:S(2)}, u32[]{:S(2)}) collective-permute-start(bf16[2,1,2,128,128]{4,3,2,1,0:T(8,128)(2,1)S(1)} %get-tuple-element.66), channel_id=1, source_target_pairs={{0,1},{1,0},{2,3},{3,2},{4,5},{5,4},{6,7},{7,6},{8,9},{9,8},{10,11... | collective-permute-start | bytes 393224 | tf_op jit(solution)/shard_map/ppermute | solution.py:410
  62.5 6.6 %collective-permute-start.24 = (bf16[2,1,2,128,128]{4,3,2,1,0:T(8,128)(2,1)S(1)}, bf16[2,1,2,128,128]{4,3,2,1,0:T(8,128)(2,1)S(1)}, u32[]{:S(2)}, u32[]{:S(2)}) collective-permute-start(bf16[2,1,2,128,128]{4,3,2,1,0:T(8,128)(2,1)S(1)} %get-tuple-element.78), channel_id=1, source_target_pairs={{0,1},{1,0},{2,3},{3,2},{4,5},{5,4},{6,7},{7,6},{8,9},{9,8},{10,11... | collective-permute-start | bytes 393224 | tf_op jit(solution)/shard_map/ppermute | solution.py:410
  63.0 6.1 %collective-permute-start.25 = (bf16[2,1,2,128,128]{4,3,2,1,0:T(8,128)(2,1)S(1)}, bf16[2,1,2,128,128]{4,3,2,1,0:T(8,128)(2,1)S(1)}, u32[]{:S(2)}, u32[]{:S(2)}) collective-permute-start(bf16[2,1,2,128,128]{4,3,2,1,0:T(8,128)(2,1)S(1)} %get-tuple-element.79), channel_id=1, source_target_pairs={{0,2},{1,3},{2,0},{3,1},{4,6},{5,7},{6,4},{7,5},{8,10},{9,11},{10,... | collective-permute-start | bytes 393224 | tf_op jit(solution)/shard_map/ppermute | solution.py:410
  65.1 5.8 %collective-permute-start.26 = (bf16[2,1,2,128,128]{4,3,2,1,0:T(8,128)(2,1)S(1)}, bf16[2,1,2,128,128]{4,3,2,1,0:T(8,128)(2,1)S(1)}, u32[]{:S(2)}, u32[]{:S(2)}) collective-permute-start(bf16[2,1,2,128,128]{4,3,2,1,0:T(8,128)(2,1)S(1)} %get-tuple-element.80), channel_id=1, source_target_pairs={{0,3},{1,2},{2,1},{3,0},{4,7},{5,6},{6,5},{7,4},{8,11},{9,10},{10,... | collective-permute-start | bytes 393224 | tf_op jit(solution)/shard_map/ppermute | solution.py:410
  65.1 9.4 %collective-permute-start.16 = (bf16[2,1,2,128,128]{4,3,2,1,0:T(8,128)(2,1)S(1)}, bf16[2,1,2,128,128]{4,3,2,1,0:T(8,128)(2,1)S(1)}, u32[]{:S(2)}, u32[]{:S(2)}) collective-permute-start(bf16[2,1,2,128,128]{4,3,2,1,0:T(8,128)(2,1)S(1)} %get-tuple-element.67), channel_id=1, source_target_pairs={{0,2},{1,3},{2,0},{3,1},{4,6},{5,7},{6,4},{7,5},{8,10},{9,11},{10,... | collective-permute-start | bytes 393224 | tf_op jit(solution)/shard_map/ppermute | solution.py:410
  67.6 8.9 %collective-permute-start.17 = (bf16[2,1,2,128,128]{4,3,2,1,0:T(8,128)(2,1)S(1)}, bf16[2,1,2,128,128]{4,3,2,1,0:T(8,128)(2,1)S(1)}, u32[]{:S(2)}, u32[]{:S(2)}) collective-permute-start(bf16[2,1,2,128,128]{4,3,2,1,0:T(8,128)(2,1)S(1)} %get-tuple-element.68), channel_id=1, source_target_pairs={{0,3},{1,2},{2,1},{3,0},{4,7},{5,6},{6,5},{7,4},{8,11},{9,10},{10,... | collective-permute-start | bytes 393224 | tf_op jit(solution)/shard_map/ppermute | solution.py:410
  69.1 8.4 %collective-permute-start.6 = (bf16[2,1,2,128,128]{4,3,2,1,0:T(8,128)(2,1)S(1)}, bf16[2,1,2,128,128]{4,3,2,1,0:T(8,128)(2,1)S(1)}, u32[]{:S(2)}, u32[]{:S(2)}) collective-permute-start(bf16[2,1,2,128,128]{4,3,2,1,0:T(8,128)(2,1)S(1)} %get-tuple-element.55), channel_id=1, source_target_pairs={{0,1},{1,0},{2,3},{3,2},{4,5},{5,4},{6,7},{7,6},{8,9},{9,8},{10,11... | collective-permute-start | bytes 393224 | tf_op jit(solution)/shard_map/ppermute | solution.py:410
  69.2 11.0 %collective-permute-start.7 = (bf16[2,1,2,128,128]{4,3,2,1,0:T(8,128)(2,1)S(1)}, bf16[2,1,2,128,128]{4,3,2,1,0:T(8,128)(2,1)S(1)}, u32[]{:S(2)}, u32[]{:S(2)}) collective-permute-start(bf16[2,1,2,128,128]{4,3,2,1,0:T(8,128)(2,1)S(1)} %get-tuple-element.56), channel_id=1, source_target_pairs={{0,2},{1,3},{2,0},{3,1},{4,6},{5,7},{6,4},{7,5},{8,10},{9,11},{10,... | collective-permute-start | bytes 393224 | tf_op jit(solution)/shard_map/ppermute | solution.py:410
  70.9 11.2 %collective-permute-start.8 = (bf16[2,1,2,128,128]{4,3,2,1,0:T(8,128)(2,1)S(1)}, bf16[2,1,2,128,128]{4,3,2,1,0:T(8,128)(2,1)S(1)}, u32[]{:S(2)}, u32[]{:S(2)}) collective-permute-start(bf16[2,1,2,128,128]{4,3,2,1,0:T(8,128)(2,1)S(1)} %get-tuple-element.57), channel_id=1, source_target_pairs={{0,3},{1,2},{2,1},{3,0},{4,7},{5,6},{6,5},{7,4},{8,11},{9,10},{10,... | collective-permute-start | bytes 393224 | tf_op jit(solution)/shard_map/ppermute | solution.py:410

commit v4 on v3

--- a/solution.py
+++ b/solution.py
@@ -111,12 +111,12 @@
 
 
 def first_chain_kernel(plans, count, sets, width, *refs):
-    counts, neighbours, rows, z_ref, inverse_ref, operator_ref = refs[:6]
-    slots = rows.shape[0]
+    z_ref, inverse_ref, operator_ref = refs[3:6]
+    slots = refs[2].shape[0]
     early = slots // 2
     outs = refs[6 : 6 + early]
     inverse, operator, selector, z_wide, image = refs[6 + early : 11 + early]
-    z_in, first_a, first_b, second_a, second_b, sems = refs[11 + early :]
+    counts, neighbours, rows, z_in, first_a, first_b, second_a, second_b, sems = refs[11 + early :]
     block = inverse.shape[1] // 2
 
     def fetch(source, target, part, sem):
@@ -126,8 +126,14 @@
     z_copy = pltpu.make_async_copy(z_ref, z_in, sems.at[0])
     inverse_loads = [fetch(inverse_ref, inverse, part, sems.at[1 + part]) for part in range(2)]
     operator_loads = [fetch(operator_ref, operator, part, sems.at[3 + part]) for part in range(2)]
-    for copy in [z_copy] + inverse_loads:
+    small = [
+        pltpu.make_async_copy(source, target, sems.at[5 + index])
+        for index, (source, target) in enumerate(zip(refs[:3], (counts, neighbours, rows)))
+    ]
+    for copy in small + [z_copy] + inverse_loads:
         copy.start()
+    for copy in small:
+        copy.wait()
     fill_selector(plans, count, rows, counts, neighbours, selector)
     z_copy.wait()
     z_wide[...] = z_in[...].astype(F32)
@@ -186,7 +192,6 @@
     slots, _, margin = rows.shape
     edges = inverse.shape[1]
     hbm = pl.BlockSpec(memory_space=pltpu.HBM)
-    smem = pl.BlockSpec(memory_space=pltpu.SMEM)
     vmem = pl.BlockSpec(memory_space=pltpu.VMEM)
     flops = 4 * edges * width * (6 * edges + slots * margin)
     early = slots // 2
@@ -200,13 +205,16 @@
     results = pl.pallas_call(
         functools.partial(first_chain_kernel, plans, count, sets, width),
         out_shape=outs,
-        in_specs=[smem, smem, vmem, hbm, hbm, hbm],
+        in_specs=[hbm] * 6,
         out_specs=[vmem] * len(outs),
         scratch_shapes=[
+            pltpu.SMEM(counts.shape, jnp.int32),
+            pltpu.SMEM(neighbours.shape, jnp.int32),
+            pltpu.VMEM(rows.shape, jnp.int32),
             pltpu.VMEM(z.shape, BF16),
         ]
         + [pltpu.VMEM((edges, 2 * width), BF16)] * 4
-        + [pltpu.SemaphoreType.DMA((5,))],
+        + [pltpu.SemaphoreType.DMA((8,))],
         compiler_params=pltpu.CompilerParams(vmem_limit_bytes=CHAIN_VMEM),
         cost_estimate=pl.CostEstimate(flops=flops, bytes_accessed=12 << 20, transcendentals=0),
         name="chain0",

time: 83.9 us -> 83.2 us (level)
  transfers between devices with their start and end apart: 27 -> 27, of which waited for: 8 -> 8; matrix products, arithmetic and copies ran while one was open for 0% -> 0% of each run, Pallas kernels for 20% -> 21%
where the time goes in v4:
time: 83.2 us; the launch traced here: 82.6 us
  starting transfers between devices  46.1 us (55%)
  Pallas kernels  24.6 us (30%)
  waiting for transfers between devices  11.7 us (14%)
    ppermute x18, starting transfers between devices, exchanged(): pieces[back] = lax.ppermute(outgoing[place], 'dom', pairs)  38.2 us
    pallas_call x2, Pallas kernels, next_chain(): pl.pallas_call(functools.partial(next_chain_kernel, index, sets, width),...  8.82 us
    ppermute x9, waiting for transfers between devices, on_device(): sent.append(lax.ppermute(blocks[hop], 'grp', pairs))  8.1 us
    ppermute x9, starting transfers between devices, on_device(): sent.append(lax.ppermute(blocks[hop], 'grp', pairs))  7.87 us
    pallas_call x1, Pallas kernels, first_chain(): pl.pallas_call(functools.partial(first_chain_kernel, plans, count, sets,...  6.61 us
    ppermute x18, waiting for transfers between devices, exchanged(): pieces[back] = lax.ppermute(outgoing[place], 'dom', pairs)  3.56 us
    pallas_call x3, Pallas kernels, spread(): pl.pallas_call(body, out_shape=jax.ShapeDtypeStruct((places, sets, 2, wid...  3.06 us
    pallas_call x3, Pallas kernels, gram_blocks(): pl.pallas_call(functools.partial(gram_kernel, plans, count, group, width,...  2.87 us
  transfers between devices with their start and end apart: 27, of which 8 were waited for; matrix products, arithmetic and copies ran while one was open for 0% of the time, Pallas kernels for 21%

profile of v4, /device:TPU:0, one launch (start us, length us, event | category | flops | bytes accessed | tf_op | source)
XLA Modules:
  0.0 82.6 jit_solution(11766714814812677367)
XLA Ops:
  0.0 6.6 %chain0.1 = (bf16[256,256]{1,0:T(8,128)(2,1)S(1)}, bf16[256,256]{1,0:T(8,128)(2,1)S(1)}, bf16[256,256]{1,0:T(8,128)(2,1)S(1)}, bf16[2,1024,1024]{2,1,0:T(8,128)(...) custom-call(s32[1,6]{1,0:T(1,128)} %refs_0_.1, ...), custom_call_target="tpu_custom_call" | custom-call | flops 4026531840 | bytes 12582912 | tf_op jit(solution)/shard_map/chain0/pallas_call | solution.py:205
  6.6 5.1 %collective-permute-start.18 = (bf16[256,256]{1,0:T(8,128)(2,1)S(1)}, bf16[256,256]{1,0:T(8,128)(2,1)S(1)}, u32[]{:S(2)}, u32[]{:S(2)}) collective-permute-start(bf16[256,256]{1,0:T(8,128)(2,1)S(1)} %get-tuple-element.70), channel_id=1, source_target_pairs={{0,24},{4,28},{8,16},{12,20},{16,8},{20,12},{24,0},{28,4},{1,25},{... | collective-permute-start | bytes 393224 | tf_op jit(solution)/shard_map/ppermute | solution.py:384
  12.1 2.4 %collective-permute-start.20 = (bf16[256,256]{1,0:T(8,128)(2,1)S(1)}, bf16[256,256]{1,0:T(8,128)(2,1)S(1)}, u32[]{:S(2)}, u32[]{:S(2)}) collective-permute-start(bf16[256,256]{1,0:T(8,128)(2,1)S(1)} %get-tuple-element.72), channel_id=1, source_target_pairs={{0,28},{4,24},{8,20},{12,16},{16,12},{20,8},{24,4},{28,0},{1,29},{... | collective-permute-start | bytes 393224 | tf_op jit(solution)/shard_map/ppermute | solution.py:384
  15.2 1.6 %collective-permute-start.21 = (bf16[256,256]{1,0:T(8,128)(2,1)S(1)}, bf16[256,256]{1,0:T(8,128)(2,1)S(1)}, u32[]{:S(2)}, u32[]{:S(2)}) collective-permute-start(bf16[256,256]{1,0:T(8,128)(2,1)S(1)} %get-tuple-element.74), channel_id=1, source_target_pairs={{0,8},{4,12},{8,0},{12,4},{16,24},{20,28},{24,16},{28,20},{1,9},{5... | collective-permute-start | bytes 393224 | tf_op jit(solution)/shard_map/ppermute | solution.py:384
  16.8 1.5 %collective-permute-start.22 = (bf16[256,256]{1,0:T(8,128)(2,1)S(1)}, bf16[256,256]{1,0:T(8,128)(2,1)S(1)}, u32[]{:S(2)}, u32[]{:S(2)}) collective-permute-start(bf16[256,256]{1,0:T(8,128)(2,1)S(1)} %get-tuple-element.75), channel_id=1, source_target_pairs={{0,4},{4,0},{8,12},{12,8},{16,20},{20,16},{24,28},{28,24},{1,5},{5... | collective-permute-start | bytes 393224 | tf_op jit(solution)/shard_map/ppermute | solution.py:384
  18.3 4.3 %shard_map.75 = (bf16[256,256]{1,0:T(8,128)(2,1)S(1)}, bf16[256,256]{1,0:T(8,128)(2,1)S(1)}, bf16[256,256]{1,0:T(8,128)(2,1)S(1)}, bf16[256,256]{1,0:T(8,128)(2,...) custom-call(bf16[2,1024,1024]{2,1,0:T(8,128)(2,1)S(1)} %get-tuple-element.46.inverse, ...), custom_call_target="tpu_custom_call" | custom-call | flops 4026531840 | bytes 12582912 | tf_op jit(solution)/shard_map/pallas_call | solution.py:240
  22.6 2.6 %collective-permute-start.23 = (bf16[256,256]{1,0:T(8,128)(2,1)S(1)}, bf16[256,256]{1,0:T(8,128)(2,1)S(1)}, u32[]{:S(2)}, u32[]{:S(2)}) collective-permute-start(bf16[256,256]{1,0:T(8,128)(2,1)S(1)} %get-tuple-element.76), channel_id=1, source_target_pairs={{0,12},{4,8},{8,4},{12,0},{16,28},{20,24},{24,20},{28,16},{1,13},{... | collective-permute-start | bytes 393224 | tf_op jit(solution)/shard_map/ppermute | solution.py:384
  25.3 2.2 %collective-permute-done.19.rest_2_ = bf16[256,256]{1,0:T(8,128)(2,1)S(1)} collective-permute-done((bf16[256,256]{1,0:T(8,128)(2,1)S(1)}, bf16[256,256]{1,0:T(8,128)(2,1)S(1)}, u32[]{:S(2)}, u32[]{:S(2)}) %collective-permute-start.19) | collective-permute-done | bytes 131104 | tf_op jit(solution)/shard_map/ppermute | solution.py:384
  27.5 2.7 %collective-permute-start.9 = (bf16[256,256]{1,0:T(8,128)(2,1)S(1)}, bf16[256,256]{1,0:T(8,128)(2,1)S(1)}, u32[]{:S(2)}, u32[]{:S(2)}) collective-permute-start(bf16[256,256]{1,0:T(8,128)(2,1)S(1)} %get-tuple-element.59), channel_id=1, source_target_pairs={{0,24},{4,28},{8,16},{12,20},{16,8},{20,12},{24,0},{28,4},{1,25},{... | collective-permute-start | bytes 393224 | tf_op jit(solution)/shard_map/ppermute | solution.py:384
  30.2 1.8 %collective-permute-start.10 = (bf16[256,256]{1,0:T(8,128)(2,1)S(1)}, bf16[256,256]{1,0:T(8,128)(2,1)S(1)}, u32[]{:S(2)}, u32[]{:S(2)}) collective-permute-start(bf16[256,256]{1,0:T(8,128)(2,1)S(1)} %get-tuple-element.60), channel_id=1, source_target_pairs={{0,20},{4,16},{8,28},{12,24},{16,4},{20,0},{24,12},{28,8},{1,21},{... | collective-permute-start | bytes 393224 | tf_op jit(solution)/shard_map/ppermute | solution.py:384
  32.1 3.8 %collective-permute-start.11 = (bf16[256,256]{1,0:T(8,128)(2,1)S(1)}, bf16[256,256]{1,0:T(8,128)(2,1)S(1)}, u32[]{:S(2)}, u32[]{:S(2)}) collective-permute-start(bf16[256,256]{1,0:T(8,128)(2,1)S(1)} %get-tuple-element.61), channel_id=1, source_target_pairs={{0,28},{4,24},{8,20},{12,16},{16,12},{20,8},{24,4},{28,0},{1,29},{... | collective-permute-start | bytes 393224 | tf_op jit(solution)/shard_map/ppermute | solution.py:384
  36.0 5.3 %collective-permute-start.14 = (bf16[256,256]{1,0:T(8,128)(2,1)S(1)}, bf16[256,256]{1,0:T(8,128)(2,1)S(1)}, u32[]{:S(2)}, u32[]{:S(2)}) collective-permute-start(bf16[256,256]{1,0:T(8,128)(2,1)S(1)} %get-tuple-element.64), channel_id=1, source_target_pairs={{0,12},{4,8},{8,4},{12,0},{16,28},{20,24},{24,20},{28,16},{1,13},{... | collective-permute-start | bytes 393224 | tf_op jit(solution)/shard_map/ppermute | solution.py:384
  41.3 4.5 %shard_map.73 = (bf16[256,256]{1,0:T(8,128)(2,1)S(1)}, bf16[256,256]{1,0:T(8,128)(2,1)S(1)}, bf16[256,256]{1,0:T(8,128)(2,1)S(1)}, bf16[256,256]{1,0:T(8,128)(2,...) custom-call(bf16[2,1024,1024]{2,1,0:T(8,128)(2,1)S(1)} %get-tuple-element.46.inverse, ...), custom_call_target="tpu_custom_call" | custom-call | flops 4026531840 | bytes 12582912 | tf_op jit(solution)/shard_map/pallas_call | solution.py:240
  45.8 2.5 %collective-permute-start = (bf16[256,256]{1,0:T(8,128)(2,1)S(1)}, bf16[256,256]{1,0:T(8,128)(2,1)S(1)}, u32[]{:S(2)}, u32[]{:S(2)}) collective-permute-start(bf16[256,256]{1,0:T(8,128)(2,1)S(1)} %get-tuple-element.48), channel_id=1, source_target_pairs={{0,24},{4,28},{8,16},{12,20},{16,8},{20,12},{24,0},{28,4},{1,25},{... | collective-permute-start | bytes 393224 | tf_op jit(solution)/shard_map/ppermute | solution.py:384
  49.2 3.8 %collective-permute-start.2 = (bf16[256,256]{1,0:T(8,128)(2,1)S(1)}, bf16[256,256]{1,0:T(8,128)(2,1)S(1)}, u32[]{:S(2)}, u32[]{:S(2)}) collective-permute-start(bf16[256,256]{1,0:T(8,128)(2,1)S(1)} %get-tuple-element.50), channel_id=1, source_target_pairs={{0,28},{4,24},{8,20},{12,16},{16,12},{20,8},{24,4},{28,0},{1,29},{... | collective-permute-start | bytes 393224 | tf_op jit(solution)/shard_map/ppermute | solution.py:384
  53.1 2.7 %project.1 = (bf16[6,256,256]{2,1,0:T(8,128)(2,1)S(1)}, bf16[6,256,256]{2,1,0:T(8,128)(2,1)S(1)}, bf16[6,256,256]{2,1,0:T(8,128)(2,1)S(1)}) custom-call(bf16[1536,1024]{1,0:T(8,128)(2,1)S(1)} %get-tuple-element.43.selector.selector_ref, f32[6144,128]{1,0:T(8,128)S(1)} %get-tuple-element.44.z_wide), custom_call_target="tpu_custom_call" | custom-call | flops 2415919104 | bytes 6291456 | tf_op jit(solution)/shard_map/project/pallas_call | solution.py:273
  55.8 1.0 %shard_map.77 = (bf16[2,1,2,128,128]{4,3,2,1,0:T(8,128)(2,1)S(1)}, bf16[2,1,2,128,128]{4,3,2,1,0:T(8,128)(2,1)S(1)}, bf16[2,1,2,128,128]{4,3,2,1,0:T(8,128)(2,1)S(1)}, bf16[2,1,2,128,128]{4,3,2,1,0:T(8,128)(2,1)S(1)}) custom-call(s32[1,6]{1,0:T(1,128)S(1)} %bitcast.5, bf16[6,256,256]{2,1,0:T(8,128)(2,1)S(1)} %get-tuple-element.69.rest_0_, ...), custom_call_target="tpu_custom_call" | custom-call | flops 201326592 | bytes 2097152 | tf_op jit(solution)/shard_map/pallas_call | solution.py:320
  56.7 3.5 %collective-permute-start.5 = (bf16[256,256]{1,0:T(8,128)(2,1)S(1)}, bf16[256,256]{1,0:T(8,128)(2,1)S(1)}, u32[]{:S(2)}, u32[]{:S(2)}) collective-permute-start(bf16[256,256]{1,0:T(8,128)(2,1)S(1)} %get-tuple-element.53), channel_id=1, source_target_pairs={{0,12},{4,8},{8,4},{12,0},{16,28},{20,24},{24,20},{28,16},{1,13},{... | collective-permute-start | bytes 393224 | tf_op jit(solution)/shard_map/ppermute | solution.py:384
  60.2 1.0 %shard_map.76 = (bf16[2,1,2,128,128]{4,3,2,1,0:T(8,128)(2,1)S(1)}, bf16[2,1,2,128,128]{4,3,2,1,0:T(8,128)(2,1)S(1)}, bf16[2,1,2,128,128]{4,3,2,1,0:T(8,128)(2,1)S(1)}, bf16[2,1,2,128,128]{4,3,2,1,0:T(8,128)(2,1)S(1)}) custom-call(s32[1,6]{1,0:T(1,128)S(1)} %bitcast.6, bf16[6,256,256]{2,1,0:T(8,128)(2,1)S(1)} %get-tuple-element.58.rest_0_, ...), custom_call_target="tpu_custom_call" | custom-call | flops 201326592 | bytes 2097152 | tf_op jit(solution)/shard_map/pallas_call | solution.py:320
  62.3 1.5 %collective-permute-start.25 = (bf16[2,1,2,128,128]{4,3,2,1,0:T(8,128)(2,1)S(1)}, bf16[2,1,2,128,128]{4,3,2,1,0:T(8,128)(2,1)S(1)}, u32[]{:S(2)}, u32[]{:S(2)}) collective-permute-start(bf16[2,1,2,128,128]{4,3,2,1,0:T(8,128)(2,1)S(1)} %get-tuple-element.79), channel_id=1, source_target_pairs={{0,2},{1,3},{2,0},{3,1},{4,6},{5,7},{6,4},{7,5},{8,10},{9,11},{10,... | collective-permute-start | bytes 393224 | tf_op jit(solution)/shard_map/ppermute | solution.py:418
  64.4 1.5 %collective-permute-start.16 = (bf16[2,1,2,128,128]{4,3,2,1,0:T(8,128)(2,1)S(1)}, bf16[2,1,2,128,128]{4,3,2,1,0:T(8,128)(2,1)S(1)}, u32[]{:S(2)}, u32[]{:S(2)}) collective-permute-start(bf16[2,1,2,128,128]{4,3,2,1,0:T(8,128)(2,1)S(1)} %get-tuple-element.67), channel_id=1, source_target_pairs={{0,2},{1,3},{2,0},{3,1},{4,6},{5,7},{6,4},{7,5},{8,10},{9,11},{10,... | collective-permute-start | bytes 393224 | tf_op jit(solution)/shard_map/ppermute | solution.py:418
  65.9 1.0 %shard_map.74 = (bf16[2,1,2,128,128]{4,3,2,1,0:T(8,128)(2,1)S(1)}, bf16[2,1,2,128,128]{4,3,2,1,0:T(8,128)(2,1)S(1)}, bf16[2,1,2,128,128]{4,3,2,1,0:T(8,128)(2,1)S(1)}, bf16[2,1,2,128,128]{4,3,2,1,0:T(8,128)(2,1)S(1)}) custom-call(s32[1,6]{1,0:T(1,128)S(1)} %bitcast.7, bf16[6,256,256]{2,1,0:T(8,128)(2,1)S(1)} %get-tuple-element.45.rest_0_, ...), custom_call_target="tpu_custom_call" | custom-call | flops 201326592 | bytes 2097152 | tf_op jit(solution)/shard_map/pallas_call | solution.py:320
  66.9 1.5 %collective-permute-start.17 = (bf16[2,1,2,128,128]{4,3,2,1,0:T(8,128)(2,1)S(1)}, bf16[2,1,2,128,128]{4,3,2,1,0:T(8,128)(2,1)S(1)}, u32[]{:S(2)}, u32[]{:S(2)}) collective-permute-start(bf16[2,1,2,128,128]{4,3,2,1,0:T(8,128)(2,1)S(1)} %get-tuple-element.68), channel_id=1, source_target_pairs={{0,3},{1,2},{2,1},{3,0},{4,7},{5,6},{6,5},{7,4},{8,11},{9,10},{10,... | collective-permute-start | bytes 393224 | tf_op jit(solution)/shard_map/ppermute | solution.py:418
  68.4 1.2 %collective-permute-start.7 = (bf16[2,1,2,128,128]{4,3,2,1,0:T(8,128)(2,1)S(1)}, bf16[2,1,2,128,128]{4,3,2,1,0:T(8,128)(2,1)S(1)}, u32[]{:S(2)}, u32[]{:S(2)}) collective-permute-start(bf16[2,1,2,128,128]{4,3,2,1,0:T(8,128)(2,1)S(1)} %get-tuple-element.56), channel_id=1, source_target_pairs={{0,2},{1,3},{2,0},{3,1},{4,6},{5,7},{6,4},{7,5},{8,10},{9,11},{10,... | collective-permute-start | bytes 393224 | tf_op jit(solution)/shard_map/ppermute | solution.py:418
  70.2 1.7 %collective-permute-start.8 = (bf16[2,1,2,128,128]{4,3,2,1,0:T(8,128)(2,1)S(1)}, bf16[2,1,2,128,128]{4,3,2,1,0:T(8,128)(2,1)S(1)}, u32[]{:S(2)}, u32[]{:S(2)}) collective-permute-start(bf16[2,1,2,128,128]{4,3,2,1,0:T(8,128)(2,1)S(1)} %get-tuple-element.57), channel_id=1, source_target_pairs={{0,3},{1,2},{2,1},{3,0},{4,7},{5,6},{6,5},{7,4},{8,11},{9,10},{10,... | collective-permute-start | bytes 393224 | tf_op jit(solution)/shard_map/ppermute | solution.py:418
  71.9 1.0 %shard_map.78.rest_4_ = f32[8,3,2,128,128]{4,3,2,1,0:T(8,128)} custom-call(bf16[2,1,2,128,128]{4,3,2,1,0:T(8,128)(2,1)S(1)} %get-tuple-element.77.rest_0_, bf16[2,1,2,128,128]{4,3,2,1,0:T(8,128)(2,1)S(1)} %collective-permute-done.24.rest_1_, bf16[2,1,2,128,128]{4,3,2,1,0:T(8,128)(2,1)S(1)} %collective-permute-done.25.rest_2_, ...), custom_call_target="tpu_custom_call" | custom-call | flops 1048576 | bytes 2097152 | tf_op jit(solution)/shard_map/pallas_call | solution.py:361
  72.9 0.9 %collective-permute-done.16.rest_2_ = bf16[2,1,2,128,128]{4,3,2,1,0:T(8,128)(2,1)S(1)} collective-permute-done((bf16[2,1,2,128,128]{4,3,2,1,0:T(8,128)(2,1)S(1)}, bf16[2,1,2,128,128]{4,3,2,1,0:T(8,128)(2,1)S(1)}, u32[]{:S(2)}, u32[]{:S(2)}) %collective-permute-start.16) | collective-permute-done | bytes 131104 | tf_op jit(solution)/shard_map/ppermute | solution.py:418
  73.8 2.1 %collective-permute-done.17.rest_3_ = bf16[2,1,2,128,128]{4,3,2,1,0:T(8,128)(2,1)S(1)} collective-permute-done((bf16[2,1,2,128,128]{4,3,2,1,0:T(8,128)(2,1)S(1)}, bf16[2,1,2,128,128]{4,3,2,1,0:T(8,128)(2,1)S(1)}, u32[]{:S(2)}, u32[]{:S(2)}) %collective-permute-start.17) | collective-permute-done | bytes 131104 | tf_op jit(solution)/shard_map/ppermute | solution.py:418
  75.8 1.0 %shard_map.79.rest_4_ = f32[8,3,2,128,128]{4,3,2,1,0:T(8,128)} custom-call(bf16[2,1,2,128,128]{4,3,2,1,0:T(8,128)(2,1)S(1)} %get-tuple-element.65.rest_0_, bf16[2,1,2,128,128]{4,3,2,1,0:T(8,128)(2,1)S(1)} %collective-permute-done.15.rest_1_, bf16[2,1,2,128,128]{4,3,2,1,0:T(8,128)(2,1)S(1)} %collective-permute-done.16.rest_2_, ...), custom_call_target="tpu_custom_call", output_to_operand_aliasing={{}: (4, {})} | custom-call | flops 1048576 | bytes 2097152 | tf_op jit(solution)/shard_map/pallas_call | solution.py:361
  76.9 2.5 %collective-permute-done.7.rest_2_ = bf16[2,1,2,128,128]{4,3,2,1,0:T(8,128)(2,1)S(1)} collective-permute-done((bf16[2,1,2,128,128]{4,3,2,1,0:T(8,128)(2,1)S(1)}, bf16[2,1,2,128,128]{4,3,2,1,0:T(8,128)(2,1)S(1)}, u32[]{:S(2)}, u32[]{:S(2)}) %collective-permute-start.7) | collective-permute-done | bytes 131104 | tf_op jit(solution)/shard_map/ppermute | solution.py:418
  79.4 2.1 %collective-permute-done.8.rest_3_ = bf16[2,1,2,128,128]{4,3,2,1,0:T(8,128)(2,1)S(1)} collective-permute-done((bf16[2,1,2,128,128]{4,3,2,1,0:T(8,128)(2,1)S(1)}, bf16[2,1,2,128,128]{4,3,2,1,0:T(8,128)(2,1)S(1)}, u32[]{:S(2)}, u32[]{:S(2)}) %collective-permute-start.8) | collective-permute-done | bytes 131104 | tf_op jit(solution)/shard_map/ppermute | solution.py:418
  81.5 1.0 %shard_map.80 = f32[8,3,2,128,128]{4,3,2,1,0:T(8,128)} custom-call(bf16[2,1,2,128,128]{4,3,2,1,0:T(8,128)(2,1)S(1)} %get-tuple-element.54.rest_0_, bf16[2,1,2,128,128]{4,3,2,1,0:T(8,128)(2,1)S(1)} %collective-permute-done.6.rest_1_, bf16[2,1,2,128,128]{4,3,2,1,0:T(8,128)(2,1)S(1)} %collective-permute-done.7.rest_2_, ...), custom_call_target="tpu_custom_call", output_to_operand_aliasing={{}: (4, {})} | custom-call | flops 1048576 | bytes 2097152 | tf_op jit(solution)/shard_map/pallas_call | solution.py:361
  (35 shorter events, 4.4 us)
Async XLA Ops:
  6.6 16.0 %collective-permute-start.18 = (bf16[256,256]{1,0:T(8,128)(2,1)S(1)}, bf16[256,256]{1,0:T(8,128)(2,1)S(1)}, u32[]{:S(2)}, u32[]{:S(2)}) collective-permute-start(bf16[256,256]{1,0:T(8,128)(2,1)S(1)} %get-tuple-element.70), channel_id=1, source_target_pairs={{0,24},{4,28},{8,16},{12,20},{16,8},{20,12},{24,0},{28,4},{1,25},{... | collective-permute-start | bytes 393224 | tf_op jit(solution)/shard_map/ppermute | solution.py:384
  11.8 15.8 %collective-permute-start.19 = (bf16[256,256]{1,0:T(8,128)(2,1)S(1)}, bf16[256,256]{1,0:T(8,128)(2,1)S(1)}, u32[]{:S(2)}, u32[]{:S(2)}) collective-permute-start(bf16[256,256]{1,0:T(8,128)(2,1)S(1)} %get-tuple-element.71), channel_id=1, source_target_pairs={{0,20},{4,16},{8,28},{12,24},{16,4},{20,0},{24,12},{28,8},{1,21},{... | collective-permute-start | bytes 393224 | tf_op jit(solution)/shard_map/ppermute | solution.py:384
  12.1 18.1 %collective-permute-start.20 = (bf16[256,256]{1,0:T(8,128)(2,1)S(1)}, bf16[256,256]{1,0:T(8,128)(2,1)S(1)}, u32[]{:S(2)}, u32[]{:S(2)}) collective-permute-start(bf16[256,256]{1,0:T(8,128)(2,1)S(1)} %get-tuple-element.72), channel_id=1, source_target_pairs={{0,28},{4,24},{8,20},{12,16},{16,12},{20,8},{24,4},{28,0},{1,29},{... | collective-permute-start | bytes 393224 | tf_op jit(solution)/shard_map/ppermute | solution.py:384
  15.2 16.9 %collective-permute-start.21 = (bf16[256,256]{1,0:T(8,128)(2,1)S(1)}, bf16[256,256]{1,0:T(8,128)(2,1)S(1)}, u32[]{:S(2)}, u32[]{:S(2)}) collective-permute-start(bf16[256,256]{1,0:T(8,128)(2,1)S(1)} %get-tuple-element.74), channel_id=1, source_target_pairs={{0,8},{4,12},{8,0},{12,4},{16,24},{20,28},{24,16},{28,20},{1,9},{5... | collective-permute-start | bytes 393224 | tf_op jit(solution)/shard_map/ppermute | solution.py:384
  16.8 19.1 %collective-permute-start.22 = (bf16[256,256]{1,0:T(8,128)(2,1)S(1)}, bf16[256,256]{1,0:T(8,128)(2,1)S(1)}, u32[]{:S(2)}, u32[]{:S(2)}) collective-permute-start(bf16[256,256]{1,0:T(8,128)(2,1)S(1)} %get-tuple-element.75), channel_id=1, source_target_pairs={{0,4},{4,0},{8,12},{12,8},{16,20},{20,16},{24,28},{28,24},{1,5},{5... | collective-permute-start | bytes 393224 | tf_op jit(solution)/shard_map/ppermute | solution.py:384
  22.6 13.3 %collective-permute-start.23 = (bf16[256,256]{1,0:T(8,128)(2,1)S(1)}, bf16[256,256]{1,0:T(8,128)(2,1)S(1)}, u32[]{:S(2)}, u32[]{:S(2)}) collective-permute-start(bf16[256,256]{1,0:T(8,128)(2,1)S(1)} %get-tuple-element.76), channel_id=1, source_target_pairs={{0,12},{4,8},{8,4},{12,0},{16,28},{20,24},{24,20},{28,16},{1,13},{... | collective-permute-start | bytes 393224 | tf_op jit(solution)/shard_map/ppermute | solution.py:384
  27.5 8.5 %collective-permute-start.9 = (bf16[256,256]{1,0:T(8,128)(2,1)S(1)}, bf16[256,256]{1,0:T(8,128)(2,1)S(1)}, u32[]{:S(2)}, u32[]{:S(2)}) collective-permute-start(bf16[256,256]{1,0:T(8,128)(2,1)S(1)} %get-tuple-element.59), channel_id=1, source_target_pairs={{0,24},{4,28},{8,16},{12,20},{16,8},{20,12},{24,0},{28,4},{1,25},{... | collective-permute-start | bytes 393224 | tf_op jit(solution)/shard_map/ppermute | solution.py:384
  30.2 15.6 %collective-permute-start.10 = (bf16[256,256]{1,0:T(8,128)(2,1)S(1)}, bf16[256,256]{1,0:T(8,128)(2,1)S(1)}, u32[]{:S(2)}, u32[]{:S(2)}) collective-permute-start(bf16[256,256]{1,0:T(8,128)(2,1)S(1)} %get-tuple-element.60), channel_id=1, source_target_pairs={{0,20},{4,16},{8,28},{12,24},{16,4},{20,0},{24,12},{28,8},{1,21},{... | collective-permute-start | bytes 393224 | tf_op jit(solution)/shard_map/ppermute | solution.py:384
  32.1 16.3 %collective-permute-start.11 = (bf16[256,256]{1,0:T(8,128)(2,1)S(1)}, bf16[256,256]{1,0:T(8,128)(2,1)S(1)}, u32[]{:S(2)}, u32[]{:S(2)}) collective-permute-start(bf16[256,256]{1,0:T(8,128)(2,1)S(1)} %get-tuple-element.61), channel_id=1, source_target_pairs={{0,28},{4,24},{8,20},{12,16},{16,12},{20,8},{24,4},{28,0},{1,29},{... | collective-permute-start | bytes 393224 | tf_op jit(solution)/shard_map/ppermute | solution.py:384
  35.9 13.3 %collective-permute-start.12 = (bf16[256,256]{1,0:T(8,128)(2,1)S(1)}, bf16[256,256]{1,0:T(8,128)(2,1)S(1)}, u32[]{:S(2)}, u32[]{:S(2)}) collective-permute-start(bf16[256,256]{1,0:T(8,128)(2,1)S(1)} %get-tuple-element.62), channel_id=1, source_target_pairs={{0,8},{4,12},{8,0},{12,4},{16,24},{20,28},{24,16},{28,20},{1,9},{5... | collective-permute-start | bytes 393224 | tf_op jit(solution)/shard_map/ppermute | solution.py:384
  35.9 17.1 %collective-permute-start.13 = (bf16[256,256]{1,0:T(8,128)(2,1)S(1)}, bf16[256,256]{1,0:T(8,128)(2,1)S(1)}, u32[]{:S(2)}, u32[]{:S(2)}) collective-permute-start(bf16[256,256]{1,0:T(8,128)(2,1)S(1)} %get-tuple-element.63), channel_id=1, source_target_pairs={{0,4},{4,0},{8,12},{12,8},{16,20},{20,16},{24,28},{28,24},{1,5},{5... | collective-permute-start | bytes 393224 | tf_op jit(solution)/shard_map/ppermute | solution.py:384
  36.0 17.0 %collective-permute-start.14 = (bf16[256,256]{1,0:T(8,128)(2,1)S(1)}, bf16[256,256]{1,0:T(8,128)(2,1)S(1)}, u32[]{:S(2)}, u32[]{:S(2)}) collective-permute-start(bf16[256,256]{1,0:T(8,128)(2,1)S(1)} %get-tuple-element.64), channel_id=1, source_target_pairs={{0,12},{4,8},{8,4},{12,0},{16,28},{20,24},{24,20},{28,16},{1,13},{... | collective-permute-start | bytes 393224 | tf_op jit(solution)/shard_map/ppermute | solution.py:384
  45.8 10.9 %collective-permute-start = (bf16[256,256]{1,0:T(8,128)(2,1)S(1)}, bf16[256,256]{1,0:T(8,128)(2,1)S(1)}, u32[]{:S(2)}, u32[]{:S(2)}) collective-permute-start(bf16[256,256]{1,0:T(8,128)(2,1)S(1)} %get-tuple-element.48), channel_id=1, source_target_pairs={{0,24},{4,28},{8,16},{12,20},{16,8},{20,12},{24,0},{28,4},{1,25},{... | collective-permute-start | bytes 393224 | tf_op jit(solution)/shard_map/ppermute | solution.py:384
  48.4 13.5 %collective-permute-start.1 = (bf16[256,256]{1,0:T(8,128)(2,1)S(1)}, bf16[256,256]{1,0:T(8,128)(2,1)S(1)}, u32[]{:S(2)}, u32[]{:S(2)}) collective-permute-start(bf16[256,256]{1,0:T(8,128)(2,1)S(1)} %get-tuple-element.49), channel_id=1, source_target_pairs={{0,20},{4,16},{8,28},{12,24},{16,4},{20,0},{24,12},{28,8},{1,21},{... | collective-permute-start | bytes 393224 | tf_op jit(solution)/shard_map/ppermute | solution.py:384
  49.2 12.6 %collective-permute-start.2 = (bf16[256,256]{1,0:T(8,128)(2,1)S(1)}, bf16[256,256]{1,0:T(8,128)(2,1)S(1)}, u32[]{:S(2)}, u32[]{:S(2)}) collective-permute-start(bf16[256,256]{1,0:T(8,128)(2,1)S(1)} %get-tuple-element.50), channel_id=1, source_target_pairs={{0,28},{4,24},{8,20},{12,16},{16,12},{20,8},{24,4},{28,0},{1,29},{... | collective-permute-start | bytes 393224 | tf_op jit(solution)/shard_map/ppermute | solution.py:384
  53.0 9.3 %collective-permute-start.3 = (bf16[256,256]{1,0:T(8,128)(2,1)S(1)}, bf16[256,256]{1,0:T(8,128)(2,1)S(1)}, u32[]{:S(2)}, u32[]{:S(2)}) collective-permute-start(bf16[256,256]{1,0:T(8,128)(2,1)S(1)} %get-tuple-element.51), channel_id=1, source_target_pairs={{0,8},{4,12},{8,0},{12,4},{16,24},{20,28},{24,16},{28,20},{1,9},{5... | collective-permute-start | bytes 393224 | tf_op jit(solution)/shard_map/ppermute | solution.py:384
  53.0 2.8 %copy-start = (s32[1,6,1]{1,2,0:T(1,128)S(1)}, s32[1,6,1]{1,2,0:T(1,128)}, u32[]{:S(2)}) copy-start(s32[1,6,1]{1,2,0:T(1,128)} %param.13) | copy-start | bytes 76
  53.0 11.4 %collective-permute-start.4 = (bf16[256,256]{1,0:T(8,128)(2,1)S(1)}, bf16[256,256]{1,0:T(8,128)(2,1)S(1)}, u32[]{:S(2)}, u32[]{:S(2)}) collective-permute-start(bf16[256,256]{1,0:T(8,128)(2,1)S(1)} %get-tuple-element.52), channel_id=1, source_target_pairs={{0,4},{4,0},{8,12},{12,8},{16,20},{20,16},{24,28},{28,24},{1,5},{5... | collective-permute-start | bytes 393224 | tf_op jit(solution)/shard_map/ppermute | solution.py:384
  56.7 7.7 %collective-permute-start.5 = (bf16[256,256]{1,0:T(8,128)(2,1)S(1)}, bf16[256,256]{1,0:T(8,128)(2,1)S(1)}, u32[]{:S(2)}, u32[]{:S(2)}) collective-permute-start(bf16[256,256]{1,0:T(8,128)(2,1)S(1)} %get-tuple-element.53), channel_id=1, source_target_pairs={{0,12},{4,8},{8,4},{12,0},{16,28},{20,24},{24,20},{28,16},{1,13},{... | collective-permute-start | bytes 393224 | tf_op jit(solution)/shard_map/ppermute | solution.py:384
  61.8 5.1 %collective-permute-start.15 = (bf16[2,1,2,128,128]{4,3,2,1,0:T(8,128)(2,1)S(1)}, bf16[2,1,2,128,128]{4,3,2,1,0:T(8,128)(2,1)S(1)}, u32[]{:S(2)}, u32[]{:S(2)}) collective-permute-start(bf16[2,1,2,128,128]{4,3,2,1,0:T(8,128)(2,1)S(1)} %get-tuple-element.66), channel_id=1, source_target_pairs={{0,1},{1,0},{2,3},{3,2},{4,5},{5,4},{6,7},{7,6},{8,9},{9,8},{10,11... | collective-permute-start | bytes 393224 | tf_op jit(solution)/shard_map/ppermute | solution.py:418
  61.8 6.6 %collective-permute-start.24 = (bf16[2,1,2,128,128]{4,3,2,1,0:T(8,128)(2,1)S(1)}, bf16[2,1,2,128,128]{4,3,2,1,0:T(8,128)(2,1)S(1)}, u32[]{:S(2)}, u32[]{:S(2)}) collective-permute-start(bf16[2,1,2,128,128]{4,3,2,1,0:T(8,128)(2,1)S(1)} %get-tuple-element.78), channel_id=1, source_target_pairs={{0,1},{1,0},{2,3},{3,2},{4,5},{5,4},{6,7},{7,6},{8,9},{9,8},{10,11... | collective-permute-start | bytes 393224 | tf_op jit(solution)/shard_map/ppermute | solution.py:418
  62.3 6.1 %collective-permute-start.25 = (bf16[2,1,2,128,128]{4,3,2,1,0:T(8,128)(2,1)S(1)}, bf16[2,1,2,128,128]{4,3,2,1,0:T(8,128)(2,1)S(1)}, u32[]{:S(2)}, u32[]{:S(2)}) collective-permute-start(bf16[2,1,2,128,128]{4,3,2,1,0:T(8,128)(2,1)S(1)} %get-tuple-element.79), channel_id=1, source_target_pairs={{0,2},{1,3},{2,0},{3,1},{4,6},{5,7},{6,4},{7,5},{8,10},{9,11},{10,... | collective-permute-start | bytes 393224 | tf_op jit(solution)/shard_map/ppermute | solution.py:418
  64.4 5.8 %collective-permute-start.26 = (bf16[2,1,2,128,128]{4,3,2,1,0:T(8,128)(2,1)S(1)}, bf16[2,1,2,128,128]{4,3,2,1,0:T(8,128)(2,1)S(1)}, u32[]{:S(2)}, u32[]{:S(2)}) collective-permute-start(bf16[2,1,2,128,128]{4,3,2,1,0:T(8,128)(2,1)S(1)} %get-tuple-element.80), channel_id=1, source_target_pairs={{0,3},{1,2},{2,1},{3,0},{4,7},{5,6},{6,5},{7,4},{8,11},{9,10},{10,... | collective-permute-start | bytes 393224 | tf_op jit(solution)/shard_map/ppermute | solution.py:418
  64.4 9.3 %collective-permute-start.16 = (bf16[2,1,2,128,128]{4,3,2,1,0:T(8,128)(2,1)S(1)}, bf16[2,1,2,128,128]{4,3,2,1,0:T(8,128)(2,1)S(1)}, u32[]{:S(2)}, u32[]{:S(2)}) collective-permute-start(bf16[2,1,2,128,128]{4,3,2,1,0:T(8,128)(2,1)S(1)} %get-tuple-element.67), channel_id=1, source_target_pairs={{0,2},{1,3},{2,0},{3,1},{4,6},{5,7},{6,4},{7,5},{8,10},{9,11},{10,... | collective-permute-start | bytes 393224 | tf_op jit(solution)/shard_map/ppermute | solution.py:418
  66.9 9.0 %collective-permute-start.17 = (bf16[2,1,2,128,128]{4,3,2,1,0:T(8,128)(2,1)S(1)}, bf16[2,1,2,128,128]{4,3,2,1,0:T(8,128)(2,1)S(1)}, u32[]{:S(2)}, u32[]{:S(2)}) collective-permute-start(bf16[2,1,2,128,128]{4,3,2,1,0:T(8,128)(2,1)S(1)} %get-tuple-element.68), channel_id=1, source_target_pairs={{0,3},{1,2},{2,1},{3,0},{4,7},{5,6},{6,5},{7,4},{8,11},{9,10},{10,... | collective-permute-start | bytes 393224 | tf_op jit(solution)/shard_map/ppermute | solution.py:418
  68.4 8.5 %collective-permute-start.6 = (bf16[2,1,2,128,128]{4,3,2,1,0:T(8,128)(2,1)S(1)}, bf16[2,1,2,128,128]{4,3,2,1,0:T(8,128)(2,1)S(1)}, u32[]{:S(2)}, u32[]{:S(2)}) collective-permute-start(bf16[2,1,2,128,128]{4,3,2,1,0:T(8,128)(2,1)S(1)} %get-tuple-element.55), channel_id=1, source_target_pairs={{0,1},{1,0},{2,3},{3,2},{4,5},{5,4},{6,7},{7,6},{8,9},{9,8},{10,11... | collective-permute-start | bytes 393224 | tf_op jit(solution)/shard_map/ppermute | solution.py:418
  68.4 11.0 %collective-permute-start.7 = (bf16[2,1,2,128,128]{4,3,2,1,0:T(8,128)(2,1)S(1)}, bf16[2,1,2,128,128]{4,3,2,1,0:T(8,128)(2,1)S(1)}, u32[]{:S(2)}, u32[]{:S(2)}) collective-permute-start(bf16[2,1,2,128,128]{4,3,2,1,0:T(8,128)(2,1)S(1)} %get-tuple-element.56), channel_id=1, source_target_pairs={{0,2},{1,3},{2,0},{3,1},{4,6},{5,7},{6,4},{7,5},{8,10},{9,11},{10,... | collective-permute-start | bytes 393224 | tf_op jit(solution)/shard_map/ppermute | solution.py:418
  70.2 11.2 %collective-permute-start.8 = (bf16[2,1,2,128,128]{4,3,2,1,0:T(8,128)(2,1)S(1)}, bf16[2,1,2,128,128]{4,3,2,1,0:T(8,128)(2,1)S(1)}, u32[]{:S(2)}, u32[]{:S(2)}) collective-permute-start(bf16[2,1,2,128,128]{4,3,2,1,0:T(8,128)(2,1)S(1)} %get-tuple-element.57), channel_id=1, source_target_pairs={{0,3},{1,2},{2,1},{3,0},{4,7},{5,6},{6,5},{7,4},{8,11},{9,10},{10,... | collective-permute-start | bytes 393224 | tf_op jit(solution)/shard_map/ppermute | solution.py:418

commit v5 on v4

--- a/solution.py
+++ b/solution.py
@@ -332,11 +332,13 @@
     )(owners, *projectors, *incoming)
 
 
-def spread(group, sets, width, capacity, arrived, held):
+def spread(group, sets, width, capacity, chosen_hops, received, held):
+    total_hops = len(received)
+    arrived = [received[hop] for hop in chosen_hops]
     hops = len(arrived)
     vmem = pl.BlockSpec(memory_space=pltpu.VMEM)
     any_space = pl.BlockSpec(memory_space=pl.ANY)
-    places = hops * capacity
+    places = total_hops * capacity
     extra = [] if held is None else [held]
 
     def body(*rest):
@@ -344,12 +346,11 @@
         mine = lax.axis_index("grp")
         copies = []
         for hop in range(hops):
-            source = hop_from(mine, hop, hops)
-            for place in range(capacity):
-                wide[source * capacity + place] = inputs[hop][place].astype(F32)
+            source = hop_from(mine, chosen_hops[hop], total_hops)
+            wide[hop * capacity : (hop + 1) * capacity] = inputs[hop][...].astype(F32)
             span = pl.ds(source * capacity, capacity)
             copy = pltpu.make_async_copy(
-                wide.at[span],
+                wide.at[pl.ds(hop * capacity, capacity)],
                 out_ref.at[span, group[0] : group[0] + len(group)],
                 sem.at[hop],
             )
@@ -364,7 +365,7 @@
         in_specs=[vmem] * hops + [any_space] * len(extra),
         out_specs=any_space,
         scratch_shapes=[
-            pltpu.VMEM((places, len(group), 2, width, width), F32),
+            pltpu.VMEM((hops * capacity, len(group), 2, width, width), F32),
             pltpu.SemaphoreType.DMA((hops,)),
         ],
         input_output_aliases={hops: 0} if extra else {},
@@ -418,8 +419,12 @@
             sent.append(lax.ppermute(blocks[hop], "grp", pairs))
         received.append(sent)
     result = None
-    for index in range(sets):
-        result = spread((index,), sets, width, capacity, received[index], result)
+    everyone = tuple(range(group_count))
+    for index in range(sets - 1):
+        result = spread((index,), sets, width, capacity, everyone, received[index], result)
+    index, near = sets - 1, everyone[: group_count // 2]
+    for hops in (near, everyone[len(near) :]):
+        result = spread((index,), sets, width, capacity, hops, received[index], result)
     return result
 
 

time: 83.2 us -> 83.4 us (level)
    pallas_call x3 -> x4, Pallas kernels: 3.06 us -> 3.68 us  [spread(): pl.pallas_call(body, out_shape=jax.ShapeDtypeStruct((places, sets, 2, wid...]
where the time goes in v5:
time: 83.4 us; the launch traced here: 83 us
  starting transfers between devices  46.2 us (55%)
  Pallas kernels  25.2 us (30%)
  waiting for transfers between devices  11.2 us (13%)
    ppermute x18, starting transfers between devices, exchanged(): pieces[back] = lax.ppermute(outgoing[place], 'dom', pairs)  38.2 us
    pallas_call x2, Pallas kernels, next_chain(): pl.pallas_call(functools.partial(next_chain_kernel, index, sets, width),...  8.82 us
    ppermute x9, starting transfers between devices, on_device(): sent.append(lax.ppermute(blocks[hop], 'grp', pairs))  8.01 us
    ppermute x9, waiting for transfers between devices, on_device(): sent.append(lax.ppermute(blocks[hop], 'grp', pairs))  7.32 us
    pallas_call x1, Pallas kernels, first_chain(): pl.pallas_call(functools.partial(first_chain_kernel, plans, count, sets,...  6.61 us
    ppermute x18, waiting for transfers between devices, exchanged(): pieces[back] = lax.ppermute(outgoing[place], 'dom', pairs)  3.89 us
    pallas_call x4, Pallas kernels, spread(): pl.pallas_call(body, out_shape=jax.ShapeDtypeStruct((places, sets, 2, wid...  3.68 us
    pallas_call x3, Pallas kernels, gram_blocks(): pl.pallas_call(functools.partial(gram_kernel, plans, count, group, width,...  2.88 us
  transfers between devices with their start and end apart: 27, of which 8 were waited for; matrix products, arithmetic and copies ran while one was open for 0% of the time, Pallas kernels for 21%

profile of v5, /device:TPU:0, one launch (start us, length us, event | category | flops | bytes accessed | tf_op | source)
XLA Modules:
  0.0 83.0 jit_solution(9590951314343306635)
XLA Ops:
  0.0 6.6 %chain0.1 = (bf16[256,256]{1,0:T(8,128)(2,1)S(1)}, bf16[256,256]{1,0:T(8,128)(2,1)S(1)}, bf16[256,256]{1,0:T(8,128)(2,1)S(1)}, bf16[2,1024,1024]{2,1,0:T(8,128)(...) custom-call(s32[1,6]{1,0:T(1,128)} %refs_0_.1, ...), custom_call_target="tpu_custom_call" | custom-call | flops 4026531840 | bytes 12582912 | tf_op jit(solution)/shard_map/chain0/pallas_call | solution.py:205
  6.6 5.1 %collective-permute-start.18 = (bf16[256,256]{1,0:T(8,128)(2,1)S(1)}, bf16[256,256]{1,0:T(8,128)(2,1)S(1)}, u32[]{:S(2)}, u32[]{:S(2)}) collective-permute-start(bf16[256,256]{1,0:T(8,128)(2,1)S(1)} %get-tuple-element.70), channel_id=1, source_target_pairs={{0,24},{4,28},{8,16},{12,20},{16,8},{20,12},{24,0},{28,4},{1,25},{... | collective-permute-start | bytes 393224 | tf_op jit(solution)/shard_map/ppermute | solution.py:385
  12.1 2.4 %collective-permute-start.20 = (bf16[256,256]{1,0:T(8,128)(2,1)S(1)}, bf16[256,256]{1,0:T(8,128)(2,1)S(1)}, u32[]{:S(2)}, u32[]{:S(2)}) collective-permute-start(bf16[256,256]{1,0:T(8,128)(2,1)S(1)} %get-tuple-element.72), channel_id=1, source_target_pairs={{0,28},{4,24},{8,20},{12,16},{16,12},{20,8},{24,4},{28,0},{1,29},{... | collective-permute-start | bytes 393224 | tf_op jit(solution)/shard_map/ppermute | solution.py:385
  15.2 1.6 %collective-permute-start.21 = (bf16[256,256]{1,0:T(8,128)(2,1)S(1)}, bf16[256,256]{1,0:T(8,128)(2,1)S(1)}, u32[]{:S(2)}, u32[]{:S(2)}) collective-permute-start(bf16[256,256]{1,0:T(8,128)(2,1)S(1)} %get-tuple-element.74), channel_id=1, source_target_pairs={{0,8},{4,12},{8,0},{12,4},{16,24},{20,28},{24,16},{28,20},{1,9},{5... | collective-permute-start | bytes 393224 | tf_op jit(solution)/shard_map/ppermute | solution.py:385
  16.8 1.5 %collective-permute-start.22 = (bf16[256,256]{1,0:T(8,128)(2,1)S(1)}, bf16[256,256]{1,0:T(8,128)(2,1)S(1)}, u32[]{:S(2)}, u32[]{:S(2)}) collective-permute-start(bf16[256,256]{1,0:T(8,128)(2,1)S(1)} %get-tuple-element.75), channel_id=1, source_target_pairs={{0,4},{4,0},{8,12},{12,8},{16,20},{20,16},{24,28},{28,24},{1,5},{5... | collective-permute-start | bytes 393224 | tf_op jit(solution)/shard_map/ppermute | solution.py:385
  18.3 4.3 %shard_map.75 = (bf16[256,256]{1,0:T(8,128)(2,1)S(1)}, bf16[256,256]{1,0:T(8,128)(2,1)S(1)}, bf16[256,256]{1,0:T(8,128)(2,1)S(1)}, bf16[256,256]{1,0:T(8,128)(2,...) custom-call(bf16[2,1024,1024]{2,1,0:T(8,128)(2,1)S(1)} %get-tuple-element.46.inverse, ...), custom_call_target="tpu_custom_call" | custom-call | flops 4026531840 | bytes 12582912 | tf_op jit(solution)/shard_map/pallas_call | solution.py:240
  22.6 2.6 %collective-permute-start.23 = (bf16[256,256]{1,0:T(8,128)(2,1)S(1)}, bf16[256,256]{1,0:T(8,128)(2,1)S(1)}, u32[]{:S(2)}, u32[]{:S(2)}) collective-permute-start(bf16[256,256]{1,0:T(8,128)(2,1)S(1)} %get-tuple-element.76), channel_id=1, source_target_pairs={{0,12},{4,8},{8,4},{12,0},{16,28},{20,24},{24,20},{28,16},{1,13},{... | collective-permute-start | bytes 393224 | tf_op jit(solution)/shard_map/ppermute | solution.py:385
  25.3 2.2 %collective-permute-done.19.rest_2_ = bf16[256,256]{1,0:T(8,128)(2,1)S(1)} collective-permute-done((bf16[256,256]{1,0:T(8,128)(2,1)S(1)}, bf16[256,256]{1,0:T(8,128)(2,1)S(1)}, u32[]{:S(2)}, u32[]{:S(2)}) %collective-permute-start.19) | collective-permute-done | bytes 131104 | tf_op jit(solution)/shard_map/ppermute | solution.py:385
  27.5 2.7 %collective-permute-start.9 = (bf16[256,256]{1,0:T(8,128)(2,1)S(1)}, bf16[256,256]{1,0:T(8,128)(2,1)S(1)}, u32[]{:S(2)}, u32[]{:S(2)}) collective-permute-start(bf16[256,256]{1,0:T(8,128)(2,1)S(1)} %get-tuple-element.59), channel_id=1, source_target_pairs={{0,24},{4,28},{8,16},{12,20},{16,8},{20,12},{24,0},{28,4},{1,25},{... | collective-permute-start | bytes 393224 | tf_op jit(solution)/shard_map/ppermute | solution.py:385
  30.2 1.8 %collective-permute-start.10 = (bf16[256,256]{1,0:T(8,128)(2,1)S(1)}, bf16[256,256]{1,0:T(8,128)(2,1)S(1)}, u32[]{:S(2)}, u32[]{:S(2)}) collective-permute-start(bf16[256,256]{1,0:T(8,128)(2,1)S(1)} %get-tuple-element.60), channel_id=1, source_target_pairs={{0,20},{4,16},{8,28},{12,24},{16,4},{20,0},{24,12},{28,8},{1,21},{... | collective-permute-start | bytes 393224 | tf_op jit(solution)/shard_map/ppermute | solution.py:385
  32.1 3.8 %collective-permute-start.11 = (bf16[256,256]{1,0:T(8,128)(2,1)S(1)}, bf16[256,256]{1,0:T(8,128)(2,1)S(1)}, u32[]{:S(2)}, u32[]{:S(2)}) collective-permute-start(bf16[256,256]{1,0:T(8,128)(2,1)S(1)} %get-tuple-element.61), channel_id=1, source_target_pairs={{0,28},{4,24},{8,20},{12,16},{16,12},{20,8},{24,4},{28,0},{1,29},{... | collective-permute-start | bytes 393224 | tf_op jit(solution)/shard_map/ppermute | solution.py:385
  36.0 5.3 %collective-permute-start.14 = (bf16[256,256]{1,0:T(8,128)(2,1)S(1)}, bf16[256,256]{1,0:T(8,128)(2,1)S(1)}, u32[]{:S(2)}, u32[]{:S(2)}) collective-permute-start(bf16[256,256]{1,0:T(8,128)(2,1)S(1)} %get-tuple-element.64), channel_id=1, source_target_pairs={{0,12},{4,8},{8,4},{12,0},{16,28},{20,24},{24,20},{28,16},{1,13},{... | collective-permute-start | bytes 393224 | tf_op jit(solution)/shard_map/ppermute | solution.py:385
  41.3 4.5 %shard_map.73 = (bf16[256,256]{1,0:T(8,128)(2,1)S(1)}, bf16[256,256]{1,0:T(8,128)(2,1)S(1)}, bf16[256,256]{1,0:T(8,128)(2,1)S(1)}, bf16[256,256]{1,0:T(8,128)(2,...) custom-call(bf16[2,1024,1024]{2,1,0:T(8,128)(2,1)S(1)} %get-tuple-element.46.inverse, ...), custom_call_target="tpu_custom_call" | custom-call | flops 4026531840 | bytes 12582912 | tf_op jit(solution)/shard_map/pallas_call | solution.py:240
  45.8 2.5 %collective-permute-start = (bf16[256,256]{1,0:T(8,128)(2,1)S(1)}, bf16[256,256]{1,0:T(8,128)(2,1)S(1)}, u32[]{:S(2)}, u32[]{:S(2)}) collective-permute-start(bf16[256,256]{1,0:T(8,128)(2,1)S(1)} %get-tuple-element.48), channel_id=1, source_target_pairs={{0,24},{4,28},{8,16},{12,20},{16,8},{20,12},{24,0},{28,4},{1,25},{... | collective-permute-start | bytes 393224 | tf_op jit(solution)/shard_map/ppermute | solution.py:385
  49.2 3.8 %collective-permute-start.2 = (bf16[256,256]{1,0:T(8,128)(2,1)S(1)}, bf16[256,256]{1,0:T(8,128)(2,1)S(1)}, u32[]{:S(2)}, u32[]{:S(2)}) collective-permute-start(bf16[256,256]{1,0:T(8,128)(2,1)S(1)} %get-tuple-element.50), channel_id=1, source_target_pairs={{0,28},{4,24},{8,20},{12,16},{16,12},{20,8},{24,4},{28,0},{1,29},{... | collective-permute-start | bytes 393224 | tf_op jit(solution)/shard_map/ppermute | solution.py:385
  53.1 2.7 %project.1 = (bf16[6,256,256]{2,1,0:T(8,128)(2,1)S(1)}, bf16[6,256,256]{2,1,0:T(8,128)(2,1)S(1)}, bf16[6,256,256]{2,1,0:T(8,128)(2,1)S(1)}) custom-call(bf16[1536,1024]{1,0:T(8,128)(2,1)S(1)} %get-tuple-element.43.selector.selector_ref, f32[6144,128]{1,0:T(8,128)S(1)} %get-tuple-element.44.z_wide), custom_call_target="tpu_custom_call" | custom-call | flops 2415919104 | bytes 6291456 | tf_op jit(solution)/shard_map/project/pallas_call | solution.py:273
  55.8 1.0 %shard_map.76 = (bf16[2,1,2,128,128]{4,3,2,1,0:T(8,128)(2,1)S(1)}, bf16[2,1,2,128,128]{4,3,2,1,0:T(8,128)(2,1)S(1)}, bf16[2,1,2,128,128]{4,3,2,1,0:T(8,128)(2,1)S(1)}, bf16[2,1,2,128,128]{4,3,2,1,0:T(8,128)(2,1)S(1)}) custom-call(s32[1,6]{1,0:T(1,128)S(1)} %bitcast.5, bf16[6,256,256]{2,1,0:T(8,128)(2,1)S(1)} %get-tuple-element.58.rest_0_, ...), custom_call_target="tpu_custom_call" | custom-call | flops 201326592 | bytes 2097152 | tf_op jit(solution)/shard_map/pallas_call | solution.py:320
  56.7 3.5 %collective-permute-start.5 = (bf16[256,256]{1,0:T(8,128)(2,1)S(1)}, bf16[256,256]{1,0:T(8,128)(2,1)S(1)}, u32[]{:S(2)}, u32[]{:S(2)}) collective-permute-start(bf16[256,256]{1,0:T(8,128)(2,1)S(1)} %get-tuple-element.53), channel_id=1, source_target_pairs={{0,12},{4,8},{8,4},{12,0},{16,28},{20,24},{24,20},{28,16},{1,13},{... | collective-permute-start | bytes 393224 | tf_op jit(solution)/shard_map/ppermute | solution.py:385
  60.2 1.6 %collective-permute-done.1.rest_2_ = bf16[256,256]{1,0:T(8,128)(2,1)S(1)} collective-permute-done((bf16[256,256]{1,0:T(8,128)(2,1)S(1)}, bf16[256,256]{1,0:T(8,128)(2,1)S(1)}, u32[]{:S(2)}, u32[]{:S(2)}) %collective-permute-start.1) | collective-permute-done | bytes 131104 | tf_op jit(solution)/shard_map/ppermute | solution.py:385
  61.8 1.0 %shard_map.77 = (bf16[2,1,2,128,128]{4,3,2,1,0:T(8,128)(2,1)S(1)}, bf16[2,1,2,128,128]{4,3,2,1,0:T(8,128)(2,1)S(1)}, bf16[2,1,2,128,128]{4,3,2,1,0:T(8,128)(2,1)S(1)}, bf16[2,1,2,128,128]{4,3,2,1,0:T(8,128)(2,1)S(1)}) custom-call(s32[1,6]{1,0:T(1,128)S(1)} %bitcast.6, bf16[6,256,256]{2,1,0:T(8,128)(2,1)S(1)} %get-tuple-element.69.rest_0_, ...), custom_call_target="tpu_custom_call" | custom-call | flops 201326592 | bytes 2097152 | tf_op jit(solution)/shard_map/pallas_call | solution.py:320
  63.4 1.5 %collective-permute-start.25 = (bf16[2,1,2,128,128]{4,3,2,1,0:T(8,128)(2,1)S(1)}, bf16[2,1,2,128,128]{4,3,2,1,0:T(8,128)(2,1)S(1)}, u32[]{:S(2)}, u32[]{:S(2)}) collective-permute-start(bf16[2,1,2,128,128]{4,3,2,1,0:T(8,128)(2,1)S(1)} %get-tuple-element.79), channel_id=1, source_target_pairs={{0,2},{1,3},{2,0},{3,1},{4,6},{5,7},{6,4},{7,5},{8,10},{9,11},{10,... | collective-permute-start | bytes 393224 | tf_op jit(solution)/shard_map/ppermute | solution.py:419
  64.8 1.4 %collective-permute-start.16 = (bf16[2,1,2,128,128]{4,3,2,1,0:T(8,128)(2,1)S(1)}, bf16[2,1,2,128,128]{4,3,2,1,0:T(8,128)(2,1)S(1)}, u32[]{:S(2)}, u32[]{:S(2)}) collective-permute-start(bf16[2,1,2,128,128]{4,3,2,1,0:T(8,128)(2,1)S(1)} %get-tuple-element.67), channel_id=1, source_target_pairs={{0,2},{1,3},{2,0},{3,1},{4,6},{5,7},{6,4},{7,5},{8,10},{9,11},{10,... | collective-permute-start | bytes 393224 | tf_op jit(solution)/shard_map/ppermute | solution.py:419
  66.3 1.1 %collective-permute-start.17 = (bf16[2,1,2,128,128]{4,3,2,1,0:T(8,128)(2,1)S(1)}, bf16[2,1,2,128,128]{4,3,2,1,0:T(8,128)(2,1)S(1)}, u32[]{:S(2)}, u32[]{:S(2)}) collective-permute-start(bf16[2,1,2,128,128]{4,3,2,1,0:T(8,128)(2,1)S(1)} %get-tuple-element.68), channel_id=1, source_target_pairs={{0,3},{1,2},{2,1},{3,0},{4,7},{5,6},{6,5},{7,4},{8,11},{9,10},{10,... | collective-permute-start | bytes 393224 | tf_op jit(solution)/shard_map/ppermute | solution.py:419
  67.4 1.0 %shard_map.74 = (bf16[2,1,2,128,128]{4,3,2,1,0:T(8,128)(2,1)S(1)}, bf16[2,1,2,128,128]{4,3,2,1,0:T(8,128)(2,1)S(1)}, bf16[2,1,2,128,128]{4,3,2,1,0:T(8,128)(2,1)S(1)}, bf16[2,1,2,128,128]{4,3,2,1,0:T(8,128)(2,1)S(1)}) custom-call(s32[1,6]{1,0:T(1,128)S(1)} %bitcast.7, bf16[6,256,256]{2,1,0:T(8,128)(2,1)S(1)} %get-tuple-element.45.rest_0_, ...), custom_call_target="tpu_custom_call" | custom-call | flops 201326592 | bytes 2097152 | tf_op jit(solution)/shard_map/pallas_call | solution.py:320
  68.4 1.3 %collective-permute-done.25.rest_2_ = bf16[2,1,2,128,128]{4,3,2,1,0:T(8,128)(2,1)S(1)} collective-permute-done((bf16[2,1,2,128,128]{4,3,2,1,0:T(8,128)(2,1)S(1)}, bf16[2,1,2,128,128]{4,3,2,1,0:T(8,128)(2,1)S(1)}, u32[]{:S(2)}, u32[]{:S(2)}) %collective-permute-start.25) | collective-permute-done | bytes 131104 | tf_op jit(solution)/shard_map/ppermute | solution.py:419
  69.7 1.5 %collective-permute-start.6 = (bf16[2,1,2,128,128]{4,3,2,1,0:T(8,128)(2,1)S(1)}, bf16[2,1,2,128,128]{4,3,2,1,0:T(8,128)(2,1)S(1)}, u32[]{:S(2)}, u32[]{:S(2)}) collective-permute-start(bf16[2,1,2,128,128]{4,3,2,1,0:T(8,128)(2,1)S(1)} %get-tuple-element.54), channel_id=1, source_target_pairs={{0,2},{1,3},{2,0},{3,1},{4,6},{5,7},{6,4},{7,5},{8,10},{9,11},{10,... | collective-permute-start | bytes 393224 | tf_op jit(solution)/shard_map/ppermute | solution.py:419
  71.5 1.9 %collective-permute-start.7 = (bf16[2,1,2,128,128]{4,3,2,1,0:T(8,128)(2,1)S(1)}, bf16[2,1,2,128,128]{4,3,2,1,0:T(8,128)(2,1)S(1)}, u32[]{:S(2)}, u32[]{:S(2)}) collective-permute-start(bf16[2,1,2,128,128]{4,3,2,1,0:T(8,128)(2,1)S(1)} %get-tuple-element.55), channel_id=1, source_target_pairs={{0,3},{1,2},{2,1},{3,0},{4,7},{5,6},{6,5},{7,4},{8,11},{9,10},{10,... | collective-permute-start | bytes 393224 | tf_op jit(solution)/shard_map/ppermute | solution.py:419
  73.4 1.0 %shard_map.78.rest_4_ = f32[8,3,2,128,128]{4,3,2,1,0:T(8,128)} custom-call(bf16[2,1,2,128,128]{4,3,2,1,0:T(8,128)(2,1)S(1)} %get-tuple-element.77.rest_0_, bf16[2,1,2,128,128]{4,3,2,1,0:T(8,128)(2,1)S(1)} %collective-permute-done.24.rest_1_, bf16[2,1,2,128,128]{4,3,2,1,0:T(8,128)(2,1)S(1)} %collective-permute-done.25.rest_2_, ...), custom_call_target="tpu_custom_call" | custom-call | flops 1048576 | bytes 2097152 | tf_op jit(solution)/shard_map/pallas_call | solution.py:362
  75.3 1.8 %collective-permute-done.17.rest_3_ = bf16[2,1,2,128,128]{4,3,2,1,0:T(8,128)(2,1)S(1)} collective-permute-done((bf16[2,1,2,128,128]{4,3,2,1,0:T(8,128)(2,1)S(1)}, bf16[2,1,2,128,128]{4,3,2,1,0:T(8,128)(2,1)S(1)}, u32[]{:S(2)}, u32[]{:S(2)}) %collective-permute-start.17) | collective-permute-done | bytes 131104 | tf_op jit(solution)/shard_map/ppermute | solution.py:419
  77.1 1.0 %shard_map.79.rest_2_ = f32[8,3,2,128,128]{4,3,2,1,0:T(8,128)} custom-call(bf16[2,1,2,128,128]{4,3,2,1,0:T(8,128)(2,1)S(1)} %get-tuple-element.65.rest_0_, bf16[2,1,2,128,128]{4,3,2,1,0:T(8,128)(2,1)S(1)} %collective-permute-done.15.rest_1_, bf16[2,1,2,128,128]{4,3,2,1,0:T(8,128)(2,1)S(1)} %collective-permute-done.16.rest_2_, ...), custom_call_target="tpu_custom_call", output_to_operand_aliasing={{}: (4, {})} | custom-call | flops 1048576 | bytes 2097152 | tf_op jit(solution)/shard_map/pallas_call | solution.py:362
  79.0 2.0 %collective-permute-done.6.rest_0_ = bf16[2,1,2,128,128]{4,3,2,1,0:T(8,128)(2,1)S(1)} collective-permute-done((bf16[2,1,2,128,128]{4,3,2,1,0:T(8,128)(2,1)S(1)}, bf16[2,1,2,128,128]{4,3,2,1,0:T(8,128)(2,1)S(1)}, u32[]{:S(2)}, u32[]{:S(2)}) %collective-permute-start.6) | collective-permute-done | bytes 131104 | tf_op jit(solution)/shard_map/ppermute | solution.py:419
  81.0 1.0 %collective-permute-done.7.rest_1_ = bf16[2,1,2,128,128]{4,3,2,1,0:T(8,128)(2,1)S(1)} collective-permute-done((bf16[2,1,2,128,128]{4,3,2,1,0:T(8,128)(2,1)S(1)}, bf16[2,1,2,128,128]{4,3,2,1,0:T(8,128)(2,1)S(1)}, u32[]{:S(2)}, u32[]{:S(2)}) %collective-permute-start.7) | collective-permute-done | bytes 131104 | tf_op jit(solution)/shard_map/ppermute | solution.py:419
  (36 shorter events, 5.5 us)
Async XLA Ops:
  6.6 16.0 %collective-permute-start.18 = (bf16[256,256]{1,0:T(8,128)(2,1)S(1)}, bf16[256,256]{1,0:T(8,128)(2,1)S(1)}, u32[]{:S(2)}, u32[]{:S(2)}) collective-permute-start(bf16[256,256]{1,0:T(8,128)(2,1)S(1)} %get-tuple-element.70), channel_id=1, source_target_pairs={{0,24},{4,28},{8,16},{12,20},{16,8},{20,12},{24,0},{28,4},{1,25},{... | collective-permute-start | bytes 393224 | tf_op jit(solution)/shard_map/ppermute | solution.py:385
  11.8 15.8 %collective-permute-start.19 = (bf16[256,256]{1,0:T(8,128)(2,1)S(1)}, bf16[256,256]{1,0:T(8,128)(2,1)S(1)}, u32[]{:S(2)}, u32[]{:S(2)}) collective-permute-start(bf16[256,256]{1,0:T(8,128)(2,1)S(1)} %get-tuple-element.71), channel_id=1, source_target_pairs={{0,20},{4,16},{8,28},{12,24},{16,4},{20,0},{24,12},{28,8},{1,21},{... | collective-permute-start | bytes 393224 | tf_op jit(solution)/shard_map/ppermute | solution.py:385
  12.1 18.1 %collective-permute-start.20 = (bf16[256,256]{1,0:T(8,128)(2,1)S(1)}, bf16[256,256]{1,0:T(8,128)(2,1)S(1)}, u32[]{:S(2)}, u32[]{:S(2)}) collective-permute-start(bf16[256,256]{1,0:T(8,128)(2,1)S(1)} %get-tuple-element.72), channel_id=1, source_target_pairs={{0,28},{4,24},{8,20},{12,16},{16,12},{20,8},{24,4},{28,0},{1,29},{... | collective-permute-start | bytes 393224 | tf_op jit(solution)/shard_map/ppermute | solution.py:385
  15.2 16.9 %collective-permute-start.21 = (bf16[256,256]{1,0:T(8,128)(2,1)S(1)}, bf16[256,256]{1,0:T(8,128)(2,1)S(1)}, u32[]{:S(2)}, u32[]{:S(2)}) collective-permute-start(bf16[256,256]{1,0:T(8,128)(2,1)S(1)} %get-tuple-element.74), channel_id=1, source_target_pairs={{0,8},{4,12},{8,0},{12,4},{16,24},{20,28},{24,16},{28,20},{1,9},{5... | collective-permute-start | bytes 393224 | tf_op jit(solution)/shard_map/ppermute | solution.py:385
  16.8 19.1 %collective-permute-start.22 = (bf16[256,256]{1,0:T(8,128)(2,1)S(1)}, bf16[256,256]{1,0:T(8,128)(2,1)S(1)}, u32[]{:S(2)}, u32[]{:S(2)}) collective-permute-start(bf16[256,256]{1,0:T(8,128)(2,1)S(1)} %get-tuple-element.75), channel_id=1, source_target_pairs={{0,4},{4,0},{8,12},{12,8},{16,20},{20,16},{24,28},{28,24},{1,5},{5... | collective-permute-start | bytes 393224 | tf_op jit(solution)/shard_map/ppermute | solution.py:385
  22.6 13.3 %collective-permute-start.23 = (bf16[256,256]{1,0:T(8,128)(2,1)S(1)}, bf16[256,256]{1,0:T(8,128)(2,1)S(1)}, u32[]{:S(2)}, u32[]{:S(2)}) collective-permute-start(bf16[256,256]{1,0:T(8,128)(2,1)S(1)} %get-tuple-element.76), channel_id=1, source_target_pairs={{0,12},{4,8},{8,4},{12,0},{16,28},{20,24},{24,20},{28,16},{1,13},{... | collective-permute-start | bytes 393224 | tf_op jit(solution)/shard_map/ppermute | solution.py:385
  27.5 8.5 %collective-permute-start.9 = (bf16[256,256]{1,0:T(8,128)(2,1)S(1)}, bf16[256,256]{1,0:T(8,128)(2,1)S(1)}, u32[]{:S(2)}, u32[]{:S(2)}) collective-permute-start(bf16[256,256]{1,0:T(8,128)(2,1)S(1)} %get-tuple-element.59), channel_id=1, source_target_pairs={{0,24},{4,28},{8,16},{12,20},{16,8},{20,12},{24,0},{28,4},{1,25},{... | collective-permute-start | bytes 393224 | tf_op jit(solution)/shard_map/ppermute | solution.py:385
  30.2 15.6 %collective-permute-start.10 = (bf16[256,256]{1,0:T(8,128)(2,1)S(1)}, bf16[256,256]{1,0:T(8,128)(2,1)S(1)}, u32[]{:S(2)}, u32[]{:S(2)}) collective-permute-start(bf16[256,256]{1,0:T(8,128)(2,1)S(1)} %get-tuple-element.60), channel_id=1, source_target_pairs={{0,20},{4,16},{8,28},{12,24},{16,4},{20,0},{24,12},{28,8},{1,21},{... | collective-permute-start | bytes 393224 | tf_op jit(solution)/shard_map/ppermute | solution.py:385
  32.1 16.3 %collective-permute-start.11 = (bf16[256,256]{1,0:T(8,128)(2,1)S(1)}, bf16[256,256]{1,0:T(8,128)(2,1)S(1)}, u32[]{:S(2)}, u32[]{:S(2)}) collective-permute-start(bf16[256,256]{1,0:T(8,128)(2,1)S(1)} %get-tuple-element.61), channel_id=1, source_target_pairs={{0,28},{4,24},{8,20},{12,16},{16,12},{20,8},{24,4},{28,0},{1,29},{... | collective-permute-start | bytes 393224 | tf_op jit(solution)/shard_map/ppermute | solution.py:385
  35.9 13.3 %collective-permute-start.12 = (bf16[256,256]{1,0:T(8,128)(2,1)S(1)}, bf16[256,256]{1,0:T(8,128)(2,1)S(1)}, u32[]{:S(2)}, u32[]{:S(2)}) collective-permute-start(bf16[256,256]{1,0:T(8,128)(2,1)S(1)} %get-tuple-element.62), channel_id=1, source_target_pairs={{0,8},{4,12},{8,0},{12,4},{16,24},{20,28},{24,16},{28,20},{1,9},{5... | collective-permute-start | bytes 393224 | tf_op jit(solution)/shard_map/ppermute | solution.py:385
  35.9 17.1 %collective-permute-start.13 = (bf16[256,256]{1,0:T(8,128)(2,1)S(1)}, bf16[256,256]{1,0:T(8,128)(2,1)S(1)}, u32[]{:S(2)}, u32[]{:S(2)}) collective-permute-start(bf16[256,256]{1,0:T(8,128)(2,1)S(1)} %get-tuple-element.63), channel_id=1, source_target_pairs={{0,4},{4,0},{8,12},{12,8},{16,20},{20,16},{24,28},{28,24},{1,5},{5... | collective-permute-start | bytes 393224 | tf_op jit(solution)/shard_map/ppermute | solution.py:385
  36.0 17.0 %collective-permute-start.14 = (bf16[256,256]{1,0:T(8,128)(2,1)S(1)}, bf16[256,256]{1,0:T(8,128)(2,1)S(1)}, u32[]{:S(2)}, u32[]{:S(2)}) collective-permute-start(bf16[256,256]{1,0:T(8,128)(2,1)S(1)} %get-tuple-element.64), channel_id=1, source_target_pairs={{0,12},{4,8},{8,4},{12,0},{16,28},{20,24},{24,20},{28,16},{1,13},{... | collective-permute-start | bytes 393224 | tf_op jit(solution)/shard_map/ppermute | solution.py:385
  45.8 10.9 %collective-permute-start = (bf16[256,256]{1,0:T(8,128)(2,1)S(1)}, bf16[256,256]{1,0:T(8,128)(2,1)S(1)}, u32[]{:S(2)}, u32[]{:S(2)}) collective-permute-start(bf16[256,256]{1,0:T(8,128)(2,1)S(1)} %get-tuple-element.48), channel_id=1, source_target_pairs={{0,24},{4,28},{8,16},{12,20},{16,8},{20,12},{24,0},{28,4},{1,25},{... | collective-permute-start | bytes 393224 | tf_op jit(solution)/shard_map/ppermute | solution.py:385
  48.4 13.5 %collective-permute-start.1 = (bf16[256,256]{1,0:T(8,128)(2,1)S(1)}, bf16[256,256]{1,0:T(8,128)(2,1)S(1)}, u32[]{:S(2)}, u32[]{:S(2)}) collective-permute-start(bf16[256,256]{1,0:T(8,128)(2,1)S(1)} %get-tuple-element.49), channel_id=1, source_target_pairs={{0,20},{4,16},{8,28},{12,24},{16,4},{20,0},{24,12},{28,8},{1,21},{... | collective-permute-start | bytes 393224 | tf_op jit(solution)/shard_map/ppermute | solution.py:385
  49.2 13.6 %collective-permute-start.2 = (bf16[256,256]{1,0:T(8,128)(2,1)S(1)}, bf16[256,256]{1,0:T(8,128)(2,1)S(1)}, u32[]{:S(2)}, u32[]{:S(2)}) collective-permute-start(bf16[256,256]{1,0:T(8,128)(2,1)S(1)} %get-tuple-element.50), channel_id=1, source_target_pairs={{0,28},{4,24},{8,20},{12,16},{16,12},{20,8},{24,4},{28,0},{1,29},{... | collective-permute-start | bytes 393224 | tf_op jit(solution)/shard_map/ppermute | solution.py:385
  53.0 10.4 %collective-permute-start.3 = (bf16[256,256]{1,0:T(8,128)(2,1)S(1)}, bf16[256,256]{1,0:T(8,128)(2,1)S(1)}, u32[]{:S(2)}, u32[]{:S(2)}) collective-permute-start(bf16[256,256]{1,0:T(8,128)(2,1)S(1)} %get-tuple-element.51), channel_id=1, source_target_pairs={{0,8},{4,12},{8,0},{12,4},{16,24},{20,28},{24,16},{28,20},{1,9},{5... | collective-permute-start | bytes 393224 | tf_op jit(solution)/shard_map/ppermute | solution.py:385
  53.0 2.8 %copy-start = (s32[1,6,1]{1,2,0:T(1,128)S(1)}, s32[1,6,1]{1,2,0:T(1,128)}, u32[]{:S(2)}) copy-start(s32[1,6,1]{1,2,0:T(1,128)} %param.13) | copy-start | bytes 76
  53.0 11.8 %collective-permute-start.4 = (bf16[256,256]{1,0:T(8,128)(2,1)S(1)}, bf16[256,256]{1,0:T(8,128)(2,1)S(1)}, u32[]{:S(2)}, u32[]{:S(2)}) collective-permute-start(bf16[256,256]{1,0:T(8,128)(2,1)S(1)} %get-tuple-element.52), channel_id=1, source_target_pairs={{0,4},{4,0},{8,12},{12,8},{16,20},{20,16},{24,28},{28,24},{1,5},{5... | collective-permute-start | bytes 393224 | tf_op jit(solution)/shard_map/ppermute | solution.py:385
  56.7 8.1 %collective-permute-start.5 = (bf16[256,256]{1,0:T(8,128)(2,1)S(1)}, bf16[256,256]{1,0:T(8,128)(2,1)S(1)}, u32[]{:S(2)}, u32[]{:S(2)}) collective-permute-start(bf16[256,256]{1,0:T(8,128)(2,1)S(1)} %get-tuple-element.53), channel_id=1, source_target_pairs={{0,12},{4,8},{8,4},{12,0},{16,28},{20,24},{24,20},{28,16},{1,13},{... | collective-permute-start | bytes 393224 | tf_op jit(solution)/shard_map/ppermute | solution.py:385
  61.8 4.5 %collective-permute-start.15 = (bf16[2,1,2,128,128]{4,3,2,1,0:T(8,128)(2,1)S(1)}, bf16[2,1,2,128,128]{4,3,2,1,0:T(8,128)(2,1)S(1)}, u32[]{:S(2)}, u32[]{:S(2)}) collective-permute-start(bf16[2,1,2,128,128]{4,3,2,1,0:T(8,128)(2,1)S(1)} %get-tuple-element.66), channel_id=1, source_target_pairs={{0,1},{1,0},{2,3},{3,2},{4,5},{5,4},{6,7},{7,6},{8,9},{9,8},{10,11... | collective-permute-start | bytes 393224 | tf_op jit(solution)/shard_map/ppermute | solution.py:419
  62.8 5.5 %collective-permute-start.24 = (bf16[2,1,2,128,128]{4,3,2,1,0:T(8,128)(2,1)S(1)}, bf16[2,1,2,128,128]{4,3,2,1,0:T(8,128)(2,1)S(1)}, u32[]{:S(2)}, u32[]{:S(2)}) collective-permute-start(bf16[2,1,2,128,128]{4,3,2,1,0:T(8,128)(2,1)S(1)} %get-tuple-element.78), channel_id=1, source_target_pairs={{0,1},{1,0},{2,3},{3,2},{4,5},{5,4},{6,7},{7,6},{8,9},{9,8},{10,11... | collective-permute-start | bytes 393224 | tf_op jit(solution)/shard_map/ppermute | solution.py:419
  63.4 6.4 %collective-permute-start.25 = (bf16[2,1,2,128,128]{4,3,2,1,0:T(8,128)(2,1)S(1)}, bf16[2,1,2,128,128]{4,3,2,1,0:T(8,128)(2,1)S(1)}, u32[]{:S(2)}, u32[]{:S(2)}) collective-permute-start(bf16[2,1,2,128,128]{4,3,2,1,0:T(8,128)(2,1)S(1)} %get-tuple-element.79), channel_id=1, source_target_pairs={{0,2},{1,3},{2,0},{3,1},{4,6},{5,7},{6,4},{7,5},{8,10},{9,11},{10,... | collective-permute-start | bytes 393224 | tf_op jit(solution)/shard_map/ppermute | solution.py:419
  64.8 6.7 %collective-permute-start.26 = (bf16[2,1,2,128,128]{4,3,2,1,0:T(8,128)(2,1)S(1)}, bf16[2,1,2,128,128]{4,3,2,1,0:T(8,128)(2,1)S(1)}, u32[]{:S(2)}, u32[]{:S(2)}) collective-permute-start(bf16[2,1,2,128,128]{4,3,2,1,0:T(8,128)(2,1)S(1)} %get-tuple-element.80), channel_id=1, source_target_pairs={{0,3},{1,2},{2,1},{3,0},{4,7},{5,6},{6,5},{7,4},{8,11},{9,10},{10,... | collective-permute-start | bytes 393224 | tf_op jit(solution)/shard_map/ppermute | solution.py:419
  64.8 10.5 %collective-permute-start.16 = (bf16[2,1,2,128,128]{4,3,2,1,0:T(8,128)(2,1)S(1)}, bf16[2,1,2,128,128]{4,3,2,1,0:T(8,128)(2,1)S(1)}, u32[]{:S(2)}, u32[]{:S(2)}) collective-permute-start(bf16[2,1,2,128,128]{4,3,2,1,0:T(8,128)(2,1)S(1)} %get-tuple-element.67), channel_id=1, source_target_pairs={{0,2},{1,3},{2,0},{3,1},{4,6},{5,7},{6,4},{7,5},{8,10},{9,11},{10,... | collective-permute-start | bytes 393224 | tf_op jit(solution)/shard_map/ppermute | solution.py:419
  66.3 10.9 %collective-permute-start.17 = (bf16[2,1,2,128,128]{4,3,2,1,0:T(8,128)(2,1)S(1)}, bf16[2,1,2,128,128]{4,3,2,1,0:T(8,128)(2,1)S(1)}, u32[]{:S(2)}, u32[]{:S(2)}) collective-permute-start(bf16[2,1,2,128,128]{4,3,2,1,0:T(8,128)(2,1)S(1)} %get-tuple-element.68), channel_id=1, source_target_pairs={{0,3},{1,2},{2,1},{3,0},{4,7},{5,6},{6,5},{7,4},{8,11},{9,10},{10,... | collective-permute-start | bytes 393224 | tf_op jit(solution)/shard_map/ppermute | solution.py:419
  68.3 9.8 %collective-permute-start.8 = (bf16[2,1,2,128,128]{4,3,2,1,0:T(8,128)(2,1)S(1)}, bf16[2,1,2,128,128]{4,3,2,1,0:T(8,128)(2,1)S(1)}, u32[]{:S(2)}, u32[]{:S(2)}) collective-permute-start(bf16[2,1,2,128,128]{4,3,2,1,0:T(8,128)(2,1)S(1)} %get-tuple-element.57), channel_id=1, source_target_pairs={{0,1},{1,0},{2,3},{3,2},{4,5},{5,4},{6,7},{7,6},{8,9},{9,8},{10,11... | collective-permute-start | bytes 393224 | tf_op jit(solution)/shard_map/ppermute | solution.py:419
  69.7 11.2 %collective-permute-start.6 = (bf16[2,1,2,128,128]{4,3,2,1,0:T(8,128)(2,1)S(1)}, bf16[2,1,2,128,128]{4,3,2,1,0:T(8,128)(2,1)S(1)}, u32[]{:S(2)}, u32[]{:S(2)}) collective-permute-start(bf16[2,1,2,128,128]{4,3,2,1,0:T(8,128)(2,1)S(1)} %get-tuple-element.54), channel_id=1, source_target_pairs={{0,2},{1,3},{2,0},{3,1},{4,6},{5,7},{6,4},{7,5},{8,10},{9,11},{10,... | collective-permute-start | bytes 393224 | tf_op jit(solution)/shard_map/ppermute | solution.py:419
  71.5 10.5 %collective-permute-start.7 = (bf16[2,1,2,128,128]{4,3,2,1,0:T(8,128)(2,1)S(1)}, bf16[2,1,2,128,128]{4,3,2,1,0:T(8,128)(2,1)S(1)}, u32[]{:S(2)}, u32[]{:S(2)}) collective-permute-start(bf16[2,1,2,128,128]{4,3,2,1,0:T(8,128)(2,1)S(1)} %get-tuple-element.55), channel_id=1, source_target_pairs={{0,3},{1,2},{2,1},{3,0},{4,7},{5,6},{6,5},{7,4},{8,11},{9,10},{10,... | collective-permute-start | bytes 393224 | tf_op jit(solution)/shard_map/ppermute | solution.py:419
